TPU v7x, 512 devices: a whole 4x8x8 slice. The times are simulated.
512 devices in a mesh: dp: 64 (over x, z, core), tile: 8 (over y).
Axes of the slice: x: 4, y: 8, z: 8, core: 2. Of those that a mesh axis runs over, the one named last changes fastest.
Arguments:
- proposal_boxes: int32 [64, 4, 512], P('dp'), may hold values from 0 to 1344, as said below
- level_plan: int32 [64, 512], P('dp'), may hold values from 0 to 1
- fine_map: bfloat16 [64, 336, 168, 128], P('dp', 'tile'), may hold values from -6 to 6
- coarse_map: bfloat16 [64, 168, 84, 128], P('dp', 'tile'), may hold values from -6 to 6
- first_weight: bfloat16 [6272, 1024], P('tile', 'dp'), may hold values from -0.078125 to 0.078125
- second_weight: bfloat16 [1024, 1024], P('tile', 'dp'), may hold values from -0.1875 to 0.1875
- upstream: bfloat16 [64, 512, 1024], P('dp'), may hold values from -6 to 6
Outputs:
- first_grad: float32 [6272, 1024], P('tile', 'dp')
- second_grad: float32 [1024, 1024], P('tile', 'dp')
Inputs may be any that keep to these rules, and one draw needn't show every extreme that they name: `proposal_boxes`: with s = 4 where level_plan is 0 and s = 8 where it is 1: h >= 1, w >= 1, y0 + h <= 1344, x0 + w <= 672, (y0 mod s) + h <= 14 * s and (x0 mod s) + w <= 14 * s. Band b holds the proposals with b * 168 <= y0 < (b + 1) * 168; at most 128 of an image's proposals lie in one band, and in every image some band holds exactly 128.
All inputs are finite; a program needn't handle non-finite values.
Results may differ from a plain program's by a relative error of at most 0.017.
Values may be sent and summed in bfloat16 or wider, within the bound.
No kernel may reach another device: no remote copies, remote signals or barrier semaphores. Data moves between devices by JAX's collectives and lax.ppermute only.
A program may use at most 64 MiB of HBM per device.

v0:
```python
import jax
import jax.numpy as jnp
from jax import lax
from jax.sharding import PartitionSpec as P

WIN = 16


def from_behind(block, axis, distance):
    devices = range(lax.axis_size(axis))
    route = [(i - distance, i) for i in devices if i - distance in devices]
    return lax.ppermute(block, axis, route)


def sent_to_all(shard, axis):
    copies = jnp.broadcast_to(shard, (lax.axis_size(axis), *shard.shape))
    return lax.all_to_all(copies, axis, split_axis=0, concat_axis=0, tiled=True)


def in_order(parts, dim):
    lengths = list(parts.shape[1:])
    lengths[dim] *= parts.shape[0]
    return jnp.moveaxis(parts, 0, dim).reshape(lengths)


def collect(shard, axis, dim):
    parts = sent_to_all(shard, axis)
    return in_order(parts, dim)


def cut_along(shard, dim, length):
    before, after = (shard.shape[:dim], shard.shape[dim + 1 :])
    return jnp.moveaxis(shard.reshape(*before, length, -1, *after), dim, 0)


def sent_and_summed(shard, axis, dim):
    parts = cut_along(shard, dim, lax.axis_size(axis))
    arrived = lax.all_to_all(parts, axis, split_axis=0, concat_axis=0, tiled=True)
    return arrived.astype(jnp.float32).sum(axis=0)


def gelu_parts(hidden):
    factor = 0.7978845608028654
    cubic_term = 0.044715
    inner_term = factor * (hidden + cubic_term * hidden * hidden * hidden)
    tangent = jnp.tanh(inner_term)
    gelu_value = 0.5 * hidden * (1.0 + tangent)
    gelu_slope = 0.5 * (1.0 + tangent) + 0.5 * hidden * (1.0 - tangent * tangent) * factor * (
        1.0 + 3.0 * cubic_term * hidden * hidden
    )
    return (gelu_value, gelu_slope)


def block_size():
    return 16


def sample_weights(begin_px, extent, stride, cell_pos):
    stride_float = stride.astype(jnp.float32)[:, None]
    bin_index = jnp.arange(7, dtype=jnp.float32)[None, :]
    sample_pos = begin_px.astype(jnp.float32)[:, None] / stride_float + (
        bin_index + 0.5
    ) * extent.astype(jnp.float32)[:, None] / (7.0 * stride_float)
    return jnp.maximum(0.0, 1.0 - jnp.abs(sample_pos[:, :, None] - cell_pos[None, None, :]))


def crop_block(combined, fields, levels_blk, live_slot, row_pos, fine_part, col_pos):
    top_pixel = fields[0]
    left_pixel = fields[1]
    height = fields[2]
    box_width = fields[3]
    stride = jnp.where(levels_blk == 0, 4, 8).astype(jnp.int32)
    level_match = (fine_part[None, :] == (levels_blk == 0)[:, None]).astype(jnp.float32)
    row_mask = level_match * live_slot.astype(jnp.float32)[:, None]
    row_low = (sample_weights(top_pixel, height, stride, row_pos) * row_mask[:, None, :]).astype(
        jnp.bfloat16
    )
    col_low = sample_weights(left_pixel, box_width, stride, col_pos).astype(jnp.bfloat16)
    count = levels_blk.shape[0]
    total_rows, total_cols, channels = combined.shape
    by_column = lax.dot_general(
        col_low.reshape(count * 7, total_cols),
        combined,
        (((1,), (1,)), ((), ())),
        preferred_element_type=jnp.float32,
    )
    by_column = by_column.reshape(count, 7, total_rows, channels)
    crop_rows = jnp.einsum("bia,bjac->bijc", row_low.astype(jnp.float32), by_column)
    return crop_rows.reshape(count, 49 * channels).astype(jnp.bfloat16)


def per_device(
    proposal_boxes, level_plan, fine_map, coarse_map, first_weight, second_weight, upstream
):
    tile_count = lax.axis_size("tile")
    band_index = lax.axis_index("tile")
    num_props = level_plan.shape[1]
    capacity = max(num_props // 4, num_props // tile_count)
    fine_tile = fine_map[0]
    coarse = coarse_map[0]
    fine_rows, fine_cols, channels = fine_tile.shape
    coarse_rows, coarse_cols = (coarse.shape[0], coarse.shape[1])
    fields = proposal_boxes[0]
    levels_img = level_plan[0]
    owner_band = fields[0] // (4 * fine_rows)
    members = (owner_band[:, None] == jnp.arange(tile_count, dtype=jnp.int32)[None, :]).astype(
        jnp.int32
    )
    slot_rank = jnp.sum((jnp.cumsum(members, axis=0) - 1) * members, axis=1)
    slot_id = owner_band * capacity + slot_rank
    target = jnp.where(owner_band == band_index, slot_rank, capacity)
    slot_prop = (
        jnp.full((capacity,), num_props, jnp.int32)
        .at[target]
        .set(jnp.arange(num_props, dtype=jnp.int32), mode="drop")
    )
    live_slot = (slot_prop < num_props).astype(jnp.int32)
    chosen = jnp.minimum(slot_prop, num_props - 1)
    slot_fields = jnp.take(fields, chosen, axis=1)
    slot_levels = jnp.take(levels_img, chosen)
    top_rows = jnp.concatenate([fine_tile[:WIN], coarse[:WIN]], axis=1)
    below_rows = from_behind(top_rows, "tile", -1)
    fine_ext = jnp.concatenate([fine_tile, below_rows[:, :fine_cols]], axis=0)
    coarse_ext = jnp.concatenate([coarse, below_rows[:, fine_cols:]], axis=0)
    coarse_ext = jnp.pad(coarse_ext, ((0, 0), (0, fine_cols - coarse_cols), (0, 0)))
    combined = jnp.concatenate([fine_ext, coarse_ext], axis=0)
    fine_count = fine_rows + WIN
    coarse_count = coarse_rows + WIN
    fine_pos = (band_index * fine_rows).astype(jnp.float32) + jnp.arange(
        fine_count, dtype=jnp.float32
    )
    coarse_pos = (band_index * coarse_rows).astype(jnp.float32) + jnp.arange(
        coarse_count, dtype=jnp.float32
    )
    row_pos = jnp.concatenate([fine_pos, coarse_pos], axis=0)
    fine_part = jnp.arange(fine_count + coarse_count) < fine_count
    col_pos = jnp.arange(fine_cols, dtype=jnp.float32)
    block_len = block_size()
    grouped_fields = slot_fields.reshape(4, capacity // block_len, block_len).transpose(1, 0, 2)
    grouped_levels = slot_levels.reshape(capacity // block_len, block_len)
    grouped_live = live_slot.reshape(capacity // block_len, block_len)

    def crop_group(pieces):
        part_fields, part_levels, part_live = pieces
        return crop_block(
            combined, part_fields, part_levels, part_live, row_pos, fine_part, col_pos
        )

    crop_rows = lax.map(crop_group, (grouped_fields, grouped_levels, grouped_live)).reshape(
        capacity, 49 * channels
    )
    received = lax.all_to_all(crop_rows, "tile", split_axis=1, concat_axis=0, tiled=True)
    own_feats = jnp.take(received, slot_id, axis=0)
    partial_hidden = jnp.dot(
        own_feats,
        lax.all_gather(first_weight, "dp", axis=1, tiled=True),
        preferred_element_type=jnp.float32,
    )
    share_width = partial_hidden.shape[1] // tile_count
    upstream_rows = upstream[0]
    second_rows = collect(second_weight, "dp", 1)
    pieces = lax.all_to_all(
        partial_hidden.astype(jnp.bfloat16), "tile", split_axis=1, concat_axis=0, tiled=True
    ).astype(partial_hidden.dtype)
    hidden_own = jnp.sum(pieces.reshape(tile_count, num_props, share_width), axis=0)
    gelu_value, gelu_slope = gelu_parts(hidden_own)
    activated = gelu_value.astype(jnp.bfloat16)
    back_grad = lax.dot_general(
        upstream_rows, second_rows, (((1,), (1,)), ((), ())), preferred_element_type=jnp.float32
    )
    pre_own = (back_grad * gelu_slope).astype(jnp.bfloat16)
    pre_grad = collect(pre_own, "tile", 1)
    second_grad = sent_and_summed(
        lax.dot_general(
            upstream_rows, activated, (((0,), (0,)), ((), ())), preferred_element_type=jnp.float32
        ).astype(jnp.bfloat16),
        "dp",
        0,
    ).T
    first_grad = sent_and_summed(
        lax.dot_general(
            pre_grad, own_feats, (((0,), (0,)), ((), ())), preferred_element_type=jnp.float32
        ).astype(jnp.bfloat16),
        "dp",
        0,
    ).T
    return (first_grad, second_grad)


def solution(mesh):
    placed = (
        P("dp", None, None),
        P("dp", None),
        P("dp", "tile", None, None),
        P("dp", "tile", None, None),
        P("tile", "dp"),
        P("tile", "dp"),
        P("dp", None, None),
    )
    return jax.shard_map(
        per_device,
        mesh=mesh,
        in_specs=placed,
        out_specs=(P("tile", "dp"), P("tile", "dp")),
        check_vma=False,
    )
```

profile of v0, /device:TPU:1, one launch (start us, length us, event | category | flops | bytes accessed | tf_op | source)
XLA Modules:
  0.0 344.6 jit_solution(7589161557355145243)
XLA Ops:
  16.9 12.7 %collective-permute-done = bf16[16,252,128]{2,0,1:T(8,128)(2,1)S(1)} collective-permute-done((bf16[16,252,128]{2,0,1:T(8,128)(2,1)S(1)}, bf16[16,252,128]{2,0,1:T(8,128)(2,1)S(1)}, u32[]{:S(2)}, u32[]{:S(2)}) %collective-permute-start) | collective-permute-done | bytes 1032224 | tf_op jit(solution)/shard_map/ppermute | solution.py:12
  31.4 3.6 %pad_maximum_fusion = bf16[95,168,128]{2,1,0:T(8,128)(2,1)} fusion(bf16[37,168,128]{2,1,0:T(8,128)(2,1)S(1)} %fusion.35, bf16[16,168,128]{2,1,0:T(8,128)(2,1)S(1)} %copy.43, bf16[42,168,128]{2,1,0:T(8,128)(2,1)S(1)} %bitcast.109), kind=kLoop, calls=%fused_computation.49 | loop fusion | flops 4085760 | bytes 8171520 | tf_op jit(solution)/shard_map/concatenate | solution.py:126
  35.0 69.5 %while.11 = (s32[]{:T(128)}, bf16[8,16,6272]{2,1,0:T(8,128)(2,1)}, s32[8,4,16]{2,1,0:T(4,128)S(1)}, s32[8,16]{1,0:T(8,128)S(1)}, f32[95]{0:T(128)S(1)}, /*index=...) while((s32[]{:T(128)}, bf16[8,16,6272]{2,1,0:T(8,128)(2,1)}, ...), condition=%wide.region_5.6_spmd.clone, body=%wide.region_4.5_spmd.clone.sunk | while | flops 476833952 | bytes 10956163 | solution.py:149
  35.1 4.7 %fusion.75 = bf16[16,7,95,128]{3,0,2,1:T(8,128)(2,1)} fusion(bf16[95,168,128]{2,1,0:T(8,128)(2,1)} %get-tuple-element.177, f32[16,7]{0,1:T(8,128)S(1)} %get-tuple-element.153), kind=kOutput, calls=%fused_computation.8.clone.1 | convolution fusion | flops 457699200 | bytes 6810048 | tf_op jit(solution)/shard_map/while/body/eval_jaxpr/dot_general | solution.py:81
  43.8 4.7 %fusion.75 = bf16[16,7,95,128]{3,0,2,1:T(8,128)(2,1)} fusion(bf16[95,168,128]{2,1,0:T(8,128)(2,1)} %get-tuple-element.177, f32[16,7]{0,1:T(8,128)S(1)} %get-tuple-element.153), kind=kOutput, calls=%fused_computation.8.clone.1 | convolution fusion | flops 457699200 | bytes 6810048 | tf_op jit(solution)/shard_map/while/body/eval_jaxpr/dot_general | solution.py:81
  52.5 4.7 %fusion.75 = bf16[16,7,95,128]{3,0,2,1:T(8,128)(2,1)} fusion(bf16[95,168,128]{2,1,0:T(8,128)(2,1)} %get-tuple-element.177, f32[16,7]{0,1:T(8,128)S(1)} %get-tuple-element.153), kind=kOutput, calls=%fused_computation.8.clone.1 | convolution fusion | flops 457699200 | bytes 6810048 | tf_op jit(solution)/shard_map/while/body/eval_jaxpr/dot_general | solution.py:81
  61.1 4.7 %fusion.75 = bf16[16,7,95,128]{3,0,2,1:T(8,128)(2,1)} fusion(bf16[95,168,128]{2,1,0:T(8,128)(2,1)} %get-tuple-element.177, f32[16,7]{0,1:T(8,128)S(1)} %get-tuple-element.153), kind=kOutput, calls=%fused_computation.8.clone.1 | convolution fusion | flops 457699200 | bytes 6810048 | tf_op jit(solution)/shard_map/while/body/eval_jaxpr/dot_general | solution.py:81
  69.8 4.7 %fusion.75 = bf16[16,7,95,128]{3,0,2,1:T(8,128)(2,1)} fusion(bf16[95,168,128]{2,1,0:T(8,128)(2,1)} %get-tuple-element.177, f32[16,7]{0,1:T(8,128)S(1)} %get-tuple-element.153), kind=kOutput, calls=%fused_computation.8.clone.1 | convolution fusion | flops 457699200 | bytes 6810048 | tf_op jit(solution)/shard_map/while/body/eval_jaxpr/dot_general | solution.py:81
  78.5 4.7 %fusion.75 = bf16[16,7,95,128]{3,0,2,1:T(8,128)(2,1)} fusion(bf16[95,168,128]{2,1,0:T(8,128)(2,1)} %get-tuple-element.177, f32[16,7]{0,1:T(8,128)S(1)} %get-tuple-element.153), kind=kOutput, calls=%fused_computation.8.clone.1 | convolution fusion | flops 457699200 | bytes 6810048 | tf_op jit(solution)/shard_map/while/body/eval_jaxpr/dot_general | solution.py:81
  87.2 4.7 %fusion.75 = bf16[16,7,95,128]{3,0,2,1:T(8,128)(2,1)} fusion(bf16[95,168,128]{2,1,0:T(8,128)(2,1)} %get-tuple-element.177, f32[16,7]{0,1:T(8,128)S(1)} %get-tuple-element.153), kind=kOutput, calls=%fused_computation.8.clone.1 | convolution fusion | flops 457699200 | bytes 6810048 | tf_op jit(solution)/shard_map/while/body/eval_jaxpr/dot_general | solution.py:81
  95.9 4.7 %fusion.75 = bf16[16,7,95,128]{3,0,2,1:T(8,128)(2,1)} fusion(bf16[95,168,128]{2,1,0:T(8,128)(2,1)} %get-tuple-element.177, f32[16,7]{0,1:T(8,128)S(1)} %get-tuple-element.153), kind=kOutput, calls=%fused_computation.8.clone.1 | convolution fusion | flops 457699200 | bytes 6810048 | tf_op jit(solution)/shard_map/while/body/eval_jaxpr/dot_general | solution.py:81
  104.5 3.9 %all_to_all.37 = bf16[128,8,784]{2,1,0:T(8,128)(2,1)S(1)} reshape(bf16[8,16,6272]{2,1,0:T(8,128)(2,1)} %get-tuple-element.49) | data formatting | bytes 3211264 | tf_op jit(solution)/shard_map/all_to_all | solution.py:152
  111.0 12.7 %all-to-all-start.1 = ((bf16[128,8,784]{0,2,1:T(8,128)(2,1)}), bf16[128,8,784]{0,2,1:T(8,128)(2,1)S(1)}, u32[]{:S(2)}, u32[]{:S(2)}) async-start(bf16[128,8,784]{0,2,1:T(8,128)(2,1)} %copy.44), calls=%async_computation.1 | async-start | bytes 3211264 | tf_op jit(solution)/shard_map/all_to_all | solution.py:152
  123.7 41.1 %all-to-all-done.1 = bf16[128,8,784]{0,2,1:T(8,128)(2,1)S(1)} async-done(((bf16[128,8,784]{0,2,1:T(8,128)(2,1)}), bf16[128,8,784]{0,2,1:T(8,128)(2,1)S(1)}, u32[]{:S(2)}, u32[]{:S(2)}) %all-to-all-start.1) | async-done | bytes 1605664 | tf_op jit(solution)/shard_map/all_to_all | solution.py:152
  171.7 3.1 fusion.36
  175.0 31.0 %all_to_all.52 = bf16[512,8,128]{2,0,1:T(8,128)(2,1)S(1)} all-to-all(bf16[512,8,128]{2,0,1:T(8,128)(2,1)S(1)} %bitcast.108), channel_id=1, replica_groups=mesh['dp'=64,'tile'=8] {'tile'}, dimensions={1} | all-to-all | bytes 2097152 | tf_op jit(solution)/shard_map/all_to_all | solution.py:162
  206.8 14.3 %all-to-all-start = ((bf16[64,128,16]{1,2,0:T(8,128)(2,1)}), bf16[64,128,16]{1,2,0:T(8,128)(2,1)S(1)}, u32[]{:S(2)}, u32[]{:S(2)}) async-start(bf16[64,128,16]{1,2,0:T(8,128)(2,1)} %broadcast_in_dim.70), calls=%async_computation | async-start | bytes 524288 | tf_op jit(solution)/shard_map/all_to_all | solution.py:17
  221.2 11.8 %all-to-all-done = bf16[64,128,16]{1,2,0:T(8,128)(2,1)S(1)} async-done(((bf16[64,128,16]{1,2,0:T(8,128)(2,1)}), bf16[64,128,16]{1,2,0:T(8,128)(2,1)S(1)}, u32[]{:S(2)}, u32[]{:S(2)}) %all-to-all-start) | async-done | bytes 262176 | tf_op jit(solution)/shard_map/all_to_all | solution.py:17
  234.7 3.6 %all-to-all-start.3 = ((bf16[8,512,128]{1,2,0:T(8,128)(2,1)}), bf16[8,512,128]{1,2,0:T(8,128)(2,1)S(1)}, u32[]{:S(2)}, u32[]{:S(2)}) async-start(bf16[8,512,128]{1,2,0:T(8,128)(2,1)} %broadcast_in_dim.79), calls=%async_computation.3 | async-start | bytes 2097152 | tf_op jit(solution)/shard_map/all_to_all | solution.py:17
  239.5 27.9 %all-to-all-done.3 = bf16[8,512,128]{1,2,0:T(8,128)(2,1)S(1)} async-done(((bf16[8,512,128]{1,2,0:T(8,128)(2,1)}), bf16[8,512,128]{1,2,0:T(8,128)(2,1)S(1)}, u32[]{:S(2)}, u32[]{:S(2)}) %all-to-all-start.3) | async-done | bytes 1048608 | tf_op jit(solution)/shard_map/all_to_all | solution.py:17
  267.4 6.0 %all-to-all-start.5 = ((bf16[64,16,128]{2,1,0:T(8,128)(2,1)}), bf16[64,16,128]{2,1,0:T(8,128)(2,1)S(1)}, u32[]{:S(2)}, u32[]{:S(2)}) async-start(bf16[64,16,128]{2,1,0:T(8,128)(2,1)} %bitcast.28), calls=%async_computation.5 | async-start | bytes 524288 | tf_op jit(solution)/shard_map/all_to_all | solution.py:38
  278.6 6.9 %all-to-all-done.5 = bf16[64,16,128]{2,1,0:T(8,128)(2,1)S(1)} async-done(((bf16[64,16,128]{2,1,0:T(8,128)(2,1)}), bf16[64,16,128]{2,1,0:T(8,128)(2,1)S(1)}, u32[]{:S(2)}, u32[]{:S(2)}) %all-to-all-start.5) | async-done | bytes 262176 | tf_op jit(solution)/shard_map/all_to_all | solution.py:38
  285.4 6.0 %all-to-all-start.4 = ((bf16[64,16,784]{2,1,0:T(8,128)(2,1)}), bf16[64,16,784]{2,1,0:T(8,128)(2,1)S(1)}, u32[]{:S(2)}, u32[]{:S(2)}) async-start(bf16[64,16,784]{2,1,0:T(8,128)(2,1)} %bitcast.25), calls=%async_computation.4 | async-start | bytes 3670016 | tf_op jit(solution)/shard_map/all_to_all | solution.py:38
  292.1 44.7 %all-to-all-done.4 = bf16[64,16,784]{2,1,0:T(8,128)(2,1)S(1)} async-done(((bf16[64,16,784]{2,1,0:T(8,128)(2,1)}), bf16[64,16,784]{2,1,0:T(8,128)(2,1)S(1)}, u32[]{:S(2)}, u32[]{:S(2)}) %all-to-all-start.4) | async-done | bytes 1605664 | tf_op jit(solution)/shard_map/all_to_all | solution.py:38
  (189 shorter events, 63.1 us)
Async XLA Ops:
  7.2 225.9 %copy-start = (bf16[1,512,1024]{2,1,0:T(8,128)(2,1)S(1)}, bf16[1,512,1024]{2,1,0:T(8,128)(2,1)}, u32[]{:S(2)}) copy-start(bf16[1,512,1024]{2,1,0:T(8,128)(2,1)} %param.15) | copy-start | bytes 3145732
  7.2 1.4 slice-start
  7.2 1.5 slice-start.1
  7.2 164.5 %all-gather.2.cloned.1.call-start = ((), (), s32[]{:S(2)}) async-start(), calls=%async_computation.6 | async-start | bytes 1863680 | tf_op jit(solution)/shard_map/all_gather | solution.py:156
  8.7 1.5 copy-start.6
  8.7 6.6 %copy-start.1 = (s32[1,512]{1,0:T(1,128)S(1)}, s32[1,512]{1,0:T(1,128)}, u32[]{:S(2)}) copy-start(s32[1,512]{1,0:T(1,128)} %param.10) | copy-start | bytes 6148
  8.9 20.7 %collective-permute-start = (bf16[16,252,128]{2,0,1:T(8,128)(2,1)S(1)}, bf16[16,252,128]{2,0,1:T(8,128)(2,1)S(1)}, u32[]{:S(2)}, u32[]{:S(2)}) collective-permute-start(bf16[16,252,128]{2,0,1:T(8,128)(2,1)S(1)} %pad_maximum_fusion.1), channel_id=1, source_target_pairs={{1,0},{2,1},{3,2},{4,3},{5,4},{6,5},{7,6},{9,8},{10,9},{11,10},{12... | collective-permute-start | bytes 3096584 | tf_op jit(solution)/shard_map/ppermute | solution.py:12
  29.6 1.0 copy-start.4
  29.9 1.5 copy-start.3
  111.0 53.8 %all-to-all-start.1 = ((bf16[128,8,784]{0,2,1:T(8,128)(2,1)}), bf16[128,8,784]{0,2,1:T(8,128)(2,1)S(1)}, u32[]{:S(2)}, u32[]{:S(2)}) async-start(bf16[128,8,784]{0,2,1:T(8,128)(2,1)} %copy.44), calls=%async_computation.1 | async-start | bytes 3211264 | tf_op jit(solution)/shard_map/all_to_all | solution.py:152
  164.8 1.1 copy-start.2
  174.8 31.2 %copy-start.7 = (bf16[128,16]{0,1:T(8,128)(2,1)S(1)}, bf16[128,16]{0,1:T(8,128)(2,1)}, u32[]{:S(2)}) copy-start(bf16[128,16]{0,1:T(8,128)(2,1)} %param.14) | copy-start | bytes 12292
  206.8 26.3 %all-to-all-start = ((bf16[64,128,16]{1,2,0:T(8,128)(2,1)}), bf16[64,128,16]{1,2,0:T(8,128)(2,1)S(1)}, u32[]{:S(2)}, u32[]{:S(2)}) async-start(bf16[64,128,16]{1,2,0:T(8,128)(2,1)} %broadcast_in_dim.70), calls=%async_computation | async-start | bytes 524288 | tf_op jit(solution)/shard_map/all_to_all | solution.py:17
  234.7 32.7 %all-to-all-start.3 = ((bf16[8,512,128]{1,2,0:T(8,128)(2,1)}), bf16[8,512,128]{1,2,0:T(8,128)(2,1)S(1)}, u32[]{:S(2)}, u32[]{:S(2)}) async-start(bf16[8,512,128]{1,2,0:T(8,128)(2,1)} %broadcast_in_dim.79), calls=%async_computation.3 | async-start | bytes 2097152 | tf_op jit(solution)/shard_map/all_to_all | solution.py:17
  267.4 6.0 %copy-start.5 = (bf16[8,512,128]{1,2,0:T(8,128)(2,1)}, bf16[8,512,128]{1,2,0:T(8,128)(2,1)S(1)}, u32[]{:S(2)}) copy-start(bf16[8,512,128]{1,2,0:T(8,128)(2,1)S(1)} %all-to-all-done.3) | copy-start | bytes 3145732
  267.4 18.0 %all-to-all-start.5 = ((bf16[64,16,128]{2,1,0:T(8,128)(2,1)}), bf16[64,16,128]{2,1,0:T(8,128)(2,1)S(1)}, u32[]{:S(2)}, u32[]{:S(2)}) async-start(bf16[64,16,128]{2,1,0:T(8,128)(2,1)} %bitcast.28), calls=%async_computation.5 | async-start | bytes 524288 | tf_op jit(solution)/shard_map/all_to_all | solution.py:38
  285.4 51.4 %all-to-all-start.4 = ((bf16[64,16,784]{2,1,0:T(8,128)(2,1)}), bf16[64,16,784]{2,1,0:T(8,128)(2,1)S(1)}, u32[]{:S(2)}, u32[]{:S(2)}) async-start(bf16[64,16,784]{2,1,0:T(8,128)(2,1)} %bitcast.25), calls=%async_computation.4 | async-start | bytes 3670016 | tf_op jit(solution)/shard_map/all_to_all | solution.py:38
Sparse Core Ops, SparseCore 0:
  11.3 89.6 all-gather.1
where the time goes:
time: 346 us; the launch traced here: 345 us
  waiting for transfers between devices  145 us (42%)
  matrix products  65.6 us (19%)
  starting transfers between devices  43.9 us (13%)
  local copies, waits for them, and re-layouts  35.5 us (10%)
  blocking collectives  31 us (9%)
  between operations  14.4 us (4%)
  other arithmetic  8.6 us (2%)
    all_to_all x2, waiting for transfers between devices, sent_and_summed(): lax.all_to_all(parts, axis, split_axis=0, concat_axis=0, tiled=True)  51.6 us
    all_to_all x1, waiting for transfers between devices, per_device(): lax.all_to_all(crop_rows, 'tile', split_axis=1, concat_axis=0, tiled=True)  41.1 us
    all_to_all x2, waiting for transfers between devices, sent_to_all(): return lax.all_to_all(copies, axis, split_axis=0, concat_axis=0, tiled=True)  39.8 us
    dot_general x8, matrix products, crop_block(): lax.dot_general(col_low.reshape(count * 7, total_cols), combined, (((1,),...  37.4 us
    all_to_all x1, blocking collectives, per_device(): lax.all_to_all(partial_hidden.astype(jnp.bfloat16), 'tile', split_axis=1,...  31 us
    dot_general x8, matrix products, crop_block(): jnp.einsum('bia,bjac->bijc', row_low.astype(jnp.float32), by_column)  21.7 us
    all_to_all x2, starting transfers between devices, sent_to_all(): return lax.all_to_all(copies, axis, split_axis=0, concat_axis=0, tiled=True)  17.9 us
    ppermute x1, waiting for transfers between devices, from_behind(): return lax.ppermute(block, axis, route)  12.7 us
  transfers between devices with their start and end apart: 7, of which 6 were waited for; matrix products, arithmetic and copies ran while one was open for 28% of the time, Pallas kernels for 0%

commit v1 on v0

v1 whole, which is shorter than its diff:
```python
import jax
import jax.numpy as jnp
from jax import lax
from jax.experimental import pallas as pl
from jax.experimental.pallas import tpu as pltpu
from jax.sharding import Mesh, PartitionSpec as P


REACH = 14
SPAN = 32
GROUP = 8
BF = jnp.bfloat16
F32 = jnp.float32


def gelu_parts(hidden):
    factor = 0.7978845608028654
    cubic_term = 0.044715
    inner_term = factor * (hidden + cubic_term * hidden * hidden * hidden)
    tangent = jnp.tanh(inner_term)
    gelu_value = 0.5 * hidden * (1.0 + tangent)
    gelu_slope = 0.5 * (1.0 + tangent) + 0.5 * hidden * (1.0 - tangent * tangent) * factor * (
        1.0 + 3.0 * cubic_term * hidden * hidden
    )
    return (gelu_value, gelu_slope)


def top_kernel(fine_ref, coarse_ref, fine_top_ref, coarse_top_ref, arrived):
    moves = [
        pltpu.make_async_copy(fine_ref.at[0:REACH], fine_top_ref, arrived.at[0]),
        pltpu.make_async_copy(coarse_ref.at[0:REACH], coarse_top_ref, arrived.at[1]),
    ]
    for move in moves:
        move.start()
    for move in moves:
        move.wait()


def cut_tops(fine, coarse):
    away = pl.BlockSpec(memory_space=pl.ANY)
    return pl.pallas_call(
        top_kernel,
        out_shape=(
            jax.ShapeDtypeStruct((REACH, *fine.shape[1:]), BF),
            jax.ShapeDtypeStruct((REACH, *coarse.shape[1:]), BF),
        ),
        in_specs=[away, away],
        out_specs=(pl.BlockSpec(memory_space=pltpu.VMEM), pl.BlockSpec(memory_space=pltpu.VMEM)),
        scratch_shapes=[pltpu.SemaphoreType.DMA((2,))],
        name="tops",
    )(fine, coarse)


def plan_kernel(band_ref, box_ref, level_ref, slot_ref, ints_ref, reals_ref, *, shape):
    tiles, capacity, fine_rows, coarse_rows, stride = shape
    props = level_ref.shape[1]
    band = band_ref[0]
    top, left, height, width = (box_ref[i : i + 1, :] for i in range(4))
    level = level_ref[...]
    rows_px = stride * fine_rows
    owner = jnp.zeros_like(top)
    for b in range(1, tiles):
        owner = owner + jnp.where(top >= b * rows_px, 1, 0)
    down = (top - owner * rows_px).astype(F32)
    scale = jnp.where(level == 0, 1.0 / stride, 0.5 / stride)
    last = down * scale + 6.5 * height.astype(F32) * (scale / 7.0)
    limit = jnp.where(level == 0, float(fine_rows), float(coarse_rows))
    crosses = jnp.where(last >= limit - 1.01, 1.0, 0.0)
    inside = lax.broadcasted_iota(jnp.int32, (tiles, props), 0) == owner
    late = jnp.where(inside, crosses, 0.0)
    early = jnp.where(inside, 1.0 - crosses, 0.0)
    upto = lax.broadcasted_iota(jnp.int32, (props, props), 0) <= lax.broadcasted_iota(
        jnp.int32, (props, props), 1
    )
    upto = jnp.where(upto, 1.0, 0.0).astype(BF)
    both = jnp.concatenate([early, late], axis=0).astype(BF)
    order = jnp.dot(both, upto, preferred_element_type=F32)
    first = jnp.sum(early, axis=1, keepdims=True)
    every = first + jnp.sum(late, axis=1, keepdims=True)
    rank = early * (order[:tiles] - 1.0) + late * (order[tiles:] + first - 1.0)
    rank = jnp.sum(rank, axis=0, keepdims=True).astype(jnp.int32)
    slot = owner * capacity + rank
    slot_ref[...] = slot
    here = lax.broadcasted_iota(jnp.int32, (capacity, props), 0) + band * capacity == slot
    here = jnp.where(here, 1.0, 0.0).astype(BF)
    fields = jnp.concatenate(
        [
            down,
            (left // 8).astype(F32),
            (left % 8).astype(F32),
            height.astype(F32),
            width.astype(F32),
            level.astype(F32),
            jnp.ones_like(down),
            jnp.zeros_like(down),
        ],
        axis=0,
    ).astype(BF)
    fields = jnp.concatenate([fields, jnp.zeros_like(fields)], axis=0)
    taken = lax.dot_general(fields, here, (((1,), (1,)), ((), ())), preferred_element_type=F32)
    down, left_high, left_low, height, width, level, live = (taken[i : i + 1] for i in range(7))
    scale = jnp.where(level > 0.5, 0.5 / stride, 1.0 / stride)
    step = lax.broadcasted_iota(jnp.int32, (8, capacity), 0).astype(F32) + 0.5
    point = down * scale + step * (height * (scale / 7.0))
    whole = jnp.floor(point)
    near = jnp.maximum(0.0, 1.0 - (point - whole)).astype(BF).astype(F32)
    far = jnp.maximum(0.0, 1.0 - (whole + 1.0 - point)).astype(BF).astype(F32)
    most = jnp.where(level > 0.5, float(coarse_rows), float(fine_rows)) + (REACH - 2.0)
    whole = jnp.clip(whole, 0.0, most) + jnp.where(level > 0.5, fine_rows + float(REACH), 0.0)
    across = (left_high * 8.0 + left_low) * scale
    col = jnp.floor(across * 0.0625) * 16.0
    own = lax.broadcasted_iota(jnp.int32, (tiles, 1), 0) == band
    early_count = jnp.sum(jnp.where(own, first, 0.0), axis=0, keepdims=True)
    every_count = jnp.sum(jnp.where(own, every, 0.0), axis=0, keepdims=True)
    at = lax.broadcasted_iota(jnp.int32, (8, capacity), 0)
    extra = jnp.where(at == 0, col, jnp.where(at == 1, early_count, every_count))
    ints_ref[0:8] = whole.astype(jnp.int32)
    ints_ref[8:16] = extra.astype(jnp.int32)
    reals_ref[0:8] = near * live
    reals_ref[8:16] = far * live
    reals_ref[16:24] = jnp.where(at == 0, across - col, width * (scale / 7.0))


def make_plan(band, boxes, levels, tiles, capacity, fine_rows, coarse_rows, stride):
    smem = pl.BlockSpec(memory_space=pltpu.SMEM)
    vmem = pl.BlockSpec(memory_space=pltpu.VMEM)

    def kernel(*refs):
        plan_kernel(*refs, shape=(tiles, capacity, fine_rows, coarse_rows, stride))

    return pl.pallas_call(
        kernel,
        out_shape=(
            jax.ShapeDtypeStruct(levels.shape, jnp.int32),
            jax.ShapeDtypeStruct((16, capacity), jnp.int32),
            jax.ShapeDtypeStruct((24, capacity), F32),
        ),
        in_specs=[smem, vmem, vmem],
        out_specs=(vmem, vmem, vmem),
        name="plan",
    )(band, boxes, levels)


def fill_maps(maps, fine_ref, coarse_ref, below, arrived):
    fine_rows, fine_cols, channels = fine_ref.shape
    coarse_rows, coarse_cols, _ = coarse_ref.shape
    total, pitch, _ = maps.shape
    base = fine_rows + REACH
    fine_copy = pltpu.make_async_copy(
        fine_ref, maps.at[0:fine_rows, 0:fine_cols, :], arrived.at[0]
    )
    fine_copy.start()
    maps[0:base, fine_cols:pitch, :] = jnp.zeros((base, pitch - fine_cols, channels), BF)
    maps[base:total, :, :] = jnp.zeros((total - base, pitch, channels), BF)
    maps[base : base + coarse_rows, 0:coarse_cols, :] = coarse_ref[...]
    if below is None:
        maps[fine_rows:base, 0:fine_cols, :] = jnp.zeros((REACH, fine_cols, channels), BF)
    else:
        maps[fine_rows:base, 0:fine_cols, :] = below[0][...]
        maps[base + coarse_rows : total, 0:coarse_cols, :] = below[1][...]
    fine_copy.wait()


def fill_cells(bin_ref, cell_ref):
    line = lax.broadcasted_iota(jnp.int32, bin_ref.shape, 0).astype(F32)
    lane = lax.broadcasted_iota(jnp.int32, bin_ref.shape, 1).astype(F32)
    row = jnp.floor((line + 0.5) * (1.0 / 7.0))
    piece = jnp.floor((lane + 0.5) * (1.0 / SPAN))
    bin_ref[...] = line - 7.0 * row + 0.5
    cell_ref[...] = jnp.where(row == piece, lane - SPAN * piece, 1.0e6)


def crop_group(step, ints_ref, reals_ref, bin_ref, cell_ref, maps, parts, crops):
    channels = maps.shape[2]
    bins = parts.shape[1]
    first = step * GROUP
    for g in range(GROUP):
        slot = first + g
        col = pl.multiple_of(ints_ref[8, slot], 16)
        lines = []
        for i in range(7):
            row = ints_ref[i, slot]
            upper = maps[row, pl.ds(col, SPAN), :].astype(F32)
            lower = maps[row + 1, pl.ds(col, SPAN), :].astype(F32)
            lines.append((reals_ref[i, slot] * upper + reals_ref[8 + i, slot] * lower).astype(BF))
        lines.append(jnp.zeros((SPAN, channels), BF))
        stacked = jnp.concatenate(lines, axis=0)
        away = (reals_ref[16, slot] + bin_ref[...] * reals_ref[17, slot]) - cell_ref[...]
        mix = jnp.maximum(0.0, 1.0 - jnp.abs(away)).astype(BF)
        parts[g] = jnp.dot(mix, stacked, preferred_element_type=F32)
    flat = parts.reshape(GROUP * bins, channels)
    start = pl.multiple_of(first, GROUP)
    for m in range(49):
        crops[m, pl.ds(start, GROUP), :] = flat[pl.ds(m, GROUP, stride=bins), :]


def inner_kernel(ints_ref, reals_ref, fine_ref, coarse_ref, crops_ref, maps, parts, bin_ref,
                 cell_ref, arrived):
    fill_cells(bin_ref, cell_ref)
    fill_maps(maps, fine_ref, coarse_ref, None, arrived)

    def body(step, carry):
        crop_group(step, ints_ref, reals_ref, bin_ref, cell_ref, maps, parts, crops_ref)
        return carry

    lax.fori_loop(0, crops_ref.shape[1] // GROUP, body, 0)


def edge_kernel(ints_ref, reals_ref, fine_ref, coarse_ref, fine_below_ref, coarse_below_ref,
                inner_ref, band_ref, *rest):
    *outs, maps, parts, bin_ref, cell_ref, arrived, crops, early, flipped = rest
    channels = fine_ref.shape[2]
    early_copy = pltpu.make_async_copy(inner_ref, early, arrived.at[1])
    early_copy.start()
    fill_cells(bin_ref, cell_ref)
    fill_maps(maps, fine_ref, coarse_ref, (fine_below_ref, coarse_below_ref), arrived)
    low = ints_ref[9, 0] // GROUP
    high = (ints_ref[10, 0] + (GROUP - 1)) // GROUP

    def body(step, carry):
        crop_group(step, ints_ref, reals_ref, bin_ref, cell_ref, maps, parts, crops)
        return carry

    lax.fori_loop(low, high, body, 0)
    early_copy.wait()
    at = lax.broadcasted_iota(jnp.int32, (crops.shape[1], channels), 0)
    redone = (at >= low * GROUP) & (at < high * GROUP)
    for m in range(49):
        block = jnp.where(redone, crops[m], early[m])
        flipped[m * channels : (m + 1) * channels, :] = block.T.astype(BF)
    share = outs[0].shape[0]
    for k, out in enumerate(outs):
        block = (band_ref[0] + k) % len(outs)
        out[...] = flipped[pl.ds(pl.multiple_of(block * share, 16), share), :]


def make_crops(ints, reals, fine, coarse, band, tiles):
    capacity = ints.shape[1]
    channels = fine.shape[2]
    total = fine.shape[0] + coarse.shape[0] + 2 * REACH
    smem = pl.BlockSpec(memory_space=pltpu.SMEM)
    vmem = pl.BlockSpec(memory_space=pltpu.VMEM)
    away = pl.BlockSpec(memory_space=pl.ANY)
    common = [
        pltpu.VMEM((total, 192, channels), BF),
        pltpu.VMEM((GROUP, 56, channels), F32),
        pltpu.VMEM((56, 8 * SPAN), F32),
        pltpu.VMEM((56, 8 * SPAN), F32),
        pltpu.SemaphoreType.DMA((2,)),
    ]
    every = jax.ShapeDtypeStruct((49, capacity, channels), F32)
    params = pltpu.CompilerParams(vmem_limit_bytes=48 << 20)
    inner = pl.pallas_call(
        inner_kernel,
        out_shape=every,
        in_specs=[smem, smem, away, vmem],
        out_specs=vmem,
        scratch_shapes=common,
        compiler_params=params,
        name="inner",
    )
    edge = pl.pallas_call(
        edge_kernel,
        out_shape=[jax.ShapeDtypeStruct((49 * channels // tiles, capacity), BF)] * tiles,
        in_specs=[smem, smem, away, vmem, vmem, vmem, away, smem],
        out_specs=[vmem] * tiles,
        scratch_shapes=common
        + [
            pltpu.VMEM(every.shape, F32),
            pltpu.VMEM(every.shape, F32),
            pltpu.VMEM((49 * channels, capacity), BF),
        ],
        compiler_params=params,
        name="edge",
    )
    early = inner(ints, reals, fine, coarse)
    return early, lambda early, fine_below, coarse_below: edge(
        ints, reals, fine, coarse, fine_below, coarse_below, early, band
    )


def hidden_kernel(band_ref, slot_ref, weight_ref, *rest):
    *recvs, feats_ref, out_ref, joined, pick, arrived = rest
    count = len(recvs)
    share, capacity = recvs[0].shape
    props = slot_ref.shape[1]
    slots = slot_ref[...]
    moves = [
        pltpu.make_async_copy(
            recv, joined.at[:, k * capacity : (k + 1) * capacity], arrived.at[k]
        )
        for k, recv in enumerate(recvs)
    ]
    for move in moves:
        move.start()
    for k in range(count):
        source = (band_ref[0] + count - k) % count
        at = lax.broadcasted_iota(jnp.int32, (capacity, props), 0) + source * capacity
        pick[k * capacity : (k + 1) * capacity, :] = jnp.where(at == slots, 1.0, 0.0).astype(BF)
    for move in moves:
        move.wait()
    feats_ref[...] = jnp.dot(joined[...], pick[...], preferred_element_type=F32).astype(BF)
    skip = weight_ref.shape[1] - share
    out_ref[...] = jnp.dot(
        weight_ref[:, skip:], feats_ref[...], preferred_element_type=F32
    ).astype(BF)


def make_hidden(band, slot_id, weight, recvs):
    share, capacity = recvs[0].shape
    props = slot_id.shape[1]
    smem = pl.BlockSpec(memory_space=pltpu.SMEM)
    vmem = pl.BlockSpec(memory_space=pltpu.VMEM)
    return pl.pallas_call(
        hidden_kernel,
        out_shape=(
            jax.ShapeDtypeStruct((share, props), BF),
            jax.ShapeDtypeStruct((weight.shape[0], props), BF),
        ),
        in_specs=[smem, vmem, vmem] + [pl.BlockSpec(memory_space=pl.ANY)] * len(recvs),
        out_specs=(vmem, vmem),
        scratch_shapes=[
            pltpu.VMEM((share, len(recvs) * capacity), BF),
            pltpu.VMEM((len(recvs) * capacity, props), BF),
            pltpu.SemaphoreType.DMA((len(recvs),)),
        ],
        compiler_params=pltpu.CompilerParams(vmem_limit_bytes=48 << 20),
        name="hidden",
    )(band, slot_id, weight, *recvs)


def act_kernel(pieces_ref, back_ref, act_ref, pre_ref):
    hidden = jnp.sum(pieces_ref[...].astype(F32), axis=0)
    value, slope = gelu_parts(hidden)
    act_ref[...] = value.astype(BF)
    pre = (back_ref[...] * slope).astype(BF)
    for t in range(pre_ref.shape[0]):
        pre_ref[t] = pre


def make_act(pieces, back):
    vmem = pl.BlockSpec(memory_space=pltpu.VMEM)
    return pl.pallas_call(
        act_kernel,
        out_shape=(
            jax.ShapeDtypeStruct(pieces.shape[1:], BF),
            jax.ShapeDtypeStruct(pieces.shape, BF),
        ),
        in_specs=[vmem, vmem],
        out_specs=(vmem, vmem),
        name="act",
    )(pieces, back)


def grads_kernel(core_ref, pre_ref, feats_ref, second_ref, keep_ref, give_ref):
    rows = 256
    unit = keep_ref.shape[1]
    lead = second_ref.shape[1]
    mine = core_ref[0] == 0

    def block(step, carry):
        start = pl.multiple_of(step * rows, rows)
        first = lax.dot_general(
            pre_ref[pl.ds(start, rows), :], feats_ref[...], (((1,), (1,)), ((), ())),
            preferred_element_type=F32,
        ).astype(BF)
        second = second_ref[pl.ds(start, rows), :]
        for n in range(rows // (2 * unit)):
            at = step * (rows // (2 * unit)) + n
            for part, low, high in ((first, lead, keep_ref.shape[2]), (second, 0, lead)):
                even = part[2 * n * unit : (2 * n + 1) * unit]
                odd = part[(2 * n + 1) * unit : (2 * n + 2) * unit]
                keep_ref[at, :, low:high] = jnp.where(mine, even, odd)
                give_ref[at, :, low:high] = jnp.where(mine, odd, even)
        return carry

    lax.fori_loop(0, pre_ref.shape[0] // rows, block, 0)


def make_grads(core, pre, feats, second, unit):
    width = feats.shape[0] + second.shape[1]
    smem = pl.BlockSpec(memory_space=pltpu.SMEM)
    vmem = pl.BlockSpec(memory_space=pltpu.VMEM)
    half = jax.ShapeDtypeStruct((pre.shape[0] // (2 * unit), unit, width), BF)
    return pl.pallas_call(
        grads_kernel,
        out_shape=(half, half),
        in_specs=[smem] + [vmem] * 3,
        out_specs=(vmem, vmem),
        compiler_params=pltpu.CompilerParams(vmem_limit_bytes=48 << 20),
        name="grads",
    )(core, pre, feats, second)


def spread(shard, axis, count):
    copies = jnp.broadcast_to(shard[None], (count, *shard.shape))
    return lax.all_to_all(copies, axis, split_axis=0, concat_axis=0, tiled=True)


def swapped(parts, axis):
    return lax.all_to_all(parts, axis, split_axis=0, concat_axis=0, tiled=True)


def per_device(sizes, proposal_boxes, level_plan, fine_map, coarse_map, first_weight,
               second_weight, upstream):
    nx, nz, nc, tile_count = sizes
    dp = ("x", "z", "core")
    dp_count = nx * nz * nc
    band = lax.axis_index("tile")
    fine = fine_map[0]
    coarse = coarse_map[0]
    up = [(i + 1, i) for i in range(tile_count - 1)]
    fine_top, coarse_top = cut_tops(fine, coarse)
    fine_below = lax.ppermute(fine_top, "tile", up)
    coarse_below = lax.ppermute(coarse_top, "tile", up)
    mine = lax.axis_index("core")
    band_at = band[None].astype(jnp.int32)
    num_props = level_plan.shape[1]
    capacity = max(num_props // 4, num_props // tile_count)
    unit = first_weight.shape[1]
    lead = second_weight.shape[0]
    upstream_rows = upstream[0]

    slot_id, ints, reals = make_plan(
        band_at, proposal_boxes[0], level_plan, tile_count, capacity, fine.shape[0],
        coarse.shape[0], 4,
    )
    early, edge = make_crops(ints, reals, fine, coarse, band_at, tile_count)
    shard = jnp.concatenate([second_weight.T, first_weight.T], axis=1)
    shard, early = lax.optimization_barrier((shard, early))
    weights = spread(shard, dp, dp_count).reshape(-1, shard.shape[1])
    crops = edge(early, fine_below, coarse_below)
    recvs = {0: crops[0]}
    for k in range(1, tile_count):
        route = [(i, (i + k) % tile_count) for i in range(tile_count)]
        recvs[k] = lax.ppermute(crops[k], "tile", route)
    weights, recvs[0] = lax.optimization_barrier((weights, recvs[0]))
    recvs = [recvs[k] for k in range(tile_count)]
    back_grad = lax.dot_general(
        weights[:, :lead], upstream_rows, (((0,), (1,)), ((), ())), preferred_element_type=F32
    )
    back_grad, weights = lax.optimization_barrier((back_grad, weights))
    feats, partial_hidden = make_hidden(band_at, slot_id, weights, recvs)
    pieces = swapped(partial_hidden.reshape(tile_count, -1, num_props), "tile")
    activated, copies = make_act(pieces, back_grad)
    pre_grad = swapped(copies, "tile").reshape(-1, num_props)
    second = lax.dot_general(
        upstream_rows, activated, (((0,), (1,)), ((), ())), preferred_element_type=F32
    ).astype(BF)
    core_at = mine[None].astype(jnp.int32)
    keep, give = make_grads(core_at, pre_grad, feats, second, unit)
    got = lax.ppermute(give, "core", [(0, 1), (1, 0)])
    both = (keep.astype(F32) + got.astype(F32)).astype(BF).reshape(nx, nz, unit, -1)
    both = swapped(both, "x").astype(F32).sum(axis=0).astype(BF)
    total = swapped(both, "z").astype(F32).sum(axis=0)
    return (total[:, lead:].T, total[:, :lead].T)


def solution(mesh):
    tile_count = mesh.shape["tile"]
    sizes = (4, mesh.shape["dp"] // 8, 2, tile_count)
    split = Mesh(mesh.devices.reshape(sizes), ("x", "z", "core", "tile"))
    dp = ("x", "z", "core")
    placed = (
        P(dp, None, None),
        P(dp, None),
        P(dp, "tile", None, None),
        P(dp, "tile", None, None),
        P("tile", dp),
        P("tile", dp),
        P(dp, None, None),
    )

    def step(*args):
        return per_device(sizes, *args)

    return jax.shard_map(
        step,
        mesh=split,
        in_specs=placed,
        out_specs=(P("tile", dp), P("tile", dp)),
        check_vma=False,
    )
```

time: 346 us -> 235 us (0.68)
  waiting for transfers between devices: 145 us -> 71.8 us
  matrix products: 65.6 us -> 2.69 us
  blocking collectives: 31 us -> 66.3 us
  Pallas kernels: 0 us -> 25.8 us
  local copies, waits for them, and re-layouts: 35.5 us -> 9.77 us
  between operations: 14.4 us -> 0.92 us
  starting transfers between devices: 43.9 us -> 53.7 us
  other arithmetic: 8.6 us -> 1.53 us
    all_to_all x5 -> x2, waiting for transfers between devices: 132 us -> 26.7 us  [the longest x1 26.7 us: swapped(): return lax.all_to_all(parts, axis, split_axis=0, concat_axis=0, tiled=True)]
    dot_general x20 -> x2, matrix products: 65.6 us -> 2.69 us  [the longest x1 2.14 us: per_device(): lax.dot_general(weights[:, :lead], upstream_rows, (((0,), (1,)), ((), ())...]
    all_to_all x1 -> x3, blocking collectives: 31 us -> 66.3 us  [swapped(): return lax.all_to_all(parts, axis, split_axis=0, concat_axis=0, tiled=True)]
    ppermute x1 -> x10, starting transfers between devices: 1.29 us -> 34.9 us  [the longest x7 28.1 us: per_device(): recvs[k] = lax.ppermute(crops[k], 'tile', route)]
    ppermute x1 -> x10, waiting for transfers between devices: 12.7 us -> 45.1 us  [the longest x7 21.9 us: per_device(): recvs[k] = lax.ppermute(crops[k], 'tile', route)]
    pallas_call x0 -> x7, Pallas kernels: none -> 25.8 us  [the longest x1 8.22 us: make_crops(): early = inner(ints, reals, fine, coarse)]
    all_to_all x5 -> x2, starting transfers between devices: 42.6 us -> 18.8 us  [the longest x1 15.1 us: spread(): return lax.all_to_all(copies, axis, split_axis=0, concat_axis=0, tiled=True)]
    all_to_all x4 -> x0, local copies, waits for them, and re-layouts: 9.68 us -> none  [the longest x3 9.49 us: per_device(): lax.all_to_all(crop_rows, 'tile', split_axis=1, concat_axis=0, tiled=True)]
  transfers between devices with their start and end apart: 7 -> 12, of which waited for: 6 -> 7; matrix products, arithmetic and copies ran while one was open for 28% -> 1% of each run, Pallas kernels for 0% -> 3%
where the time goes in v1:
time: 235 us; the launch traced here: 233 us
  waiting for transfers between devices  71.8 us (31%)
  blocking collectives  66.3 us (28%)
  starting transfers between devices  53.7 us (23%)
  Pallas kernels  25.8 us (11%)
  local copies, waits for them, and re-layouts  9.77 us (4%)
  matrix products  2.69 us (1%)
    all_to_all x3, blocking collectives, swapped(): return lax.all_to_all(parts, axis, split_axis=0, concat_axis=0, tiled=True)  66.3 us
    ppermute x7, starting transfers between devices, per_device(): recvs[k] = lax.ppermute(crops[k], 'tile', route)  28.1 us
    all_to_all x1, waiting for transfers between devices, swapped(): return lax.all_to_all(parts, axis, split_axis=0, concat_axis=0, tiled=True)  26.7 us
    ppermute x7, waiting for transfers between devices, per_device(): recvs[k] = lax.ppermute(crops[k], 'tile', route)  21.9 us
    ppermute x1, waiting for transfers between devices, per_device(): coarse_below = lax.ppermute(coarse_top, 'tile', up)  21 us
    all_to_all x1, starting transfers between devices, spread(): return lax.all_to_all(copies, axis, split_axis=0, concat_axis=0, tiled=True)  15.1 us
    pallas_call x1, Pallas kernels, make_crops(): early = inner(ints, reals, fine, coarse)  8.22 us
    unnamed x28, local copies, waits for them, and re-layouts  6.97 us
  transfers between devices with their start and end apart: 12, of which 7 were waited for; matrix products, arithmetic and copies ran while one was open for 1% of the time, Pallas kernels for 3%

profile of v1, /device:TPU:1, one launch (start us, length us, event | category | flops | bytes accessed | tf_op | source)
XLA Modules:
  0.0 232.5 jit_solution(4095361743192217386)
XLA Ops:
  7.2 8.2 %inner.1.inner_ref = f32[49,128,128]{2,1,0:T(8,128)S(1)} custom-call(s32[16,128]{1,0:T(8,128)S(1)} %copy-done.8, f32[24,128]{1,0:T(8,128)S(1)} %copy-done.6, bf16[42,168,128]{2,1,0:T(8,128)(2,1)S(1)} %bitcast.24, bf16[21,84,128]{2,1,0:T(8,128)(2,1)S(1)} %bitcast.27), custom_call_target="tpu_custom_call" | custom-call | tf_op jit(solution)/shard_map/inner/pallas_call | solution.py:276
  18.6 15.1 %all-to-all-start = ((bf16[64,16,912]{2,1,0:T(8,128)(2,1)}), bf16[64,16,912]{2,1,0:T(8,128)(2,1)}, u32[]{:S(2)}, u32[]{:S(2)}) async-start(bf16[64,16,912]{2,1,0:T(8,128)(2,1)} %broadcast_in_dim.14), calls=%async_computation | async-start | bytes 4194304 | tf_op jit(solution)/shard_map/all_to_all | solution.py:397
  33.8 2.3 %tops.1 = (bf16[14,168,128]{2,1,0:T(8,128)(2,1)}, bf16[14,84,128]{2,1,0:T(8,128)(2,1)}) custom-call(bf16[42,168,128]{2,1,0:T(8,128)(2,1)} %bitcast.23, bf16[21,84,128]{2,1,0:T(8,128)(2,1)} %bitcast.26), custom_call_target="tpu_custom_call" | custom-call | tf_op jit(solution)/shard_map/tops/pallas_call | solution.py:41
  38.7 21.0 %collective-permute-done.1.coarse_below_ref = bf16[14,84,128]{2,1,0:T(8,128)(2,1)S(1)} collective-permute-done((bf16[14,84,128]{2,1,0:T(8,128)(2,1)}, bf16[14,84,128]{2,1,0:T(8,128)(2,1)S(1)}, u32[]{:S(2)}, u32[]{:S(2)}) %collective-permute-start.1) | collective-permute-done | bytes 301088 | tf_op jit(solution)/shard_map/ppermute | solution.py:415
  59.8 4.7 %edge.1 = (bf16[784,128]{1,0:T(8,128)(2,1)S(1)}, bf16[784,128]{1,0:T(8,128)(2,1)}, bf16[784,128]{1,0:T(8,128)(2,1)}, bf16[784,128]{1,0:T(8,128)(2,1)}, bf16[784,...) custom-call(s32[16,128]{1,0:T(8,128)S(1)} %copy-done.9, ...), custom_call_target="tpu_custom_call" | custom-call | tf_op jit(solution)/shard_map/edge/pallas_call | solution.py:277
  65.9 2.9 %collective-permute-start.2 = (bf16[784,128]{1,0:T(8,128)(2,1)}, bf16[784,128]{1,0:T(8,128)(2,1)S(1)}, u32[]{:S(2)}, u32[]{:S(2)}) collective-permute-start(bf16[784,128]{1,0:T(8,128)(2,1)} %get-tuple-element.38), channel_id=1, source_target_pairs={{0,1},{1,2},{2,3},{3,4},{4,5},{5,6},{6,7},{7,0},{8,9},{9,10},{10,1... | collective-permute-start | bytes 602120 | tf_op jit(solution)/shard_map/ppermute | solution.py:436
  68.7 5.4 %collective-permute-start.3 = (bf16[784,128]{1,0:T(8,128)(2,1)}, bf16[784,128]{1,0:T(8,128)(2,1)S(1)}, u32[]{:S(2)}, u32[]{:S(2)}) collective-permute-start(bf16[784,128]{1,0:T(8,128)(2,1)} %get-tuple-element.39), channel_id=1, source_target_pairs={{0,2},{1,3},{2,4},{3,5},{4,6},{5,7},{6,0},{7,1},{8,10},{9,11},{10,... | collective-permute-start | bytes 602120 | tf_op jit(solution)/shard_map/ppermute | solution.py:436
  74.2 3.4 %collective-permute-start.4 = (bf16[784,128]{1,0:T(8,128)(2,1)}, bf16[784,128]{1,0:T(8,128)(2,1)S(1)}, u32[]{:S(2)}, u32[]{:S(2)}) collective-permute-start(bf16[784,128]{1,0:T(8,128)(2,1)} %get-tuple-element.40), channel_id=1, source_target_pairs={{0,3},{1,4},{2,5},{3,6},{4,7},{5,0},{6,1},{7,2},{8,11},{9,12},{10,... | collective-permute-start | bytes 602120 | tf_op jit(solution)/shard_map/ppermute | solution.py:436
  77.6 3.5 %collective-permute-start.5 = (bf16[784,128]{1,0:T(8,128)(2,1)}, bf16[784,128]{1,0:T(8,128)(2,1)S(1)}, u32[]{:S(2)}, u32[]{:S(2)}) collective-permute-start(bf16[784,128]{1,0:T(8,128)(2,1)} %get-tuple-element.41), channel_id=1, source_target_pairs={{0,4},{1,5},{2,6},{3,7},{4,0},{5,1},{6,2},{7,3},{8,12},{9,13},{10,... | collective-permute-start | bytes 602120 | tf_op jit(solution)/shard_map/ppermute | solution.py:436
  81.2 4.5 %collective-permute-start.6 = (bf16[784,128]{1,0:T(8,128)(2,1)}, bf16[784,128]{1,0:T(8,128)(2,1)S(1)}, u32[]{:S(2)}, u32[]{:S(2)}) collective-permute-start(bf16[784,128]{1,0:T(8,128)(2,1)} %get-tuple-element.42), channel_id=1, source_target_pairs={{0,5},{1,6},{2,7},{3,0},{4,1},{5,2},{6,3},{7,4},{8,13},{9,14},{10,... | collective-permute-start | bytes 602120 | tf_op jit(solution)/shard_map/ppermute | solution.py:436
  85.7 5.4 %collective-permute-start.7 = (bf16[784,128]{1,0:T(8,128)(2,1)}, bf16[784,128]{1,0:T(8,128)(2,1)S(1)}, u32[]{:S(2)}, u32[]{:S(2)}) collective-permute-start(bf16[784,128]{1,0:T(8,128)(2,1)} %copy-done.12), channel_id=1, source_target_pairs={{0,6},{1,7},{2,0},{3,1},{4,2},{5,3},{6,4},{7,5},{8,14},{9,15},{10,... | collective-permute-start | bytes 602120 | tf_op jit(solution)/shard_map/ppermute | solution.py:436
  91.0 3.0 %collective-permute-start.8 = (bf16[784,128]{1,0:T(8,128)(2,1)}, bf16[784,128]{1,0:T(8,128)(2,1)S(1)}, u32[]{:S(2)}, u32[]{:S(2)}) collective-permute-start(bf16[784,128]{1,0:T(8,128)(2,1)} %copy-done.11), channel_id=1, source_target_pairs={{0,7},{1,0},{2,1},{3,2},{4,3},{5,4},{6,5},{7,6},{8,15},{9,8},{10,9... | collective-permute-start | bytes 602120 | tf_op jit(solution)/shard_map/ppermute | solution.py:436
  96.2 5.0 %collective-permute-done.5.rest_4_ = bf16[784,128]{1,0:T(8,128)(2,1)S(1)} collective-permute-done((bf16[784,128]{1,0:T(8,128)(2,1)}, bf16[784,128]{1,0:T(8,128)(2,1)S(1)}, u32[]{:S(2)}, u32[]{:S(2)}) %collective-permute-start.5) | collective-permute-done | bytes 200736 | tf_op jit(solution)/shard_map/ppermute | solution.py:436
  101.2 5.3 %collective-permute-done.6.rest_5_ = bf16[784,128]{1,0:T(8,128)(2,1)S(1)} collective-permute-done((bf16[784,128]{1,0:T(8,128)(2,1)}, bf16[784,128]{1,0:T(8,128)(2,1)S(1)}, u32[]{:S(2)}, u32[]{:S(2)}) %collective-permute-start.6) | collective-permute-done | bytes 200736 | tf_op jit(solution)/shard_map/ppermute | solution.py:436
  106.5 8.4 %collective-permute-done.7.rest_6_ = bf16[784,128]{1,0:T(8,128)(2,1)S(1)} collective-permute-done((bf16[784,128]{1,0:T(8,128)(2,1)}, bf16[784,128]{1,0:T(8,128)(2,1)S(1)}, u32[]{:S(2)}, u32[]{:S(2)}) %collective-permute-start.7) | collective-permute-done | bytes 200736 | tf_op jit(solution)/shard_map/ppermute | solution.py:436
  114.8 3.2 %collective-permute-done.8.rest_7_ = bf16[784,128]{1,0:T(8,128)(2,1)S(1)} collective-permute-done((bf16[784,128]{1,0:T(8,128)(2,1)}, bf16[784,128]{1,0:T(8,128)(2,1)S(1)}, u32[]{:S(2)}, u32[]{:S(2)}) %collective-permute-start.8) | collective-permute-done | bytes 200736 | tf_op jit(solution)/shard_map/ppermute | solution.py:436
  118.0 4.3 %hidden.1 = (bf16[784,512]{1,0:T(8,128)(2,1)S(1)}, bf16[1024,512]{1,0:T(8,128)(2,1)S(1)}) custom-call(s32[1]{0:T(128)} %bitcast.1.refs_0_.band_ref, s32[1,512]{1,0:T(1,128)S(1)} %copy-done.10, bf16[1024,912]{1,0:T(8,128)(2,1)} %bitcast.7.weight_ref, bf16[784,128]{1,0:T(8,128)(2,1)S(1)} %get-tuple-element.37.rest_0_, ...), custom_call_target="tpu_custom_call" | custom-call | tf_op jit(solution)/shard_map/hidden/pallas_call | solution.py:314
  122.3 31.5 %all_to_all.25.pieces_ref = bf16[8,128,512]{2,1,0:T(8,128)(2,1)} all-to-all(bf16[8,128,512]{2,1,0:T(8,128)(2,1)S(1)} %bitcast.30), channel_id=1, replica_groups=mesh['x'=4,'z'=8,'core'=2,'tile'=8] {'tile'}, dimensions={0} | all-to-all | bytes 2097152 | tf_op jit(solution)/shard_map/all_to_all | solution.py:401
  153.8 2.6 %act.1 = (bf16[128,512]{1,0:T(8,128)(2,1)}, bf16[8,128,512]{2,1,0:T(8,128)(2,1)}) custom-call(bf16[8,128,512]{2,1,0:T(8,128)(2,1)} %all_to_all.25.pieces_ref, f32[128,512]{1,0:T(8,128)} %fusion.2.back_ref), custom_call_target="tpu_custom_call" | custom-call | tf_op jit(solution)/shard_map/act/pallas_call | solution.py:343
  156.4 3.7 %all-to-all-start.2 = ((bf16[8,128,512]{2,1,0:T(8,128)(2,1)}), bf16[8,128,512]{2,1,0:T(8,128)(2,1)S(1)}, u32[]{:S(2)}, u32[]{:S(2)}) async-start(bf16[8,128,512]{2,1,0:T(8,128)(2,1)} %get-tuple-element.47), calls=%async_computation.2 | async-start | bytes 2097152 | tf_op jit(solution)/shard_map/all_to_all | solution.py:401
  160.7 26.7 %all-to-all-done.2 = bf16[8,128,512]{2,1,0:T(8,128)(2,1)S(1)} async-done(((bf16[8,128,512]{2,1,0:T(8,128)(2,1)}), bf16[8,128,512]{2,1,0:T(8,128)(2,1)S(1)}, u32[]{:S(2)}, u32[]{:S(2)}) %all-to-all-start.2) | async-done | bytes 1048608 | tf_op jit(solution)/shard_map/all_to_all | solution.py:401
  189.3 4.2 %collective-permute-start.9 = (bf16[32,16,912]{2,1,0:T(8,128)(2,1)S(1)}, bf16[32,16,912]{2,1,0:T(8,128)(2,1)S(1)}, u32[]{:S(2)}, u32[]{:S(2)}) collective-permute-start(bf16[32,16,912]{2,1,0:T(8,128)(2,1)S(1)} %get-tuple-element.51), channel_id=1, source_target_pairs={{0,8},{8,0},{1,9},{9,1},{2,10},{10,2},{3,11},{11,3},{4,12},{12,4},... | collective-permute-start | bytes 2801672 | tf_op jit(solution)/shard_map/ppermute | solution.py:452
  196.2 19.3 %all_to_all.26 = bf16[4,8,16,912]{3,2,1,0:T(8,128)(2,1)S(1)} all-to-all(bf16[4,8,16,912]{3,2,1,0:T(8,128)(2,1)S(1)} %bitcast.31), channel_id=1, replica_groups=mesh['x'=4,'z'=8,'core'=2,'tile'=8] {'x'}, dimensions={0} | all-to-all | bytes 1867776 | tf_op jit(solution)/shard_map/all_to_all | solution.py:401
  215.8 15.5 %all_to_all.27 = bf16[8,16,912]{2,1,0:T(8,128)(2,1)S(1)} all-to-all(bf16[8,16,912]{2,1,0:T(8,128)(2,1)S(1)} %reduce_sum.21), channel_id=1, replica_groups=mesh['x'=4,'z'=8,'core'=2,'tile'=8] {'z'}, dimensions={0} | all-to-all | bytes 466944 | tf_op jit(solution)/shard_map/all_to_all | solution.py:401
  (47 shorter events, 22.5 us)
Async XLA Ops:
  0.6 93.4 %copy-start = (bf16[1,512,1024]{2,1,0:T(8,128)(2,1)S(1)}, bf16[1,512,1024]{2,1,0:T(8,128)(2,1)}, u32[]{:S(2)}) copy-start(bf16[1,512,1024]{2,1,0:T(8,128)(2,1)} %param.13) | copy-start | bytes 3145732
  3.2 1.5 copy-start.1
  4.7 1.0 copy-start.4
  5.7 0.7 copy-start.6
  6.5 0.7 copy-start.8
  15.4 1.7 copy-start.3
  18.6 41.1 %copy-start.7 = (f32[24,128]{1,0:T(8,128)S(1)}, f32[24,128]{1,0:T(8,128)}, u32[]{:S(2)}) copy-start(f32[24,128]{1,0:T(8,128)} %get-tuple-element.29.reals_ref) | copy-start | bytes 36868
  18.6 41.1 %copy-start.9 = (s32[16,128]{1,0:T(8,128)S(1)}, s32[16,128]{1,0:T(8,128)}, u32[]{:S(2)}) copy-start(s32[16,128]{1,0:T(8,128)} %get-tuple-element.28.ints_ref) | copy-start | bytes 24580
  18.6 67.0 %all-to-all-start = ((bf16[64,16,912]{2,1,0:T(8,128)(2,1)}), bf16[64,16,912]{2,1,0:T(8,128)(2,1)}, u32[]{:S(2)}, u32[]{:S(2)}) async-start(bf16[64,16,912]{2,1,0:T(8,128)(2,1)} %broadcast_in_dim.14), calls=%async_computation | async-start | bytes 4194304 | tf_op jit(solution)/shard_map/all_to_all | solution.py:397
  33.8 26.0 %copy-start.2 = (bf16[1,42,168,128]{3,2,1,0:T(8,128)(2,1)S(1)}, bf16[1,42,168,128]{3,2,1,0:T(8,128)(2,1)}, u32[]{:S(2)}) copy-start(bf16[1,42,168,128]{3,2,1,0:T(8,128)(2,1)} %param.9) | copy-start | bytes 5419012
  33.8 26.0 %copy-start.5 = (bf16[1,21,84,128]{3,2,1,0:T(8,128)(2,1)S(1)}, bf16[1,21,84,128]{3,2,1,0:T(8,128)(2,1)}, u32[]{:S(2)}) copy-start(bf16[1,21,84,128]{3,2,1,0:T(8,128)(2,1)} %param.10) | copy-start | bytes 1354756
  36.1 23.6 %collective-permute-start = (bf16[14,168,128]{2,1,0:T(8,128)(2,1)}, bf16[14,168,128]{2,1,0:T(8,128)(2,1)S(1)}, u32[]{:S(2)}, u32[]{:S(2)}) collective-permute-start(bf16[14,168,128]{2,1,0:T(8,128)(2,1)} %get-tuple-element.31), channel_id=1, source_target_pairs={{1,0},{2,1},{3,2},{4,3},{5,4},{6,5},{7,6},{9,8},{10,9},{11,10},{12... | collective-permute-start | bytes 1806344 | tf_op jit(solution)/shard_map/ppermute | solution.py:414
  37.4 80.6 %copy-start.10 = (s32[1,512]{1,0:T(1,128)S(1)}, s32[1,512]{1,0:T(1,128)}, u32[]{:S(2)}) copy-start(s32[1,512]{1,0:T(1,128)} %get-tuple-element.27.slot_ref) | copy-start | bytes 6148
  37.4 22.3 %collective-permute-start.1 = (bf16[14,84,128]{2,1,0:T(8,128)(2,1)}, bf16[14,84,128]{2,1,0:T(8,128)(2,1)S(1)}, u32[]{:S(2)}, u32[]{:S(2)}) collective-permute-start(bf16[14,84,128]{2,1,0:T(8,128)(2,1)} %get-tuple-element.32), channel_id=1, source_target_pairs={{1,0},{2,1},{3,2},{4,3},{5,4},{6,5},{7,6},{9,8},{10,9},{11,10},{12... | collective-permute-start | bytes 903176 | tf_op jit(solution)/shard_map/ppermute | solution.py:415
  65.9 19.8 %collective-permute-start.2 = (bf16[784,128]{1,0:T(8,128)(2,1)}, bf16[784,128]{1,0:T(8,128)(2,1)S(1)}, u32[]{:S(2)}, u32[]{:S(2)}) collective-permute-start(bf16[784,128]{1,0:T(8,128)(2,1)} %get-tuple-element.38), channel_id=1, source_target_pairs={{0,1},{1,2},{2,3},{3,4},{4,5},{5,6},{6,7},{7,0},{8,9},{9,10},{10,1... | collective-permute-start | bytes 602120 | tf_op jit(solution)/shard_map/ppermute | solution.py:436
  68.7 22.3 %collective-permute-start.3 = (bf16[784,128]{1,0:T(8,128)(2,1)}, bf16[784,128]{1,0:T(8,128)(2,1)S(1)}, u32[]{:S(2)}, u32[]{:S(2)}) collective-permute-start(bf16[784,128]{1,0:T(8,128)(2,1)} %get-tuple-element.39), channel_id=1, source_target_pairs={{0,2},{1,3},{2,4},{3,5},{4,6},{5,7},{6,0},{7,1},{8,10},{9,11},{10,... | collective-permute-start | bytes 602120 | tf_op jit(solution)/shard_map/ppermute | solution.py:436
  74.2 22.0 %collective-permute-start.4 = (bf16[784,128]{1,0:T(8,128)(2,1)}, bf16[784,128]{1,0:T(8,128)(2,1)S(1)}, u32[]{:S(2)}, u32[]{:S(2)}) collective-permute-start(bf16[784,128]{1,0:T(8,128)(2,1)} %get-tuple-element.40), channel_id=1, source_target_pairs={{0,3},{1,4},{2,5},{3,6},{4,7},{5,0},{6,1},{7,2},{8,11},{9,12},{10,... | collective-permute-start | bytes 602120 | tf_op jit(solution)/shard_map/ppermute | solution.py:436
  77.6 23.6 %collective-permute-start.5 = (bf16[784,128]{1,0:T(8,128)(2,1)}, bf16[784,128]{1,0:T(8,128)(2,1)S(1)}, u32[]{:S(2)}, u32[]{:S(2)}) collective-permute-start(bf16[784,128]{1,0:T(8,128)(2,1)} %get-tuple-element.41), channel_id=1, source_target_pairs={{0,4},{1,5},{2,6},{3,7},{4,0},{5,1},{6,2},{7,3},{8,12},{9,13},{10,... | collective-permute-start | bytes 602120 | tf_op jit(solution)/shard_map/ppermute | solution.py:436
  81.2 25.3 %collective-permute-start.6 = (bf16[784,128]{1,0:T(8,128)(2,1)}, bf16[784,128]{1,0:T(8,128)(2,1)S(1)}, u32[]{:S(2)}, u32[]{:S(2)}) collective-permute-start(bf16[784,128]{1,0:T(8,128)(2,1)} %get-tuple-element.42), channel_id=1, source_target_pairs={{0,5},{1,6},{2,7},{3,0},{4,1},{5,2},{6,3},{7,4},{8,13},{9,14},{10,... | collective-permute-start | bytes 602120 | tf_op jit(solution)/shard_map/ppermute | solution.py:436
  85.7 29.2 %collective-permute-start.7 = (bf16[784,128]{1,0:T(8,128)(2,1)}, bf16[784,128]{1,0:T(8,128)(2,1)S(1)}, u32[]{:S(2)}, u32[]{:S(2)}) collective-permute-start(bf16[784,128]{1,0:T(8,128)(2,1)} %copy-done.12), channel_id=1, source_target_pairs={{0,6},{1,7},{2,0},{3,1},{4,2},{5,3},{6,4},{7,5},{8,14},{9,15},{10,... | collective-permute-start | bytes 602120 | tf_op jit(solution)/shard_map/ppermute | solution.py:436
  91.0 27.0 %collective-permute-start.8 = (bf16[784,128]{1,0:T(8,128)(2,1)}, bf16[784,128]{1,0:T(8,128)(2,1)S(1)}, u32[]{:S(2)}, u32[]{:S(2)}) collective-permute-start(bf16[784,128]{1,0:T(8,128)(2,1)} %copy-done.11), channel_id=1, source_target_pairs={{0,7},{1,0},{2,1},{3,2},{4,3},{5,4},{6,5},{7,6},{8,15},{9,8},{10,9... | collective-permute-start | bytes 602120 | tf_op jit(solution)/shard_map/ppermute | solution.py:436
  156.4 3.7 %copy-start.13 = (bf16[128,512]{1,0:T(8,128)(2,1)S(1)}, bf16[128,512]{1,0:T(8,128)(2,1)}, u32[]{:S(2)}) copy-start(bf16[128,512]{1,0:T(8,128)(2,1)} %get-tuple-element.49) | copy-start | bytes 393220
  156.4 31.0 %all-to-all-start.2 = ((bf16[8,128,512]{2,1,0:T(8,128)(2,1)}), bf16[8,128,512]{2,1,0:T(8,128)(2,1)S(1)}, u32[]{:S(2)}, u32[]{:S(2)}) async-start(bf16[8,128,512]{2,1,0:T(8,128)(2,1)} %get-tuple-element.47), calls=%async_computation.2 | async-start | bytes 2097152 | tf_op jit(solution)/shard_map/all_to_all | solution.py:401
  189.3 6.5 %collective-permute-start.9 = (bf16[32,16,912]{2,1,0:T(8,128)(2,1)S(1)}, bf16[32,16,912]{2,1,0:T(8,128)(2,1)S(1)}, u32[]{:S(2)}, u32[]{:S(2)}) collective-permute-start(bf16[32,16,912]{2,1,0:T(8,128)(2,1)S(1)} %get-tuple-element.51), channel_id=1, source_target_pairs={{0,8},{8,0},{1,9},{9,1},{2,10},{10,2},{3,11},{11,3},{4,12},{12,4},... | collective-permute-start | bytes 2801672 | tf_op jit(solution)/shard_map/ppermute | solution.py:452
  (2 other events, 1.4 us)

commit v2 on v1

--- a/solution.py
+++ b/solution.py
@@ -9,6 +9,7 @@
 REACH = 14
 SPAN = 32
 GROUP = 8
+TURNS = (4, 7, 1, 6, 2, 5, 3)
 BF = jnp.bfloat16
 F32 = jnp.float32
 
@@ -37,7 +38,7 @@
 
 
 def cut_tops(fine, coarse):
-    away = pl.BlockSpec(memory_space=pl.ANY)
+    away = pl.BlockSpec(memory_space=pltpu.HBM)
     return pl.pallas_call(
         top_kernel,
         out_shape=(
@@ -47,8 +48,35 @@
         in_specs=[away, away],
         out_specs=(pl.BlockSpec(memory_space=pltpu.VMEM), pl.BlockSpec(memory_space=pltpu.VMEM)),
         scratch_shapes=[pltpu.SemaphoreType.DMA((2,))],
+        compiler_params=pltpu.CompilerParams(vmem_limit_bytes=60 << 20),
         name="tops",
     )(fine, coarse)
+
+
+def copies_kernel(first_ref, second_ref, out_ref):
+    lead = second_ref.shape[1]
+    first = first_ref[...]
+    second = second_ref[...]
+
+    def body(i, carry):
+        out_ref[i, :, 0:lead] = second
+        out_ref[i, :, lead:] = first
+        return carry
+
+    lax.fori_loop(0, out_ref.shape[0], body, 0)
+
+
+def make_copies(first, second, count):
+    vmem = pl.BlockSpec(memory_space=pltpu.VMEM)
+    width = first.shape[1] + second.shape[1]
+    return pl.pallas_call(
+        copies_kernel,
+        out_shape=jax.ShapeDtypeStruct((count, first.shape[0], width), BF),
+        in_specs=[vmem, vmem],
+        out_specs=vmem,
+        compiler_params=pltpu.CompilerParams(vmem_limit_bytes=8 << 20),
+        name="copies",
+    )(first, second)
 
 
 def plan_kernel(band_ref, box_ref, level_ref, slot_ref, ints_ref, reals_ref, *, shape):
@@ -137,6 +165,7 @@
         ),
         in_specs=[smem, vmem, vmem],
         out_specs=(vmem, vmem, vmem),
+        compiler_params=pltpu.CompilerParams(vmem_limit_bytes=8 << 20),
         name="plan",
     )(band, boxes, levels)
 
@@ -162,12 +191,10 @@
 
 
 def fill_cells(bin_ref, cell_ref):
-    line = lax.broadcasted_iota(jnp.int32, bin_ref.shape, 0).astype(F32)
-    lane = lax.broadcasted_iota(jnp.int32, bin_ref.shape, 1).astype(F32)
-    row = jnp.floor((line + 0.5) * (1.0 / 7.0))
-    piece = jnp.floor((lane + 0.5) * (1.0 / SPAN))
-    bin_ref[...] = line - 7.0 * row + 0.5
-    cell_ref[...] = jnp.where(row == piece, lane - SPAN * piece, 1.0e6)
+    line = lax.broadcasted_iota(jnp.int32, bin_ref.shape, 0)
+    lane = lax.broadcasted_iota(jnp.int32, bin_ref.shape, 1)
+    bin_ref[...] = line.astype(F32) + 0.5
+    cell_ref[...] = (lane % SPAN).astype(F32)
 
 
 def crop_group(step, ints_ref, reals_ref, bin_ref, cell_ref, maps, parts, crops):
@@ -180,18 +207,24 @@
         lines = []
         for i in range(7):
             row = ints_ref[i, slot]
-            upper = maps[row, pl.ds(col, SPAN), :].astype(F32)
-            lower = maps[row + 1, pl.ds(col, SPAN), :].astype(F32)
-            lines.append((reals_ref[i, slot] * upper + reals_ref[8 + i, slot] * lower).astype(BF))
+            upper = maps[row, pl.ds(col, SPAN), :]
+            lower = maps[row + 1, pl.ds(col, SPAN), :]
+            near = jnp.full(upper.shape, reals_ref[i, slot], F32).astype(BF)
+            far = jnp.full(upper.shape, reals_ref[8 + i, slot], F32).astype(BF)
+            lines.append(near * upper + far * lower)
         lines.append(jnp.zeros((SPAN, channels), BF))
         stacked = jnp.concatenate(lines, axis=0)
         away = (reals_ref[16, slot] + bin_ref[...] * reals_ref[17, slot]) - cell_ref[...]
-        mix = jnp.maximum(0.0, 1.0 - jnp.abs(away)).astype(BF)
+        line = jnp.maximum(0.0, 1.0 - jnp.abs(away))
+        piece = lax.broadcasted_iota(jnp.int32, line.shape, 1) // SPAN
+        mix = [jnp.where(piece == i, line, 0.0) for i in range(7)]
+        mix = jnp.concatenate(mix, axis=0).astype(BF)
         parts[g] = jnp.dot(mix, stacked, preferred_element_type=F32)
     flat = parts.reshape(GROUP * bins, channels)
     start = pl.multiple_of(first, GROUP)
     for m in range(49):
-        crops[m, pl.ds(start, GROUP), :] = flat[pl.ds(m, GROUP, stride=bins), :]
+        at = m // 7 * 8 + m % 7
+        crops[m, pl.ds(start, GROUP), :] = flat[pl.ds(at, GROUP, stride=bins), :]
 
 
 def inner_kernel(ints_ref, reals_ref, fine_ref, coarse_ref, crops_ref, maps, parts, bin_ref,
@@ -240,16 +273,16 @@
     total = fine.shape[0] + coarse.shape[0] + 2 * REACH
     smem = pl.BlockSpec(memory_space=pltpu.SMEM)
     vmem = pl.BlockSpec(memory_space=pltpu.VMEM)
-    away = pl.BlockSpec(memory_space=pl.ANY)
+    away = pl.BlockSpec(memory_space=pltpu.HBM)
     common = [
         pltpu.VMEM((total, 192, channels), BF),
         pltpu.VMEM((GROUP, 56, channels), F32),
-        pltpu.VMEM((56, 8 * SPAN), F32),
-        pltpu.VMEM((56, 8 * SPAN), F32),
+        pltpu.VMEM((8, 8 * SPAN), F32),
+        pltpu.VMEM((8, 8 * SPAN), F32),
         pltpu.SemaphoreType.DMA((2,)),
     ]
     every = jax.ShapeDtypeStruct((49, capacity, channels), F32)
-    params = pltpu.CompilerParams(vmem_limit_bytes=48 << 20)
+    params = pltpu.CompilerParams(vmem_limit_bytes=24 << 20)
     inner = pl.pallas_call(
         inner_kernel,
         out_shape=every,
@@ -279,11 +312,8 @@
     )
 
 
-def hidden_kernel(band_ref, slot_ref, weight_ref, *rest):
-    *recvs, feats_ref, out_ref, joined, pick, arrived = rest
-    count = len(recvs)
-    share, capacity = recvs[0].shape
-    props = slot_ref.shape[1]
+def pick_rows(turns, band_ref, slot_ref, recvs, joined, pick, arrived):
+    count, capacity = band_ref[1], recvs[0].shape[1]
     slots = slot_ref[...]
     moves = [
         pltpu.make_async_copy(
@@ -293,40 +323,73 @@
     ]
     for move in moves:
         move.start()
-    for k in range(count):
-        source = (band_ref[0] + count - k) % count
-        at = lax.broadcasted_iota(jnp.int32, (capacity, props), 0) + source * capacity
+    for k, turn in enumerate(turns):
+        source = (band_ref[0] + count - turn) % count
+        at = lax.broadcasted_iota(jnp.int32, (capacity, slots.shape[1]), 0) + source * capacity
         pick[k * capacity : (k + 1) * capacity, :] = jnp.where(at == slots, 1.0, 0.0).astype(BF)
     for move in moves:
         move.wait()
-    feats_ref[...] = jnp.dot(joined[...], pick[...], preferred_element_type=F32).astype(BF)
-    skip = weight_ref.shape[1] - share
-    out_ref[...] = jnp.dot(
-        weight_ref[:, skip:], feats_ref[...], preferred_element_type=F32
-    ).astype(BF)
-
-
-def make_hidden(band, slot_id, weight, recvs):
+    return jnp.dot(joined[...], pick[...], preferred_element_type=F32)
+
+
+def make_gather(band, slot_id, recvs, turns):
     share, capacity = recvs[0].shape
     props = slot_id.shape[1]
+    count = len(recvs)
     smem = pl.BlockSpec(memory_space=pltpu.SMEM)
     vmem = pl.BlockSpec(memory_space=pltpu.VMEM)
+
+    def gather_kernel(band_ref, slot_ref, *rest):
+        *pieces, out_ref, joined, pick, arrived = rest
+        out_ref[...] = pick_rows(turns, band_ref, slot_ref, pieces, joined, pick, arrived).astype(BF)
+
+    return pl.pallas_call(
+        gather_kernel,
+        out_shape=jax.ShapeDtypeStruct((share, props), BF),
+        in_specs=[smem, vmem] + [pl.BlockSpec(memory_space=pl.ANY)] * count,
+        out_specs=vmem,
+        scratch_shapes=[
+            pltpu.VMEM((share, count * capacity), BF),
+            pltpu.VMEM((count * capacity, props), BF),
+            pltpu.SemaphoreType.DMA((count,)),
+        ],
+        compiler_params=pltpu.CompilerParams(vmem_limit_bytes=16 << 20),
+        name="gather",
+    )(band, slot_id, *recvs)
+
+
+def make_hidden(band, slot_id, weight, begun, recvs, turns):
+    share, capacity = recvs[0].shape
+    props = slot_id.shape[1]
+    count = len(recvs)
+    smem = pl.BlockSpec(memory_space=pltpu.SMEM)
+    vmem = pl.BlockSpec(memory_space=pltpu.VMEM)
+
+    def hidden_kernel(band_ref, slot_ref, weight_ref, begun_ref, *rest):
+        *pieces, feats_ref, out_ref, joined, pick, arrived = rest
+        late = pick_rows(turns, band_ref, slot_ref, pieces, joined, pick, arrived)
+        feats_ref[...] = begun_ref[...] + late.astype(BF)
+        skip = weight_ref.shape[1] - share
+        out_ref[...] = jnp.dot(
+            weight_ref[:, skip:], feats_ref[...], preferred_element_type=F32
+        ).astype(BF)
+
     return pl.pallas_call(
         hidden_kernel,
         out_shape=(
             jax.ShapeDtypeStruct((share, props), BF),
             jax.ShapeDtypeStruct((weight.shape[0], props), BF),
         ),
-        in_specs=[smem, vmem, vmem] + [pl.BlockSpec(memory_space=pl.ANY)] * len(recvs),
+        in_specs=[smem, vmem, vmem, vmem] + [pl.BlockSpec(memory_space=pl.ANY)] * count,
         out_specs=(vmem, vmem),
         scratch_shapes=[
-            pltpu.VMEM((share, len(recvs) * capacity), BF),
-            pltpu.VMEM((len(recvs) * capacity, props), BF),
-            pltpu.SemaphoreType.DMA((len(recvs),)),
+            pltpu.VMEM((share, count * capacity), BF),
+            pltpu.VMEM((count * capacity, props), BF),
+            pltpu.SemaphoreType.DMA((count,)),
         ],
-        compiler_params=pltpu.CompilerParams(vmem_limit_bytes=48 << 20),
+        compiler_params=pltpu.CompilerParams(vmem_limit_bytes=24 << 20),
         name="hidden",
-    )(band, slot_id, weight, *recvs)
+    )(band, slot_id, weight, begun, *recvs)
 
 
 def act_kernel(pieces_ref, back_ref, act_ref, pre_ref):
@@ -348,6 +411,7 @@
         ),
         in_specs=[vmem, vmem],
         out_specs=(vmem, vmem),
+        compiler_params=pltpu.CompilerParams(vmem_limit_bytes=8 << 20),
         name="act",
     )(pieces, back)
 
@@ -387,14 +451,32 @@
         out_shape=(half, half),
         in_specs=[smem] + [vmem] * 3,
         out_specs=(vmem, vmem),
-        compiler_params=pltpu.CompilerParams(vmem_limit_bytes=48 << 20),
+        compiler_params=pltpu.CompilerParams(vmem_limit_bytes=24 << 20),
         name="grads",
     )(core, pre, feats, second)
 
 
-def spread(shard, axis, count):
-    copies = jnp.broadcast_to(shard[None], (count, *shard.shape))
-    return lax.all_to_all(copies, axis, split_axis=0, concat_axis=0, tiled=True)
+def finish_kernel(pieces_ref, first_ref, second_ref):
+    total = jnp.sum(pieces_ref[...].astype(F32), axis=0)
+    lead = second_ref.shape[1]
+    second_ref[...] = total[:, :lead]
+    first_ref[...] = total[:, lead:]
+
+
+def make_finish(pieces, lead):
+    vmem = pl.BlockSpec(memory_space=pltpu.VMEM)
+    rows, width = pieces.shape[1:]
+    return pl.pallas_call(
+        finish_kernel,
+        out_shape=(
+            jax.ShapeDtypeStruct((rows, width - lead), F32),
+            jax.ShapeDtypeStruct((rows, lead), F32),
+        ),
+        in_specs=[vmem],
+        out_specs=(vmem, vmem),
+        compiler_params=pltpu.CompilerParams(vmem_limit_bytes=8 << 20),
+        name="finish",
+    )(pieces)
 
 
 def swapped(parts, axis):
@@ -426,21 +508,24 @@
         coarse.shape[0], 4,
     )
     early, edge = make_crops(ints, reals, fine, coarse, band_at, tile_count)
-    shard = jnp.concatenate([second_weight.T, first_weight.T], axis=1)
-    shard, early = lax.optimization_barrier((shard, early))
-    weights = spread(shard, dp, dp_count).reshape(-1, shard.shape[1])
+    copies = make_copies(first_weight.T, second_weight.T, dp_count)
+    weights = swapped(copies, dp).reshape(-1, copies.shape[2])
     crops = edge(early, fine_below, coarse_below)
     recvs = {0: crops[0]}
     for k in range(1, tile_count):
         route = [(i, (i + k) % tile_count) for i in range(tile_count)]
         recvs[k] = lax.ppermute(crops[k], "tile", route)
-    weights, recvs[0] = lax.optimization_barrier((weights, recvs[0]))
-    recvs = [recvs[k] for k in range(tile_count)]
+    gather_at = jnp.stack([band, jnp.int32(tile_count)]).astype(jnp.int32)
+    soon, late = (0, *TURNS[:4]), TURNS[4:]
+    begun = make_gather(gather_at, slot_id, [recvs[k] for k in soon], soon)
+    weights, begun = lax.optimization_barrier((weights, begun))
     back_grad = lax.dot_general(
         weights[:, :lead], upstream_rows, (((0,), (1,)), ((), ())), preferred_element_type=F32
     )
     back_grad, weights = lax.optimization_barrier((back_grad, weights))
-    feats, partial_hidden = make_hidden(band_at, slot_id, weights, recvs)
+    feats, partial_hidden = make_hidden(
+        gather_at, slot_id, weights, begun, [recvs[k] for k in late], late
+    )
     pieces = swapped(partial_hidden.reshape(tile_count, -1, num_props), "tile")
     activated, copies = make_act(pieces, back_grad)
     pre_grad = swapped(copies, "tile").reshape(-1, num_props)
@@ -451,9 +536,9 @@
     keep, give = make_grads(core_at, pre_grad, feats, second, unit)
     got = lax.ppermute(give, "core", [(0, 1), (1, 0)])
     both = (keep.astype(F32) + got.astype(F32)).astype(BF).reshape(nx, nz, unit, -1)
-    both = swapped(both, "x").astype(F32).sum(axis=0).astype(BF)
-    total = swapped(both, "z").astype(F32).sum(axis=0)
-    return (total[:, lead:].T, total[:, :lead].T)
+    total = swapped(both, "x").astype(F32).sum(axis=0)
+    first_grad, second_grad = make_finish(swapped(total.astype(BF), "z"), lead)
+    return (first_grad.T, second_grad.T)
 
 
 def solution(mesh):

time: 235 us -> 207 us (0.88)
  waiting for transfers between devices: 71.8 us -> 53.4 us
  local copies, waits for them, and re-layouts: 9.77 us -> 1.55 us
  starting transfers between devices: 53.7 us -> 50.6 us
  blocking collectives: 66.3 us -> 68.8 us
    all_to_all x1 -> x0, starting transfers between devices: 15.1 us -> none  [spread(): return lax.all_to_all(copies, axis, split_axis=0, concat_axis=0, tiled=True)]
    all_to_all x1 -> x2, starting transfers between devices: 3.69 us -> 18.6 us  [swapped(): return lax.all_to_all(parts, axis, split_axis=0, concat_axis=0, tiled=True)]
    ppermute x7, waiting for transfers between devices: 21.9 us -> 11.9 us  [per_device(): recvs[k] = lax.ppermute(crops[k], 'tile', route)]
    ppermute x1, waiting for transfers between devices: 21 us -> 12.4 us  [per_device(): coarse_below = lax.ppermute(coarse_top, 'tile', up)]
    unnamed x28 -> x14, local copies, waits for them, and re-layouts: 6.97 us -> 1.55 us
    pallas_call x0 -> x3, Pallas kernels: none -> 3.93 us  [the longest x1 1.67 us: make_copies(): pl.pallas_call(copies_kernel, out_shape=jax.ShapeDtypeStruct((count, firs...]
    ppermute x7, starting transfers between devices: 28.1 us -> 25.5 us  [per_device(): recvs[k] = lax.ppermute(crops[k], 'tile', route)]
    all_to_all x3, blocking collectives: 66.3 us -> 68.8 us  [swapped(): return lax.all_to_all(parts, axis, split_axis=0, concat_axis=0, tiled=True)]
  transfers between devices with their start and end apart: 12 -> 12, of which waited for: 7 -> 5; matrix products, arithmetic and copies ran while one was open for 1% -> 1% of each run, Pallas kernels for 3% -> 9%
where the time goes in v2:
time: 207 us; the launch traced here: 205 us
  blocking collectives  68.8 us (33%)
  waiting for transfers between devices  53.4 us (26%)
  starting transfers between devices  50.6 us (24%)
  Pallas kernels  26.6 us (13%)
    all_to_all x3, blocking collectives, swapped(): return lax.all_to_all(parts, axis, split_axis=0, concat_axis=0, tiled=True)  68.8 us
    all_to_all x2, waiting for transfers between devices, swapped(): return lax.all_to_all(parts, axis, split_axis=0, concat_axis=0, tiled=True)  27 us
    ppermute x7, starting transfers between devices, per_device(): recvs[k] = lax.ppermute(crops[k], 'tile', route)  25.5 us
    all_to_all x2, starting transfers between devices, swapped(): return lax.all_to_all(parts, axis, split_axis=0, concat_axis=0, tiled=True)  18.6 us
    ppermute x1, waiting for transfers between devices, per_device(): coarse_below = lax.ppermute(coarse_top, 'tile', up)  12.4 us
    ppermute x7, waiting for transfers between devices, per_device(): recvs[k] = lax.ppermute(crops[k], 'tile', route)  11.9 us
    pallas_call x1, Pallas kernels, make_crops(): early = inner(ints, reals, fine, coarse)  8.14 us
    pallas_call x1, Pallas kernels, make_crops(): edge(ints, reals, fine, coarse, fine_below, coarse_below, early, band)  5.11 us
  transfers between devices with their start and end apart: 12, of which 5 were waited for; matrix products, arithmetic and copies ran while one was open for 1% of the time, Pallas kernels for 9%

profile of v2, /device:TPU:1, one launch (start us, length us, event | category | flops | bytes accessed | tf_op | source)
XLA Modules:
  0.0 204.7 jit_solution(12536393841682457531)
XLA Ops:
  2.2 1.7 copies.1
  3.8 15.0 %all-to-all-start = ((bf16[64,16,912]{2,1,0:T(8,128)(2,1)}), bf16[64,16,912]{2,1,0:T(8,128)(2,1)}, u32[]{:S(2)}, u32[]{:S(2)}) async-start(bf16[64,16,912]{2,1,0:T(8,128)(2,1)} %copies.1), calls=%async_computation | async-start | bytes 4194304 | tf_op jit(solution)/shard_map/all_to_all | solution.py:483
  18.9 2.3 %tops.1 = (bf16[14,168,128]{2,1,0:T(8,128)(2,1)}, bf16[14,84,128]{2,1,0:T(8,128)(2,1)}) custom-call(bf16[42,168,128]{2,1,0:T(8,128)(2,1)} %bitcast.21, bf16[21,84,128]{2,1,0:T(8,128)(2,1)} %bitcast.24), custom_call_target="tpu_custom_call" | custom-call | tf_op jit(solution)/shard_map/tops/pallas_call | solution.py:42
  24.3 8.1 %inner.1.inner_ref = f32[49,128,128]{2,1,0:T(8,128)S(1)} custom-call(s32[16,128]{1,0:T(8,128)S(1)} %get-tuple-element.28.ints_ref, f32[24,128]{1,0:T(8,128)S(1)} %get-tuple-element.29.reals_ref, bf16[42,168,128]{2,1,0:T(8,128)(2,1)S(1)} %bitcast.22, bf16[21,84,128]{2,1,0:T(8,128)(2,1)S(1)} %bitcast.25), custom_call_target="tpu_custom_call" | custom-call | tf_op jit(solution)/shard_map/inner/pallas_call | solution.py:309
  32.4 12.4 %collective-permute-done.1.coarse_below_ref = bf16[14,84,128]{2,1,0:T(8,128)(2,1)} collective-permute-done((bf16[14,84,128]{2,1,0:T(8,128)(2,1)}, bf16[14,84,128]{2,1,0:T(8,128)(2,1)}, u32[]{:S(2)}, u32[]{:S(2)}) %collective-permute-start.1) | collective-permute-done | bytes 301088 | tf_op jit(solution)/shard_map/ppermute | solution.py:497
  44.8 5.1 %edge.1 = (bf16[784,128]{1,0:T(8,128)(2,1)S(1)}, bf16[784,128]{1,0:T(8,128)(2,1)S(1)}, bf16[784,128]{1,0:T(8,128)(2,1)}, bf16[784,128]{1,0:T(8,128)(2,1)}, bf16[...) custom-call(s32[16,128]{1,0:T(8,128)S(1)} %get-tuple-element.28.ints, ...), custom_call_target="tpu_custom_call" | custom-call | tf_op jit(solution)/shard_map/edge/pallas_call | solution.py:310
  49.9 6.6 %collective-permute-start.2 = (bf16[784,128]{1,0:T(8,128)(2,1)S(1)}, bf16[784,128]{1,0:T(8,128)(2,1)S(1)}, u32[]{:S(2)}, u32[]{:S(2)}) collective-permute-start(bf16[784,128]{1,0:T(8,128)(2,1)S(1)} %get-tuple-element.33), channel_id=1, source_target_pairs={{0,4},{1,5},{2,6},{3,7},{4,0},{5,1},{6,2},{7,3},{8,12},{9,13},{10,... | collective-permute-start | bytes 602120 | tf_op jit(solution)/shard_map/ppermute | solution.py:517
  56.5 3.7 %collective-permute-start.3 = (bf16[784,128]{1,0:T(8,128)(2,1)S(1)}, bf16[784,128]{1,0:T(8,128)(2,1)S(1)}, u32[]{:S(2)}, u32[]{:S(2)}) collective-permute-start(bf16[784,128]{1,0:T(8,128)(2,1)S(1)} %get-tuple-element.34), channel_id=1, source_target_pairs={{0,7},{1,0},{2,1},{3,2},{4,3},{5,4},{6,5},{7,6},{8,15},{9,8},{10,9... | collective-permute-start | bytes 602120 | tf_op jit(solution)/shard_map/ppermute | solution.py:517
  60.2 1.9 collective-permute-start.4
  62.2 3.1 %collective-permute-start.5 = (bf16[784,128]{1,0:T(8,128)(2,1)S(1)}, bf16[784,128]{1,0:T(8,128)(2,1)S(1)}, u32[]{:S(2)}, u32[]{:S(2)}) collective-permute-start(bf16[784,128]{1,0:T(8,128)(2,1)S(1)} %get-tuple-element.36), channel_id=1, source_target_pairs={{0,6},{1,7},{2,0},{3,1},{4,2},{5,3},{6,4},{7,5},{8,14},{9,15},{10,... | collective-permute-start | bytes 602120 | tf_op jit(solution)/shard_map/ppermute | solution.py:517
  65.3 3.1 %collective-permute-start.6 = (bf16[784,128]{1,0:T(8,128)(2,1)}, bf16[784,128]{1,0:T(8,128)(2,1)S(1)}, u32[]{:S(2)}, u32[]{:S(2)}) collective-permute-start(bf16[784,128]{1,0:T(8,128)(2,1)} %get-tuple-element.40), channel_id=1, source_target_pairs={{0,2},{1,3},{2,4},{3,5},{4,6},{5,7},{6,0},{7,1},{8,10},{9,11},{10,... | collective-permute-start | bytes 602120 | tf_op jit(solution)/shard_map/ppermute | solution.py:517
  68.4 4.3 %collective-permute-start.7 = (bf16[784,128]{1,0:T(8,128)(2,1)}, bf16[784,128]{1,0:T(8,128)(2,1)S(1)}, u32[]{:S(2)}, u32[]{:S(2)}) collective-permute-start(bf16[784,128]{1,0:T(8,128)(2,1)} %get-tuple-element.41), channel_id=1, source_target_pairs={{0,5},{1,6},{2,7},{3,0},{4,1},{5,2},{6,3},{7,4},{8,13},{9,14},{10,... | collective-permute-start | bytes 602120 | tf_op jit(solution)/shard_map/ppermute | solution.py:517
  72.8 2.8 %collective-permute-start.8 = (bf16[784,128]{1,0:T(8,128)(2,1)}, bf16[784,128]{1,0:T(8,128)(2,1)S(1)}, u32[]{:S(2)}, u32[]{:S(2)}) collective-permute-start(bf16[784,128]{1,0:T(8,128)(2,1)} %get-tuple-element.42), channel_id=1, source_target_pairs={{0,3},{1,4},{2,5},{3,6},{4,7},{5,0},{6,1},{7,2},{8,11},{9,12},{10,... | collective-permute-start | bytes 602120 | tf_op jit(solution)/shard_map/ppermute | solution.py:517
  75.6 3.8 %collective-permute-done.5.rest_4_ = bf16[784,128]{1,0:T(8,128)(2,1)S(1)} collective-permute-done((bf16[784,128]{1,0:T(8,128)(2,1)S(1)}, bf16[784,128]{1,0:T(8,128)(2,1)S(1)}, u32[]{:S(2)}, u32[]{:S(2)}) %collective-permute-start.5) | collective-permute-done | bytes 200736 | tf_op jit(solution)/shard_map/ppermute | solution.py:517
  82.4 8.0 %collective-permute-done.7.rest_1_ = bf16[784,128]{1,0:T(8,128)(2,1)S(1)} collective-permute-done((bf16[784,128]{1,0:T(8,128)(2,1)}, bf16[784,128]{1,0:T(8,128)(2,1)S(1)}, u32[]{:S(2)}, u32[]{:S(2)}) %collective-permute-start.7) | collective-permute-done | bytes 200736 | tf_op jit(solution)/shard_map/ppermute | solution.py:517
  90.5 3.4 %hidden.1 = (bf16[784,512]{1,0:T(8,128)(2,1)S(1)}, bf16[1024,512]{1,0:T(8,128)(2,1)S(1)}) custom-call(s32[2]{0:T(128)S(1)} %pad_add_fusion.band_ref, s32[1,512]{1,0:T(1,128)S(1)} %get-tuple-element.27.slot_ref, bf16[1024,912]{1,0:T(8,128)(2,1)} %bitcast.5.weight_ref, bf16[784,512]{1,0:T(8,128)(2,1)S(1)} %gather.1.begun_ref, ...), custom_call_target="tpu_custom_call" | custom-call | tf_op jit(solution)/shard_map/hidden/pallas_call | solution.py:377
  93.9 34.6 %all_to_all.25.pieces_ref = bf16[8,128,512]{2,1,0:T(8,128)(2,1)S(1)} all-to-all(bf16[8,128,512]{2,1,0:T(8,128)(2,1)S(1)} %bitcast.28), channel_id=1, replica_groups=mesh['x'=4,'z'=8,'core'=2,'tile'=8] {'tile'}, dimensions={0} | all-to-all | bytes 2097152 | tf_op jit(solution)/shard_map/all_to_all | solution.py:483
  129.9 3.6 %all-to-all-start.2 = ((bf16[8,128,512]{2,1,0:T(8,128)(2,1)}), bf16[8,128,512]{2,1,0:T(8,128)(2,1)S(1)}, u32[]{:S(2)}, u32[]{:S(2)}) async-start(bf16[8,128,512]{2,1,0:T(8,128)(2,1)} %get-tuple-element.45), calls=%async_computation.2 | async-start | bytes 2097152 | tf_op jit(solution)/shard_map/all_to_all | solution.py:483
  134.1 26.9 %all-to-all-done.2 = bf16[8,128,512]{2,1,0:T(8,128)(2,1)S(1)} async-done(((bf16[8,128,512]{2,1,0:T(8,128)(2,1)}), bf16[8,128,512]{2,1,0:T(8,128)(2,1)S(1)}, u32[]{:S(2)}, u32[]{:S(2)}) %all-to-all-start.2) | async-done | bytes 1048608 | tf_op jit(solution)/shard_map/all_to_all | solution.py:483
  161.0 1.9 grads.1
  162.9 4.0 %collective-permute-start.9 = (bf16[32,16,912]{2,1,0:T(8,128)(2,1)S(1)}, bf16[32,16,912]{2,1,0:T(8,128)(2,1)S(1)}, u32[]{:S(2)}, u32[]{:S(2)}) collective-permute-start(bf16[32,16,912]{2,1,0:T(8,128)(2,1)S(1)} %get-tuple-element.49), channel_id=1, source_target_pairs={{0,8},{8,0},{1,9},{9,1},{2,10},{10,2},{3,11},{11,3},{4,12},{12,4},... | collective-permute-start | bytes 2801672 | tf_op jit(solution)/shard_map/ppermute | solution.py:537
  166.9 2.3 %collective-permute-done.9 = bf16[32,16,912]{2,1,0:T(8,128)(2,1)S(1)} collective-permute-done((bf16[32,16,912]{2,1,0:T(8,128)(2,1)S(1)}, bf16[32,16,912]{2,1,0:T(8,128)(2,1)S(1)}, u32[]{:S(2)}, u32[]{:S(2)}) %collective-permute-start.9) | collective-permute-done | bytes 933920 | tf_op jit(solution)/shard_map/ppermute | solution.py:537
  169.6 18.6 %all_to_all.26 = bf16[4,8,16,912]{3,2,1,0:T(8,128)(2,1)S(1)} all-to-all(bf16[4,8,16,912]{3,2,1,0:T(8,128)(2,1)S(1)} %bitcast.32), channel_id=1, replica_groups=mesh['x'=4,'z'=8,'core'=2,'tile'=8] {'x'}, dimensions={0} | all-to-all | bytes 1867776 | tf_op jit(solution)/shard_map/all_to_all | solution.py:483
  188.4 15.6 %all_to_all.27.pieces_ref = bf16[8,16,912]{2,1,0:T(8,128)(2,1)S(1)} all-to-all(bf16[8,16,912]{2,1,0:T(8,128)(2,1)S(1)} %reduce_sum.12), channel_id=1, replica_groups=mesh['x'=4,'z'=8,'core'=2,'tile'=8] {'z'}, dimensions={0} | all-to-all | bytes 466944 | tf_op jit(solution)/shard_map/all_to_all | solution.py:483
  (32 shorter events, 10.9 us)
Async XLA Ops:
  0.6 80.3 %copy-start = (bf16[1,512,1024]{2,1,0:T(8,128)(2,1)S(1)}, bf16[1,512,1024]{2,1,0:T(8,128)(2,1)}, u32[]{:S(2)}) copy-start(bf16[1,512,1024]{2,1,0:T(8,128)(2,1)} %param.13) | copy-start | bytes 3145732
  0.6 0.8 copy-start.3
  1.5 0.7 copy-start.5
  3.8 77.1 %all-to-all-start = ((bf16[64,16,912]{2,1,0:T(8,128)(2,1)}), bf16[64,16,912]{2,1,0:T(8,128)(2,1)}, u32[]{:S(2)}, u32[]{:S(2)}) async-start(bf16[64,16,912]{2,1,0:T(8,128)(2,1)} %copies.1), calls=%async_computation | async-start | bytes 4194304 | tf_op jit(solution)/shard_map/all_to_all | solution.py:483
  18.9 4.9 %copy-start.4 = (s32[1,4,512]{2,1,0:T(4,128)S(1)}, s32[1,4,512]{2,1,0:T(4,128)}, u32[]{:S(2)}) copy-start(s32[1,4,512]{2,1,0:T(4,128)} %param.7) | copy-start | bytes 24580
  18.9 4.9 %copy-start.6 = (s32[1,512]{1,0:T(1,128)S(1)}, s32[1,512]{1,0:T(1,128)}, u32[]{:S(2)}) copy-start(s32[1,512]{1,0:T(1,128)} %refs_2_.1) | copy-start | bytes 6148
  18.9 5.4 %copy-start.1 = (bf16[1,42,168,128]{3,2,1,0:T(8,128)(2,1)S(1)}, bf16[1,42,168,128]{3,2,1,0:T(8,128)(2,1)}, u32[]{:S(2)}) copy-start(bf16[1,42,168,128]{3,2,1,0:T(8,128)(2,1)} %param.9) | copy-start | bytes 5419012
  18.9 5.4 %copy-start.2 = (bf16[1,21,84,128]{3,2,1,0:T(8,128)(2,1)S(1)}, bf16[1,21,84,128]{3,2,1,0:T(8,128)(2,1)}, u32[]{:S(2)}) copy-start(bf16[1,21,84,128]{3,2,1,0:T(8,128)(2,1)} %param.10) | copy-start | bytes 1354756
  21.2 23.6 %collective-permute-start = (bf16[14,168,128]{2,1,0:T(8,128)(2,1)}, bf16[14,168,128]{2,1,0:T(8,128)(2,1)}, u32[]{:S(2)}, u32[]{:S(2)}) collective-permute-start(bf16[14,168,128]{2,1,0:T(8,128)(2,1)} %get-tuple-element.30), channel_id=1, source_target_pairs={{1,0},{2,1},{3,2},{4,3},{5,4},{6,5},{7,6},{9,8},{10,9},{11,10},{12... | collective-permute-start | bytes 1806344 | tf_op jit(solution)/shard_map/ppermute | solution.py:496
  22.5 22.3 %collective-permute-start.1 = (bf16[14,84,128]{2,1,0:T(8,128)(2,1)}, bf16[14,84,128]{2,1,0:T(8,128)(2,1)}, u32[]{:S(2)}, u32[]{:S(2)}) collective-permute-start(bf16[14,84,128]{2,1,0:T(8,128)(2,1)} %get-tuple-element.31), channel_id=1, source_target_pairs={{1,0},{2,1},{3,2},{4,3},{5,4},{6,5},{7,6},{9,8},{10,9},{11,10},{12... | collective-permute-start | bytes 903176 | tf_op jit(solution)/shard_map/ppermute | solution.py:497
  49.9 18.5 %collective-permute-start.2 = (bf16[784,128]{1,0:T(8,128)(2,1)S(1)}, bf16[784,128]{1,0:T(8,128)(2,1)S(1)}, u32[]{:S(2)}, u32[]{:S(2)}) collective-permute-start(bf16[784,128]{1,0:T(8,128)(2,1)S(1)} %get-tuple-element.33), channel_id=1, source_target_pairs={{0,4},{1,5},{2,6},{3,7},{4,0},{5,1},{6,2},{7,3},{8,12},{9,13},{10,... | collective-permute-start | bytes 602120 | tf_op jit(solution)/shard_map/ppermute | solution.py:517
  56.5 16.2 %collective-permute-start.3 = (bf16[784,128]{1,0:T(8,128)(2,1)S(1)}, bf16[784,128]{1,0:T(8,128)(2,1)S(1)}, u32[]{:S(2)}, u32[]{:S(2)}) collective-permute-start(bf16[784,128]{1,0:T(8,128)(2,1)S(1)} %get-tuple-element.34), channel_id=1, source_target_pairs={{0,7},{1,0},{2,1},{3,2},{4,3},{5,4},{6,5},{7,6},{8,15},{9,8},{10,9... | collective-permute-start | bytes 602120 | tf_op jit(solution)/shard_map/ppermute | solution.py:517
  60.2 15.3 %collective-permute-start.4 = (bf16[784,128]{1,0:T(8,128)(2,1)S(1)}, bf16[784,128]{1,0:T(8,128)(2,1)S(1)}, u32[]{:S(2)}, u32[]{:S(2)}) collective-permute-start(bf16[784,128]{1,0:T(8,128)(2,1)S(1)} %get-tuple-element.35), channel_id=1, source_target_pairs={{0,1},{1,2},{2,3},{3,4},{4,5},{5,6},{6,7},{7,0},{8,9},{9,10},{10,1... | collective-permute-start | bytes 602120 | tf_op jit(solution)/shard_map/ppermute | solution.py:517
  62.2 17.2 %collective-permute-start.5 = (bf16[784,128]{1,0:T(8,128)(2,1)S(1)}, bf16[784,128]{1,0:T(8,128)(2,1)S(1)}, u32[]{:S(2)}, u32[]{:S(2)}) collective-permute-start(bf16[784,128]{1,0:T(8,128)(2,1)S(1)} %get-tuple-element.36), channel_id=1, source_target_pairs={{0,6},{1,7},{2,0},{3,1},{4,2},{5,3},{6,4},{7,5},{8,14},{9,15},{10,... | collective-permute-start | bytes 602120 | tf_op jit(solution)/shard_map/ppermute | solution.py:517
  65.3 17.1 %collective-permute-start.6 = (bf16[784,128]{1,0:T(8,128)(2,1)}, bf16[784,128]{1,0:T(8,128)(2,1)S(1)}, u32[]{:S(2)}, u32[]{:S(2)}) collective-permute-start(bf16[784,128]{1,0:T(8,128)(2,1)} %get-tuple-element.40), channel_id=1, source_target_pairs={{0,2},{1,3},{2,4},{3,5},{4,6},{5,7},{6,0},{7,1},{8,10},{9,11},{10,... | collective-permute-start | bytes 602120 | tf_op jit(solution)/shard_map/ppermute | solution.py:517
  68.4 22.0 %collective-permute-start.7 = (bf16[784,128]{1,0:T(8,128)(2,1)}, bf16[784,128]{1,0:T(8,128)(2,1)S(1)}, u32[]{:S(2)}, u32[]{:S(2)}) collective-permute-start(bf16[784,128]{1,0:T(8,128)(2,1)} %get-tuple-element.41), channel_id=1, source_target_pairs={{0,5},{1,6},{2,7},{3,0},{4,1},{5,2},{6,3},{7,4},{8,13},{9,14},{10,... | collective-permute-start | bytes 602120 | tf_op jit(solution)/shard_map/ppermute | solution.py:517
  72.8 17.7 %collective-permute-start.8 = (bf16[784,128]{1,0:T(8,128)(2,1)}, bf16[784,128]{1,0:T(8,128)(2,1)S(1)}, u32[]{:S(2)}, u32[]{:S(2)}) collective-permute-start(bf16[784,128]{1,0:T(8,128)(2,1)} %get-tuple-element.42), channel_id=1, source_target_pairs={{0,3},{1,4},{2,5},{3,6},{4,7},{5,0},{6,1},{7,2},{8,11},{9,12},{10,... | collective-permute-start | bytes 602120 | tf_op jit(solution)/shard_map/ppermute | solution.py:517
  129.9 31.1 %all-to-all-start.2 = ((bf16[8,128,512]{2,1,0:T(8,128)(2,1)}), bf16[8,128,512]{2,1,0:T(8,128)(2,1)S(1)}, u32[]{:S(2)}, u32[]{:S(2)}) async-start(bf16[8,128,512]{2,1,0:T(8,128)(2,1)} %get-tuple-element.45), calls=%async_computation.2 | async-start | bytes 2097152 | tf_op jit(solution)/shard_map/all_to_all | solution.py:483
  162.9 6.3 %collective-permute-start.9 = (bf16[32,16,912]{2,1,0:T(8,128)(2,1)S(1)}, bf16[32,16,912]{2,1,0:T(8,128)(2,1)S(1)}, u32[]{:S(2)}, u32[]{:S(2)}) collective-permute-start(bf16[32,16,912]{2,1,0:T(8,128)(2,1)S(1)} %get-tuple-element.49), channel_id=1, source_target_pairs={{0,8},{8,0},{1,9},{9,1},{2,10},{10,2},{3,11},{11,3},{4,12},{12,4},... | collective-permute-start | bytes 2801672 | tf_op jit(solution)/shard_map/ppermute | solution.py:537

commit v3 on v2

--- a/solution.py
+++ b/solution.py
@@ -416,10 +416,9 @@
     )(pieces, back)
 
 
-def grads_kernel(core_ref, pre_ref, feats_ref, second_ref, keep_ref, give_ref):
+def grads_kernel(core_ref, pre_ref, feats_ref, keep_ref, give_ref):
     rows = 256
     unit = keep_ref.shape[1]
-    lead = second_ref.shape[1]
     mine = core_ref[0] == 0
 
     def block(step, carry):
@@ -428,32 +427,65 @@
             pre_ref[pl.ds(start, rows), :], feats_ref[...], (((1,), (1,)), ((), ())),
             preferred_element_type=F32,
         ).astype(BF)
-        second = second_ref[pl.ds(start, rows), :]
         for n in range(rows // (2 * unit)):
             at = step * (rows // (2 * unit)) + n
-            for part, low, high in ((first, lead, keep_ref.shape[2]), (second, 0, lead)):
-                even = part[2 * n * unit : (2 * n + 1) * unit]
-                odd = part[(2 * n + 1) * unit : (2 * n + 2) * unit]
-                keep_ref[at, :, low:high] = jnp.where(mine, even, odd)
-                give_ref[at, :, low:high] = jnp.where(mine, odd, even)
+            even = first[2 * n * unit : (2 * n + 1) * unit]
+            odd = first[(2 * n + 1) * unit : (2 * n + 2) * unit]
+            keep_ref[at] = jnp.where(mine, even, odd)
+            give_ref[at] = jnp.where(mine, odd, even)
         return carry
 
     lax.fori_loop(0, pre_ref.shape[0] // rows, block, 0)
 
 
-def make_grads(core, pre, feats, second, unit):
-    width = feats.shape[0] + second.shape[1]
+def make_grads(core, pre, feats, unit):
     smem = pl.BlockSpec(memory_space=pltpu.SMEM)
     vmem = pl.BlockSpec(memory_space=pltpu.VMEM)
-    half = jax.ShapeDtypeStruct((pre.shape[0] // (2 * unit), unit, width), BF)
+    half = jax.ShapeDtypeStruct((pre.shape[0] // (2 * unit), unit, feats.shape[0]), BF)
     return pl.pallas_call(
         grads_kernel,
         out_shape=(half, half),
-        in_specs=[smem] + [vmem] * 3,
+        in_specs=[smem, vmem, vmem],
         out_specs=(vmem, vmem),
         compiler_params=pltpu.CompilerParams(vmem_limit_bytes=24 << 20),
         name="grads",
-    )(core, pre, feats, second)
+    )(core, pre, feats)
+
+
+def total_kernel(*refs):
+    *parts, out_ref = refs
+    out_ref[...] = sum(part[...].astype(F32) for part in parts).astype(BF)
+
+
+def make_total(parts):
+    vmem = pl.BlockSpec(memory_space=pltpu.VMEM)
+    return pl.pallas_call(
+        total_kernel,
+        out_shape=jax.ShapeDtypeStruct(parts[0].shape, BF),
+        in_specs=[vmem] * len(parts),
+        out_specs=vmem,
+        compiler_params=pltpu.CompilerParams(vmem_limit_bytes=4 << 20),
+        name="total",
+    )(*parts)
+
+
+def merge_kernel(pieces_ref, second_ref, out_ref):
+    lead = second_ref.shape[2]
+    out_ref[:, :, 0:lead] = second_ref[...]
+    out_ref[:, :, lead:] = jnp.sum(pieces_ref[...].astype(F32), axis=0).astype(BF)
+
+
+def make_merge(pieces, second):
+    vmem = pl.BlockSpec(memory_space=pltpu.VMEM)
+    groups, unit, width = pieces.shape[1:]
+    return pl.pallas_call(
+        merge_kernel,
+        out_shape=jax.ShapeDtypeStruct((groups, unit, width + second.shape[2]), BF),
+        in_specs=[vmem, vmem],
+        out_specs=vmem,
+        compiler_params=pltpu.CompilerParams(vmem_limit_bytes=8 << 20),
+        name="merge",
+    )(pieces, second)
 
 
 def finish_kernel(pieces_ref, first_ref, second_ref):
@@ -531,13 +563,26 @@
     pre_grad = swapped(copies, "tile").reshape(-1, num_props)
     second = lax.dot_general(
         upstream_rows, activated, (((0,), (1,)), ((), ())), preferred_element_type=F32
-    ).astype(BF)
+    )
+    second = second.astype(BF).reshape(nx, nz, nc, unit, -1)
+    second_keep = jnp.where(mine == 0, second[:, :, 0], second[:, :, 1])
+    second_give = jnp.where(mine == 0, second[:, :, 1], second[:, :, 0])
+    second_got = lax.ppermute(second_give, "core", [(0, 1), (1, 0)])
+    second_both = (second_keep.astype(F32) + second_got.astype(F32)).astype(BF)
+    place = lax.axis_index("x")
+    parts = []
+    for k in range(nx):
+        part = lax.dynamic_index_in_dim(second_both, (place + k) % nx, 0, keepdims=False)
+        if k > 0:
+            part = lax.ppermute(part, "x", [(i, (i + k) % nx) for i in range(nx)])
+        parts.append(part)
+    second_total = make_total(parts)
     core_at = mine[None].astype(jnp.int32)
-    keep, give = make_grads(core_at, pre_grad, feats, second, unit)
+    keep, give = make_grads(core_at, pre_grad, feats, unit)
     got = lax.ppermute(give, "core", [(0, 1), (1, 0)])
     both = (keep.astype(F32) + got.astype(F32)).astype(BF).reshape(nx, nz, unit, -1)
-    total = swapped(both, "x").astype(F32).sum(axis=0)
-    first_grad, second_grad = make_finish(swapped(total.astype(BF), "z"), lead)
+    total = make_merge(swapped(both, "x"), second_total)
+    first_grad, second_grad = make_finish(swapped(total, "z"), lead)
     return (first_grad.T, second_grad.T)
 
 

time: 207 us -> 213 us (1.029)
  blocking collectives: 68.8 us -> 51.1 us
  starting transfers between devices: 50.6 us -> 66.5 us
  waiting for transfers between devices: 53.4 us -> 57.6 us
    all_to_all x3 -> x2, blocking collectives: 68.8 us -> 51.1 us  [swapped(): return lax.all_to_all(parts, axis, split_axis=0, concat_axis=0, tiled=True)]
    ppermute x0 -> x4, starting transfers between devices: none -> 13.6 us  [the longest x3 11 us: per_device(): part = lax.ppermute(part, 'x', [(i, (i + k) % nx) for i in range(nx)])]
    all_to_all x2 -> x3, starting transfers between devices: 18.6 us -> 22.5 us  [swapped(): return lax.all_to_all(parts, axis, split_axis=0, concat_axis=0, tiled=True)]
    ppermute x0 -> x4, waiting for transfers between devices: none -> 2.45 us  [the longest x3 1.55 us: per_device(): part = lax.ppermute(part, 'x', [(i, (i + k) % nx) for i in range(nx)])]
    all_to_all x2 -> x3, waiting for transfers between devices: 27 us -> 29.1 us  [swapped(): return lax.all_to_all(parts, axis, split_axis=0, concat_axis=0, tiled=True)]
  transfers between devices with their start and end apart: 12 -> 17, of which waited for: 5 -> 7; matrix products, arithmetic and copies ran while one was open for 1% -> 1% of each run, Pallas kernels for 9% -> 8%
where the time goes in v3:
time: 213 us; the launch traced here: 210 us
  starting transfers between devices  66.5 us (31%)
  waiting for transfers between devices  57.6 us (27%)
  blocking collectives  51.1 us (24%)
  Pallas kernels  27.7 us (13%)
  local copies, waits for them, and re-layouts  2.88 us (1%)
    all_to_all x2, blocking collectives, swapped(): return lax.all_to_all(parts, axis, split_axis=0, concat_axis=0, tiled=True)  51.1 us
    all_to_all x3, waiting for transfers between devices, swapped(): return lax.all_to_all(parts, axis, split_axis=0, concat_axis=0, tiled=True)  29.1 us
    ppermute x7, starting transfers between devices, per_device(): recvs[k] = lax.ppermute(crops[k], 'tile', route)  25.5 us
    all_to_all x3, starting transfers between devices, swapped(): return lax.all_to_all(parts, axis, split_axis=0, concat_axis=0, tiled=True)  22.5 us
    ppermute x1, waiting for transfers between devices, per_device(): coarse_below = lax.ppermute(coarse_top, 'tile', up)  12.4 us
    ppermute x7, waiting for transfers between devices, per_device(): recvs[k] = lax.ppermute(crops[k], 'tile', route)  11.9 us
    ppermute x3, starting transfers between devices, per_device(): part = lax.ppermute(part, 'x', [(i, (i + k) % nx) for i in range(nx)])  11 us
    pallas_call x1, Pallas kernels, make_crops(): early = inner(ints, reals, fine, coarse)  8.14 us
  transfers between devices with their start and end apart: 17, of which 7 were waited for; matrix products, arithmetic and copies ran while one was open for 1% of the time, Pallas kernels for 8%

profile of v3, /device:TPU:1, one launch (start us, length us, event | category | flops | bytes accessed | tf_op | source)
XLA Modules:
  0.0 209.9 jit_solution(15524576445409949838)
XLA Ops:
  3.9 15.0 %all-to-all-start = ((bf16[64,16,912]{2,1,0:T(8,128)(2,1)}), bf16[64,16,912]{2,1,0:T(8,128)(2,1)}, u32[]{:S(2)}, u32[]{:S(2)}) async-start(bf16[64,16,912]{2,1,0:T(8,128)(2,1)} %copies.1), calls=%async_computation | async-start | bytes 4194304 | tf_op jit(solution)/shard_map/all_to_all | solution.py:515
  24.3 8.1 %inner.1.inner_ref = f32[49,128,128]{2,1,0:T(8,128)S(1)} custom-call(s32[16,128]{1,0:T(8,128)S(1)} %get-tuple-element.28.ints_ref, f32[24,128]{1,0:T(8,128)S(1)} %get-tuple-element.29.reals_ref, bf16[42,168,128]{2,1,0:T(8,128)(2,1)S(1)} %bitcast.52, bf16[21,84,128]{2,1,0:T(8,128)(2,1)S(1)} %bitcast.55), custom_call_target="tpu_custom_call" | custom-call | tf_op jit(solution)/shard_map/inner/pallas_call | solution.py:309
  32.5 12.4 %collective-permute-done.1.coarse_below_ref = bf16[14,84,128]{2,1,0:T(8,128)(2,1)} collective-permute-done((bf16[14,84,128]{2,1,0:T(8,128)(2,1)}, bf16[14,84,128]{2,1,0:T(8,128)(2,1)}, u32[]{:S(2)}, u32[]{:S(2)}) %collective-permute-start.1) | collective-permute-done | bytes 301088 | tf_op jit(solution)/shard_map/ppermute | solution.py:529
  44.9 5.1 %edge.1 = (bf16[784,128]{1,0:T(8,128)(2,1)S(1)}, bf16[784,128]{1,0:T(8,128)(2,1)S(1)}, bf16[784,128]{1,0:T(8,128)(2,1)}, bf16[784,128]{1,0:T(8,128)(2,1)S(1)}, b...) custom-call(s32[16,128]{1,0:T(8,128)S(1)} %get-tuple-element.28.ints, ...), custom_call_target="tpu_custom_call" | custom-call | tf_op jit(solution)/shard_map/edge/pallas_call | solution.py:310
  49.9 6.6 %collective-permute-start.2 = (bf16[784,128]{1,0:T(8,128)(2,1)S(1)}, bf16[784,128]{1,0:T(8,128)(2,1)S(1)}, u32[]{:S(2)}, u32[]{:S(2)}) collective-permute-start(bf16[784,128]{1,0:T(8,128)(2,1)S(1)} %get-tuple-element.33), channel_id=1, source_target_pairs={{0,4},{1,5},{2,6},{3,7},{4,0},{5,1},{6,2},{7,3},{8,12},{9,13},{10,... | collective-permute-start | bytes 602120 | tf_op jit(solution)/shard_map/ppermute | solution.py:549
  56.6 3.7 %collective-permute-start.3 = (bf16[784,128]{1,0:T(8,128)(2,1)S(1)}, bf16[784,128]{1,0:T(8,128)(2,1)S(1)}, u32[]{:S(2)}, u32[]{:S(2)}) collective-permute-start(bf16[784,128]{1,0:T(8,128)(2,1)S(1)} %get-tuple-element.34), channel_id=1, source_target_pairs={{0,7},{1,0},{2,1},{3,2},{4,3},{5,4},{6,5},{7,6},{8,15},{9,8},{10,9... | collective-permute-start | bytes 602120 | tf_op jit(solution)/shard_map/ppermute | solution.py:549
  62.2 3.1 %collective-permute-start.5 = (bf16[784,128]{1,0:T(8,128)(2,1)S(1)}, bf16[784,128]{1,0:T(8,128)(2,1)S(1)}, u32[]{:S(2)}, u32[]{:S(2)}) collective-permute-start(bf16[784,128]{1,0:T(8,128)(2,1)S(1)} %get-tuple-element.36), channel_id=1, source_target_pairs={{0,6},{1,7},{2,0},{3,1},{4,2},{5,3},{6,4},{7,5},{8,14},{9,15},{10,... | collective-permute-start | bytes 602120 | tf_op jit(solution)/shard_map/ppermute | solution.py:549
  65.4 3.1 %collective-permute-start.6 = (bf16[784,128]{1,0:T(8,128)(2,1)}, bf16[784,128]{1,0:T(8,128)(2,1)S(1)}, u32[]{:S(2)}, u32[]{:S(2)}) collective-permute-start(bf16[784,128]{1,0:T(8,128)(2,1)} %get-tuple-element.40), channel_id=1, source_target_pairs={{0,2},{1,3},{2,4},{3,5},{4,6},{5,7},{6,0},{7,1},{8,10},{9,11},{10,... | collective-permute-start | bytes 602120 | tf_op jit(solution)/shard_map/ppermute | solution.py:549
  68.5 4.3 %collective-permute-start.7 = (bf16[784,128]{1,0:T(8,128)(2,1)}, bf16[784,128]{1,0:T(8,128)(2,1)S(1)}, u32[]{:S(2)}, u32[]{:S(2)}) collective-permute-start(bf16[784,128]{1,0:T(8,128)(2,1)} %get-tuple-element.41), channel_id=1, source_target_pairs={{0,5},{1,6},{2,7},{3,0},{4,1},{5,2},{6,3},{7,4},{8,13},{9,14},{10,... | collective-permute-start | bytes 602120 | tf_op jit(solution)/shard_map/ppermute | solution.py:549
  72.8 2.8 %collective-permute-start.8 = (bf16[784,128]{1,0:T(8,128)(2,1)S(1)}, bf16[784,128]{1,0:T(8,128)(2,1)S(1)}, u32[]{:S(2)}, u32[]{:S(2)}) collective-permute-start(bf16[784,128]{1,0:T(8,128)(2,1)S(1)} %get-tuple-element.42), channel_id=1, source_target_pairs={{0,3},{1,4},{2,5},{3,6},{4,7},{5,0},{6,1},{7,2},{8,11},{9,12},{10,... | collective-permute-start | bytes 602120 | tf_op jit(solution)/shard_map/ppermute | solution.py:549
  75.6 3.8 %collective-permute-done.5.rest_4_ = bf16[784,128]{1,0:T(8,128)(2,1)S(1)} collective-permute-done((bf16[784,128]{1,0:T(8,128)(2,1)S(1)}, bf16[784,128]{1,0:T(8,128)(2,1)S(1)}, u32[]{:S(2)}, u32[]{:S(2)}) %collective-permute-start.5) | collective-permute-done | bytes 200736 | tf_op jit(solution)/shard_map/ppermute | solution.py:549
  82.5 8.0 %collective-permute-done.7.rest_1_ = bf16[784,128]{1,0:T(8,128)(2,1)S(1)} collective-permute-done((bf16[784,128]{1,0:T(8,128)(2,1)}, bf16[784,128]{1,0:T(8,128)(2,1)S(1)}, u32[]{:S(2)}, u32[]{:S(2)}) %collective-permute-start.7) | collective-permute-done | bytes 200736 | tf_op jit(solution)/shard_map/ppermute | solution.py:549
  90.5 3.4 %hidden.1 = (bf16[784,512]{1,0:T(8,128)(2,1)S(1)}, bf16[1024,512]{1,0:T(8,128)(2,1)S(1)}) custom-call(s32[2]{0:T(128)S(1)} %pad_add_fusion.band_ref, s32[1,512]{1,0:T(1,128)S(1)} %get-tuple-element.27.slot_ref, bf16[1024,912]{1,0:T(8,128)(2,1)} %bitcast.5.weight_ref, bf16[784,512]{1,0:T(8,128)(2,1)S(1)} %gather.1.begun_ref, ...), custom_call_target="tpu_custom_call" | custom-call | tf_op jit(solution)/shard_map/hidden/pallas_call | solution.py:377
  94.0 35.6 %all_to_all.25.pieces_ref = bf16[8,128,512]{2,1,0:T(8,128)(2,1)S(1)} all-to-all(bf16[8,128,512]{2,1,0:T(8,128)(2,1)S(1)} %bitcast.58), channel_id=1, replica_groups=mesh['x'=4,'z'=8,'core'=2,'tile'=8] {'tile'}, dimensions={0} | all-to-all | bytes 2097152 | tf_op jit(solution)/shard_map/all_to_all | solution.py:515
  130.9 3.6 %all-to-all-start.2 = ((bf16[8,128,512]{2,1,0:T(8,128)(2,1)}), bf16[8,128,512]{2,1,0:T(8,128)(2,1)S(1)}, u32[]{:S(2)}, u32[]{:S(2)}) async-start(bf16[8,128,512]{2,1,0:T(8,128)(2,1)} %get-tuple-element.45), calls=%async_computation.2 | async-start | bytes 2097152 | tf_op jit(solution)/shard_map/all_to_all | solution.py:515
  134.5 29.1 %all-to-all-done.2 = bf16[8,128,512]{2,1,0:T(8,128)(2,1)S(1)} async-done(((bf16[8,128,512]{2,1,0:T(8,128)(2,1)}), bf16[8,128,512]{2,1,0:T(8,128)(2,1)S(1)}, u32[]{:S(2)}, u32[]{:S(2)}) %all-to-all-start.2) | async-done | bytes 1048608 | tf_op jit(solution)/shard_map/all_to_all | solution.py:515
  164.7 2.8 %grads.1 = (bf16[32,16,784]{2,1,0:T(8,128)(2,1)S(1)}, bf16[32,16,784]{2,1,0:T(8,128)(2,1)}) custom-call(s32[1]{0:T(128)} %bitcast.core_ref, bf16[1024,512]{1,0:T(8,128)(2,1)S(1)} %bitcast.57, bf16[784,512]{1,0:T(8,128)(2,1)S(1)} %copy-done.4), custom_call_target="tpu_custom_call" | custom-call | tf_op jit(solution)/shard_map/grads/pallas_call | solution.py:445
  167.6 2.4 %collective-permute-start.9 = (bf16[32,16,784]{2,1,0:T(8,128)(2,1)}, bf16[32,16,784]{2,1,0:T(8,128)(2,1)S(1)}, u32[]{:S(2)}, u32[]{:S(2)}) collective-permute-start(bf16[32,16,784]{2,1,0:T(8,128)(2,1)} %get-tuple-element.48), channel_id=1, source_target_pairs={{0,8},{8,0},{1,9},{9,1},{2,10},{10,2},{3,11},{11,3},{4,12},{12,4},... | collective-permute-start | bytes 2408456 | tf_op jit(solution)/shard_map/ppermute | solution.py:582
  173.4 3.9 %all-to-all-start.3 = ((bf16[4,8,16,784]{3,2,1,0:T(8,128)(2,1)}), bf16[4,8,16,784]{3,2,1,0:T(8,128)(2,1)S(1)}, u32[]{:S(2)}, u32[]{:S(2)}) async-start(bf16[4,8,16,784]{3,2,1,0:T(8,128)(2,1)} %bitcast.11), calls=%async_computation.3 | async-start | bytes 1835008 | tf_op jit(solution)/shard_map/all_to_all | solution.py:515
  177.3 2.6 %collective-permute-start.10 = (bf16[4,8,16,128]{3,2,1,0:T(8,128)(2,1)S(1)}, bf16[4,8,16,128]{3,2,1,0:T(8,128)(2,1)S(1)}, u32[]{:S(2)}, u32[]{:S(2)}) collective-permute-start(bf16[4,8,16,128]{3,2,1,0:T(8,128)(2,1)S(1)} %fusion.6), channel_id=1, source_target_pairs={{0,8},{8,0},{1,9},{9,1},{2,10},{10,2},{3,11},{11,3},{4,12},{12,4},... | collective-permute-start | bytes 393224 | tf_op jit(solution)/shard_map/ppermute | solution.py:570
  181.0 3.7 %collective-permute-start.11 = (bf16[8,16,128]{2,1,0:T(8,128)(2,1)S(1)}, bf16[8,16,128]{2,1,0:T(8,128)(2,1)S(1)}, u32[]{:S(2)}, u32[]{:S(2)}) collective-permute-start(bf16[8,16,128]{2,1,0:T(8,128)(2,1)S(1)} %get-tuple-element.54), channel_id=1, source_target_pairs={{0,128},{128,256},{256,384},{384,0},{1,129},{129,257},{257,385},{3... | collective-permute-start | bytes 98312 | tf_op jit(solution)/shard_map/ppermute | solution.py:577
  184.6 4.3 %collective-permute-start.12 = (bf16[8,16,128]{2,1,0:T(8,128)(2,1)S(1)}, bf16[8,16,128]{2,1,0:T(8,128)(2,1)S(1)}, u32[]{:S(2)}, u32[]{:S(2)}) collective-permute-start(bf16[8,16,128]{2,1,0:T(8,128)(2,1)S(1)} %get-tuple-element.53), channel_id=1, source_target_pairs={{0,256},{128,384},{256,0},{384,128},{1,257},{129,385},{257,1},{385... | collective-permute-start | bytes 98312 | tf_op jit(solution)/shard_map/ppermute | solution.py:577
  188.9 3.1 %collective-permute-start.13 = (bf16[8,16,128]{2,1,0:T(8,128)(2,1)S(1)}, bf16[8,16,128]{2,1,0:T(8,128)(2,1)S(1)}, u32[]{:S(2)}, u32[]{:S(2)}) collective-permute-start(bf16[8,16,128]{2,1,0:T(8,128)(2,1)S(1)} %get-tuple-element.52), channel_id=1, source_target_pairs={{0,384},{128,0},{256,128},{384,256},{1,385},{129,1},{257,129},{385... | collective-permute-start | bytes 98312 | tf_op jit(solution)/shard_map/ppermute | solution.py:577
  193.8 15.5 %all_to_all.26.pieces_ref = bf16[8,16,912]{2,1,0:T(8,128)(2,1)S(1)} all-to-all(bf16[8,16,912]{2,1,0:T(8,128)(2,1)S(1)} %merge.1), channel_id=1, replica_groups=mesh['x'=4,'z'=8,'core'=2,'tile'=8] {'z'}, dimensions={0} | all-to-all | bytes 466944 | tf_op jit(solution)/shard_map/all_to_all | solution.py:515
  (50 shorter events, 22.9 us)
Async XLA Ops:
  0.6 80.4 %copy-start = (bf16[1,512,1024]{2,1,0:T(8,128)(2,1)S(1)}, bf16[1,512,1024]{2,1,0:T(8,128)(2,1)}, u32[]{:S(2)}) copy-start(bf16[1,512,1024]{2,1,0:T(8,128)(2,1)} %param.13) | copy-start | bytes 3145732
  3.9 77.2 %all-to-all-start = ((bf16[64,16,912]{2,1,0:T(8,128)(2,1)}), bf16[64,16,912]{2,1,0:T(8,128)(2,1)}, u32[]{:S(2)}, u32[]{:S(2)}) async-start(bf16[64,16,912]{2,1,0:T(8,128)(2,1)} %copies.1), calls=%async_computation | async-start | bytes 4194304 | tf_op jit(solution)/shard_map/all_to_all | solution.py:515
  18.9 5.0 %copy-start.6 = (s32[1,4,512]{2,1,0:T(4,128)S(1)}, s32[1,4,512]{2,1,0:T(4,128)}, u32[]{:S(2)}) copy-start(s32[1,4,512]{2,1,0:T(4,128)} %param.7) | copy-start | bytes 24580
  18.9 5.0 %copy-start.8 = (s32[1,512]{1,0:T(1,128)S(1)}, s32[1,512]{1,0:T(1,128)}, u32[]{:S(2)}) copy-start(s32[1,512]{1,0:T(1,128)} %refs_2_.1) | copy-start | bytes 6148
  18.9 5.4 %copy-start.1 = (bf16[1,42,168,128]{3,2,1,0:T(8,128)(2,1)S(1)}, bf16[1,42,168,128]{3,2,1,0:T(8,128)(2,1)}, u32[]{:S(2)}) copy-start(bf16[1,42,168,128]{3,2,1,0:T(8,128)(2,1)} %param.9) | copy-start | bytes 5419012
  18.9 5.4 %copy-start.2 = (bf16[1,21,84,128]{3,2,1,0:T(8,128)(2,1)S(1)}, bf16[1,21,84,128]{3,2,1,0:T(8,128)(2,1)}, u32[]{:S(2)}) copy-start(bf16[1,21,84,128]{3,2,1,0:T(8,128)(2,1)} %param.10) | copy-start | bytes 1354756
  21.3 23.6 %collective-permute-start = (bf16[14,168,128]{2,1,0:T(8,128)(2,1)}, bf16[14,168,128]{2,1,0:T(8,128)(2,1)}, u32[]{:S(2)}, u32[]{:S(2)}) collective-permute-start(bf16[14,168,128]{2,1,0:T(8,128)(2,1)} %get-tuple-element.30), channel_id=1, source_target_pairs={{1,0},{2,1},{3,2},{4,3},{5,4},{6,5},{7,6},{9,8},{10,9},{11,10},{12... | collective-permute-start | bytes 1806344 | tf_op jit(solution)/shard_map/ppermute | solution.py:528
  22.6 22.3 %collective-permute-start.1 = (bf16[14,84,128]{2,1,0:T(8,128)(2,1)}, bf16[14,84,128]{2,1,0:T(8,128)(2,1)}, u32[]{:S(2)}, u32[]{:S(2)}) collective-permute-start(bf16[14,84,128]{2,1,0:T(8,128)(2,1)} %get-tuple-element.31), channel_id=1, source_target_pairs={{1,0},{2,1},{3,2},{4,3},{5,4},{6,5},{7,6},{9,8},{10,9},{11,10},{12... | collective-permute-start | bytes 903176 | tf_op jit(solution)/shard_map/ppermute | solution.py:529
  49.9 18.5 %collective-permute-start.2 = (bf16[784,128]{1,0:T(8,128)(2,1)S(1)}, bf16[784,128]{1,0:T(8,128)(2,1)S(1)}, u32[]{:S(2)}, u32[]{:S(2)}) collective-permute-start(bf16[784,128]{1,0:T(8,128)(2,1)S(1)} %get-tuple-element.33), channel_id=1, source_target_pairs={{0,4},{1,5},{2,6},{3,7},{4,0},{5,1},{6,2},{7,3},{8,12},{9,13},{10,... | collective-permute-start | bytes 602120 | tf_op jit(solution)/shard_map/ppermute | solution.py:549
  56.6 16.2 %collective-permute-start.3 = (bf16[784,128]{1,0:T(8,128)(2,1)S(1)}, bf16[784,128]{1,0:T(8,128)(2,1)S(1)}, u32[]{:S(2)}, u32[]{:S(2)}) collective-permute-start(bf16[784,128]{1,0:T(8,128)(2,1)S(1)} %get-tuple-element.34), channel_id=1, source_target_pairs={{0,7},{1,0},{2,1},{3,2},{4,3},{5,4},{6,5},{7,6},{8,15},{9,8},{10,9... | collective-permute-start | bytes 602120 | tf_op jit(solution)/shard_map/ppermute | solution.py:549
  60.3 15.3 %collective-permute-start.4 = (bf16[784,128]{1,0:T(8,128)(2,1)S(1)}, bf16[784,128]{1,0:T(8,128)(2,1)S(1)}, u32[]{:S(2)}, u32[]{:S(2)}) collective-permute-start(bf16[784,128]{1,0:T(8,128)(2,1)S(1)} %get-tuple-element.35), channel_id=1, source_target_pairs={{0,1},{1,2},{2,3},{3,4},{4,5},{5,6},{6,7},{7,0},{8,9},{9,10},{10,1... | collective-permute-start | bytes 602120 | tf_op jit(solution)/shard_map/ppermute | solution.py:549
  62.2 17.2 %collective-permute-start.5 = (bf16[784,128]{1,0:T(8,128)(2,1)S(1)}, bf16[784,128]{1,0:T(8,128)(2,1)S(1)}, u32[]{:S(2)}, u32[]{:S(2)}) collective-permute-start(bf16[784,128]{1,0:T(8,128)(2,1)S(1)} %get-tuple-element.36), channel_id=1, source_target_pairs={{0,6},{1,7},{2,0},{3,1},{4,2},{5,3},{6,4},{7,5},{8,14},{9,15},{10,... | collective-permute-start | bytes 602120 | tf_op jit(solution)/shard_map/ppermute | solution.py:549
  65.4 17.1 %collective-permute-start.6 = (bf16[784,128]{1,0:T(8,128)(2,1)}, bf16[784,128]{1,0:T(8,128)(2,1)S(1)}, u32[]{:S(2)}, u32[]{:S(2)}) collective-permute-start(bf16[784,128]{1,0:T(8,128)(2,1)} %get-tuple-element.40), channel_id=1, source_target_pairs={{0,2},{1,3},{2,4},{3,5},{4,6},{5,7},{6,0},{7,1},{8,10},{9,11},{10,... | collective-permute-start | bytes 602120 | tf_op jit(solution)/shard_map/ppermute | solution.py:549
  68.5 22.0 %collective-permute-start.7 = (bf16[784,128]{1,0:T(8,128)(2,1)}, bf16[784,128]{1,0:T(8,128)(2,1)S(1)}, u32[]{:S(2)}, u32[]{:S(2)}) collective-permute-start(bf16[784,128]{1,0:T(8,128)(2,1)} %get-tuple-element.41), channel_id=1, source_target_pairs={{0,5},{1,6},{2,7},{3,0},{4,1},{5,2},{6,3},{7,4},{8,13},{9,14},{10,... | collective-permute-start | bytes 602120 | tf_op jit(solution)/shard_map/ppermute | solution.py:549
  72.8 17.7 %collective-permute-start.8 = (bf16[784,128]{1,0:T(8,128)(2,1)S(1)}, bf16[784,128]{1,0:T(8,128)(2,1)S(1)}, u32[]{:S(2)}, u32[]{:S(2)}) collective-permute-start(bf16[784,128]{1,0:T(8,128)(2,1)S(1)} %get-tuple-element.42), channel_id=1, source_target_pairs={{0,3},{1,4},{2,5},{3,6},{4,7},{5,0},{6,1},{7,2},{8,11},{9,12},{10,... | collective-permute-start | bytes 602120 | tf_op jit(solution)/shard_map/ppermute | solution.py:549
  94.0 37.0 %copy-start.3 = (bf16[784,512]{1,0:T(8,128)(2,1)}, bf16[784,512]{1,0:T(8,128)(2,1)S(1)}, u32[]{:S(2)}) copy-start(bf16[784,512]{1,0:T(8,128)(2,1)S(1)} %get-tuple-element.46.feats_ref) | copy-start | bytes 2408452
  130.9 32.7 %all-to-all-start.2 = ((bf16[8,128,512]{2,1,0:T(8,128)(2,1)}), bf16[8,128,512]{2,1,0:T(8,128)(2,1)S(1)}, u32[]{:S(2)}, u32[]{:S(2)}) async-start(bf16[8,128,512]{2,1,0:T(8,128)(2,1)} %get-tuple-element.45), calls=%async_computation.2 | async-start | bytes 2097152 | tf_op jit(solution)/shard_map/all_to_all | solution.py:515
  163.6 1.1 copy-start.4
  167.6 4.7 %collective-permute-start.9 = (bf16[32,16,784]{2,1,0:T(8,128)(2,1)}, bf16[32,16,784]{2,1,0:T(8,128)(2,1)S(1)}, u32[]{:S(2)}, u32[]{:S(2)}) collective-permute-start(bf16[32,16,784]{2,1,0:T(8,128)(2,1)} %get-tuple-element.48), channel_id=1, source_target_pairs={{0,8},{8,0},{1,9},{9,1},{2,10},{10,2},{3,11},{11,3},{4,12},{12,4},... | collective-permute-start | bytes 2408456 | tf_op jit(solution)/shard_map/ppermute | solution.py:582
  173.4 20.2 %all-to-all-start.3 = ((bf16[4,8,16,784]{3,2,1,0:T(8,128)(2,1)}), bf16[4,8,16,784]{3,2,1,0:T(8,128)(2,1)S(1)}, u32[]{:S(2)}, u32[]{:S(2)}) async-start(bf16[4,8,16,784]{3,2,1,0:T(8,128)(2,1)} %bitcast.11), calls=%async_computation.3 | async-start | bytes 1835008 | tf_op jit(solution)/shard_map/all_to_all | solution.py:515
  177.3 3.5 %collective-permute-start.10 = (bf16[4,8,16,128]{3,2,1,0:T(8,128)(2,1)S(1)}, bf16[4,8,16,128]{3,2,1,0:T(8,128)(2,1)S(1)}, u32[]{:S(2)}, u32[]{:S(2)}) collective-permute-start(bf16[4,8,16,128]{3,2,1,0:T(8,128)(2,1)S(1)} %fusion.6), channel_id=1, source_target_pairs={{0,8},{8,0},{1,9},{9,1},{2,10},{10,2},{3,11},{11,3},{4,12},{12,4},... | collective-permute-start | bytes 393224 | tf_op jit(solution)/shard_map/ppermute | solution.py:570
  181.0 11.1 %collective-permute-start.11 = (bf16[8,16,128]{2,1,0:T(8,128)(2,1)S(1)}, bf16[8,16,128]{2,1,0:T(8,128)(2,1)S(1)}, u32[]{:S(2)}, u32[]{:S(2)}) collective-permute-start(bf16[8,16,128]{2,1,0:T(8,128)(2,1)S(1)} %get-tuple-element.54), channel_id=1, source_target_pairs={{0,128},{128,256},{256,384},{384,0},{1,129},{129,257},{257,385},{3... | collective-permute-start | bytes 98312 | tf_op jit(solution)/shard_map/ppermute | solution.py:577
  184.6 7.4 %collective-permute-start.12 = (bf16[8,16,128]{2,1,0:T(8,128)(2,1)S(1)}, bf16[8,16,128]{2,1,0:T(8,128)(2,1)S(1)}, u32[]{:S(2)}, u32[]{:S(2)}) collective-permute-start(bf16[8,16,128]{2,1,0:T(8,128)(2,1)S(1)} %get-tuple-element.53), channel_id=1, source_target_pairs={{0,256},{128,384},{256,0},{384,128},{1,257},{129,385},{257,1},{385... | collective-permute-start | bytes 98312 | tf_op jit(solution)/shard_map/ppermute | solution.py:577
  188.9 4.7 %collective-permute-start.13 = (bf16[8,16,128]{2,1,0:T(8,128)(2,1)S(1)}, bf16[8,16,128]{2,1,0:T(8,128)(2,1)S(1)}, u32[]{:S(2)}, u32[]{:S(2)}) collective-permute-start(bf16[8,16,128]{2,1,0:T(8,128)(2,1)S(1)} %get-tuple-element.52), channel_id=1, source_target_pairs={{0,384},{128,0},{256,128},{384,256},{1,385},{129,1},{257,129},{385... | collective-permute-start | bytes 98312 | tf_op jit(solution)/shard_map/ppermute | solution.py:577
  (2 other events, 1.5 us)

commit v4 on v3

--- a/solution.py
+++ b/solution.py
@@ -53,17 +53,17 @@
     )(fine, coarse)
 
 
-def copies_kernel(first_ref, second_ref, out_ref):
+def copies_kernel(first_ref, second_ref, out_ref, joined, sent):
     lead = second_ref.shape[1]
-    first = first_ref[...]
-    second = second_ref[...]
-
-    def body(i, carry):
-        out_ref[i, :, 0:lead] = second
-        out_ref[i, :, lead:] = first
-        return carry
-
-    lax.fori_loop(0, out_ref.shape[0], body, 0)
+    joined[:, 0:lead] = second_ref[...]
+    joined[:, lead:] = first_ref[...]
+    moves = [
+        pltpu.make_async_copy(joined, out_ref.at[i], sent.at[i]) for i in range(out_ref.shape[0])
+    ]
+    for move in moves:
+        move.start()
+    for move in moves:
+        move.wait()
 
 
 def make_copies(first, second, count):
@@ -73,7 +73,11 @@
         copies_kernel,
         out_shape=jax.ShapeDtypeStruct((count, first.shape[0], width), BF),
         in_specs=[vmem, vmem],
-        out_specs=vmem,
+        out_specs=pl.BlockSpec(memory_space=pltpu.HBM),
+        scratch_shapes=[
+            pltpu.VMEM((first.shape[0], width), BF),
+            pltpu.SemaphoreType.DMA((count,)),
+        ],
         compiler_params=pltpu.CompilerParams(vmem_limit_bytes=8 << 20),
         name="copies",
     )(first, second)
@@ -180,10 +184,12 @@
     )
     fine_copy.start()
     maps[0:base, fine_cols:pitch, :] = jnp.zeros((base, pitch - fine_cols, channels), BF)
-    maps[base:total, :, :] = jnp.zeros((total - base, pitch, channels), BF)
+    margin = coarse_cols // 16 * 16
+    maps[base:total, margin : margin + SPAN, :] = jnp.zeros((total - base, SPAN, channels), BF)
     maps[base : base + coarse_rows, 0:coarse_cols, :] = coarse_ref[...]
     if below is None:
         maps[fine_rows:base, 0:fine_cols, :] = jnp.zeros((REACH, fine_cols, channels), BF)
+        maps[base + coarse_rows : total, 0:margin, :] = jnp.zeros((REACH, margin, channels), BF)
     else:
         maps[fine_rows:base, 0:fine_cols, :] = below[0][...]
         maps[base + coarse_rows : total, 0:coarse_cols, :] = below[1][...]
@@ -241,10 +247,8 @@
 
 def edge_kernel(ints_ref, reals_ref, fine_ref, coarse_ref, fine_below_ref, coarse_below_ref,
                 inner_ref, band_ref, *rest):
-    *outs, maps, parts, bin_ref, cell_ref, arrived, crops, early, flipped = rest
+    *outs, maps, parts, bin_ref, cell_ref, arrived, crops, flipped = rest
     channels = fine_ref.shape[2]
-    early_copy = pltpu.make_async_copy(inner_ref, early, arrived.at[1])
-    early_copy.start()
     fill_cells(bin_ref, cell_ref)
     fill_maps(maps, fine_ref, coarse_ref, (fine_below_ref, coarse_below_ref), arrived)
     low = ints_ref[9, 0] // GROUP
@@ -255,11 +259,10 @@
         return carry
 
     lax.fori_loop(low, high, body, 0)
-    early_copy.wait()
     at = lax.broadcasted_iota(jnp.int32, (crops.shape[1], channels), 0)
     redone = (at >= low * GROUP) & (at < high * GROUP)
     for m in range(49):
-        block = jnp.where(redone, crops[m], early[m])
+        block = jnp.where(redone, crops[m], inner_ref[m])
         flipped[m * channels : (m + 1) * channels, :] = block.T.astype(BF)
     share = outs[0].shape[0]
     for k, out in enumerate(outs):
@@ -279,7 +282,7 @@
         pltpu.VMEM((GROUP, 56, channels), F32),
         pltpu.VMEM((8, 8 * SPAN), F32),
         pltpu.VMEM((8, 8 * SPAN), F32),
-        pltpu.SemaphoreType.DMA((2,)),
+        pltpu.SemaphoreType.DMA((1,)),
     ]
     every = jax.ShapeDtypeStruct((49, capacity, channels), F32)
     params = pltpu.CompilerParams(vmem_limit_bytes=24 << 20)
@@ -295,11 +298,10 @@
     edge = pl.pallas_call(
         edge_kernel,
         out_shape=[jax.ShapeDtypeStruct((49 * channels // tiles, capacity), BF)] * tiles,
-        in_specs=[smem, smem, away, vmem, vmem, vmem, away, smem],
+        in_specs=[smem, smem, away, vmem, vmem, vmem, vmem, smem],
         out_specs=[vmem] * tiles,
         scratch_shapes=common
         + [
-            pltpu.VMEM(every.shape, F32),
             pltpu.VMEM(every.shape, F32),
             pltpu.VMEM((49 * channels, capacity), BF),
         ],

time: 213 us -> 212 us (level)
  no operation moved by 1% of the time
where the time goes in v4:
time: 212 us; the launch traced here: 210 us
  starting transfers between devices  66.6 us (31%)
  waiting for transfers between devices  57.7 us (27%)
  blocking collectives  51.1 us (24%)
  Pallas kernels  27.3 us (13%)
  local copies, waits for them, and re-layouts  2.88 us (1%)
    all_to_all x2, blocking collectives, swapped(): return lax.all_to_all(parts, axis, split_axis=0, concat_axis=0, tiled=True)  51.1 us
    all_to_all x3, waiting for transfers between devices, swapped(): return lax.all_to_all(parts, axis, split_axis=0, concat_axis=0, tiled=True)  29.1 us
    ppermute x7, starting transfers between devices, per_device(): recvs[k] = lax.ppermute(crops[k], 'tile', route)  25.5 us
    all_to_all x3, starting transfers between devices, swapped(): return lax.all_to_all(parts, axis, split_axis=0, concat_axis=0, tiled=True)  22.5 us
    ppermute x1, waiting for transfers between devices, per_device(): coarse_below = lax.ppermute(coarse_top, 'tile', up)  12.5 us
    ppermute x7, waiting for transfers between devices, per_device(): recvs[k] = lax.ppermute(crops[k], 'tile', route)  11.8 us
    ppermute x3, starting transfers between devices, per_device(): part = lax.ppermute(part, 'x', [(i, (i + k) % nx) for i in range(nx)])  11 us
    pallas_call x1, Pallas kernels, make_crops(): early = inner(ints, reals, fine, coarse)  7.99 us
  transfers between devices with their start and end apart: 17, of which 7 were waited for; matrix products, arithmetic and copies ran while one was open for 1% of the time, Pallas kernels for 8%

profile of v4, /device:TPU:1, one launch (start us, length us, event | category | flops | bytes accessed | tf_op | source)
XLA Modules:
  0.0 209.7 jit_solution(10532298632475253879)
XLA Ops:
  4.1 15.0 %all-to-all-start = ((bf16[64,16,912]{2,1,0:T(8,128)(2,1)}), bf16[64,16,912]{2,1,0:T(8,128)(2,1)}, u32[]{:S(2)}, u32[]{:S(2)}) async-start(bf16[64,16,912]{2,1,0:T(8,128)(2,1)} %copies.1), calls=%async_computation | async-start | bytes 4194304 | tf_op jit(solution)/shard_map/all_to_all | solution.py:517
  24.6 8.0 %inner.1.inner_ref = f32[49,128,128]{2,1,0:T(8,128)S(1)} custom-call(s32[16,128]{1,0:T(8,128)S(1)} %get-tuple-element.28.ints_ref, f32[24,128]{1,0:T(8,128)S(1)} %get-tuple-element.29.reals_ref, bf16[42,168,128]{2,1,0:T(8,128)(2,1)S(1)} %bitcast.52, bf16[21,84,128]{2,1,0:T(8,128)(2,1)S(1)} %bitcast.55), custom_call_target="tpu_custom_call" | custom-call | tf_op jit(solution)/shard_map/inner/pallas_call | solution.py:311
  32.6 12.5 %collective-permute-done.1.coarse_below_ref = bf16[14,84,128]{2,1,0:T(8,128)(2,1)} collective-permute-done((bf16[14,84,128]{2,1,0:T(8,128)(2,1)}, bf16[14,84,128]{2,1,0:T(8,128)(2,1)}, u32[]{:S(2)}, u32[]{:S(2)}) %collective-permute-start.1) | collective-permute-done | bytes 301088 | tf_op jit(solution)/shard_map/ppermute | solution.py:531
  45.1 4.6 %edge.1 = (bf16[784,128]{1,0:T(8,128)(2,1)S(1)}, bf16[784,128]{1,0:T(8,128)(2,1)S(1)}, bf16[784,128]{1,0:T(8,128)(2,1)}, bf16[784,128]{1,0:T(8,128)(2,1)S(1)}, b...) custom-call(s32[16,128]{1,0:T(8,128)S(1)} %get-tuple-element.28.ints, ...), custom_call_target="tpu_custom_call" | custom-call | tf_op jit(solution)/shard_map/edge/pallas_call | solution.py:312
  49.7 6.6 %collective-permute-start.2 = (bf16[784,128]{1,0:T(8,128)(2,1)S(1)}, bf16[784,128]{1,0:T(8,128)(2,1)S(1)}, u32[]{:S(2)}, u32[]{:S(2)}) collective-permute-start(bf16[784,128]{1,0:T(8,128)(2,1)S(1)} %get-tuple-element.33), channel_id=1, source_target_pairs={{0,4},{1,5},{2,6},{3,7},{4,0},{5,1},{6,2},{7,3},{8,12},{9,13},{10,... | collective-permute-start | bytes 602120 | tf_op jit(solution)/shard_map/ppermute | solution.py:551
  56.3 3.7 %collective-permute-start.3 = (bf16[784,128]{1,0:T(8,128)(2,1)S(1)}, bf16[784,128]{1,0:T(8,128)(2,1)S(1)}, u32[]{:S(2)}, u32[]{:S(2)}) collective-permute-start(bf16[784,128]{1,0:T(8,128)(2,1)S(1)} %get-tuple-element.34), channel_id=1, source_target_pairs={{0,7},{1,0},{2,1},{3,2},{4,3},{5,4},{6,5},{7,6},{8,15},{9,8},{10,9... | collective-permute-start | bytes 602120 | tf_op jit(solution)/shard_map/ppermute | solution.py:551
  62.0 3.1 %collective-permute-start.5 = (bf16[784,128]{1,0:T(8,128)(2,1)S(1)}, bf16[784,128]{1,0:T(8,128)(2,1)S(1)}, u32[]{:S(2)}, u32[]{:S(2)}) collective-permute-start(bf16[784,128]{1,0:T(8,128)(2,1)S(1)} %get-tuple-element.36), channel_id=1, source_target_pairs={{0,6},{1,7},{2,0},{3,1},{4,2},{5,3},{6,4},{7,5},{8,14},{9,15},{10,... | collective-permute-start | bytes 602120 | tf_op jit(solution)/shard_map/ppermute | solution.py:551
  65.2 3.1 %collective-permute-start.6 = (bf16[784,128]{1,0:T(8,128)(2,1)}, bf16[784,128]{1,0:T(8,128)(2,1)S(1)}, u32[]{:S(2)}, u32[]{:S(2)}) collective-permute-start(bf16[784,128]{1,0:T(8,128)(2,1)} %get-tuple-element.40), channel_id=1, source_target_pairs={{0,2},{1,3},{2,4},{3,5},{4,6},{5,7},{6,0},{7,1},{8,10},{9,11},{10,... | collective-permute-start | bytes 602120 | tf_op jit(solution)/shard_map/ppermute | solution.py:551
  68.3 4.3 %collective-permute-start.7 = (bf16[784,128]{1,0:T(8,128)(2,1)}, bf16[784,128]{1,0:T(8,128)(2,1)S(1)}, u32[]{:S(2)}, u32[]{:S(2)}) collective-permute-start(bf16[784,128]{1,0:T(8,128)(2,1)} %get-tuple-element.41), channel_id=1, source_target_pairs={{0,5},{1,6},{2,7},{3,0},{4,1},{5,2},{6,3},{7,4},{8,13},{9,14},{10,... | collective-permute-start | bytes 602120 | tf_op jit(solution)/shard_map/ppermute | solution.py:551
  72.6 2.8 %collective-permute-start.8 = (bf16[784,128]{1,0:T(8,128)(2,1)S(1)}, bf16[784,128]{1,0:T(8,128)(2,1)S(1)}, u32[]{:S(2)}, u32[]{:S(2)}) collective-permute-start(bf16[784,128]{1,0:T(8,128)(2,1)S(1)} %get-tuple-element.42), channel_id=1, source_target_pairs={{0,3},{1,4},{2,5},{3,6},{4,7},{5,0},{6,1},{7,2},{8,11},{9,12},{10,... | collective-permute-start | bytes 602120 | tf_op jit(solution)/shard_map/ppermute | solution.py:551
  75.4 3.8 %collective-permute-done.5.rest_4_ = bf16[784,128]{1,0:T(8,128)(2,1)S(1)} collective-permute-done((bf16[784,128]{1,0:T(8,128)(2,1)S(1)}, bf16[784,128]{1,0:T(8,128)(2,1)S(1)}, u32[]{:S(2)}, u32[]{:S(2)}) %collective-permute-start.5) | collective-permute-done | bytes 200736 | tf_op jit(solution)/shard_map/ppermute | solution.py:551
  82.3 8.0 %collective-permute-done.7.rest_1_ = bf16[784,128]{1,0:T(8,128)(2,1)S(1)} collective-permute-done((bf16[784,128]{1,0:T(8,128)(2,1)}, bf16[784,128]{1,0:T(8,128)(2,1)S(1)}, u32[]{:S(2)}, u32[]{:S(2)}) %collective-permute-start.7) | collective-permute-done | bytes 200736 | tf_op jit(solution)/shard_map/ppermute | solution.py:551
  90.3 3.4 %hidden.1 = (bf16[784,512]{1,0:T(8,128)(2,1)S(1)}, bf16[1024,512]{1,0:T(8,128)(2,1)S(1)}) custom-call(s32[2]{0:T(128)S(1)} %pad_add_fusion.band_ref, s32[1,512]{1,0:T(1,128)S(1)} %get-tuple-element.27.slot_ref, bf16[1024,912]{1,0:T(8,128)(2,1)} %bitcast.5.weight_ref, bf16[784,512]{1,0:T(8,128)(2,1)S(1)} %gather.1.begun_ref, ...), custom_call_target="tpu_custom_call" | custom-call | tf_op jit(solution)/shard_map/hidden/pallas_call | solution.py:379
  93.8 35.6 %all_to_all.25.pieces_ref = bf16[8,128,512]{2,1,0:T(8,128)(2,1)S(1)} all-to-all(bf16[8,128,512]{2,1,0:T(8,128)(2,1)S(1)} %bitcast.58), channel_id=1, replica_groups=mesh['x'=4,'z'=8,'core'=2,'tile'=8] {'tile'}, dimensions={0} | all-to-all | bytes 2097152 | tf_op jit(solution)/shard_map/all_to_all | solution.py:517
  130.7 3.6 %all-to-all-start.2 = ((bf16[8,128,512]{2,1,0:T(8,128)(2,1)}), bf16[8,128,512]{2,1,0:T(8,128)(2,1)S(1)}, u32[]{:S(2)}, u32[]{:S(2)}) async-start(bf16[8,128,512]{2,1,0:T(8,128)(2,1)} %get-tuple-element.45), calls=%async_computation.2 | async-start | bytes 2097152 | tf_op jit(solution)/shard_map/all_to_all | solution.py:517
  134.3 29.1 %all-to-all-done.2 = bf16[8,128,512]{2,1,0:T(8,128)(2,1)S(1)} async-done(((bf16[8,128,512]{2,1,0:T(8,128)(2,1)}), bf16[8,128,512]{2,1,0:T(8,128)(2,1)S(1)}, u32[]{:S(2)}, u32[]{:S(2)}) %all-to-all-start.2) | async-done | bytes 1048608 | tf_op jit(solution)/shard_map/all_to_all | solution.py:517
  164.5 2.8 %grads.1 = (bf16[32,16,784]{2,1,0:T(8,128)(2,1)S(1)}, bf16[32,16,784]{2,1,0:T(8,128)(2,1)}) custom-call(s32[1]{0:T(128)} %bitcast.core_ref, bf16[1024,512]{1,0:T(8,128)(2,1)S(1)} %bitcast.57, bf16[784,512]{1,0:T(8,128)(2,1)S(1)} %copy-done.4), custom_call_target="tpu_custom_call" | custom-call | tf_op jit(solution)/shard_map/grads/pallas_call | solution.py:447
  167.4 2.4 %collective-permute-start.9 = (bf16[32,16,784]{2,1,0:T(8,128)(2,1)}, bf16[32,16,784]{2,1,0:T(8,128)(2,1)S(1)}, u32[]{:S(2)}, u32[]{:S(2)}) collective-permute-start(bf16[32,16,784]{2,1,0:T(8,128)(2,1)} %get-tuple-element.48), channel_id=1, source_target_pairs={{0,8},{8,0},{1,9},{9,1},{2,10},{10,2},{3,11},{11,3},{4,12},{12,4},... | collective-permute-start | bytes 2408456 | tf_op jit(solution)/shard_map/ppermute | solution.py:584
  173.2 3.9 %all-to-all-start.3 = ((bf16[4,8,16,784]{3,2,1,0:T(8,128)(2,1)}), bf16[4,8,16,784]{3,2,1,0:T(8,128)(2,1)S(1)}, u32[]{:S(2)}, u32[]{:S(2)}) async-start(bf16[4,8,16,784]{3,2,1,0:T(8,128)(2,1)} %bitcast.11), calls=%async_computation.3 | async-start | bytes 1835008 | tf_op jit(solution)/shard_map/all_to_all | solution.py:517
  177.1 2.6 %collective-permute-start.10 = (bf16[4,8,16,128]{3,2,1,0:T(8,128)(2,1)S(1)}, bf16[4,8,16,128]{3,2,1,0:T(8,128)(2,1)S(1)}, u32[]{:S(2)}, u32[]{:S(2)}) collective-permute-start(bf16[4,8,16,128]{3,2,1,0:T(8,128)(2,1)S(1)} %fusion.6), channel_id=1, source_target_pairs={{0,8},{8,0},{1,9},{9,1},{2,10},{10,2},{3,11},{11,3},{4,12},{12,4},... | collective-permute-start | bytes 393224 | tf_op jit(solution)/shard_map/ppermute | solution.py:572
  180.8 3.7 %collective-permute-start.11 = (bf16[8,16,128]{2,1,0:T(8,128)(2,1)S(1)}, bf16[8,16,128]{2,1,0:T(8,128)(2,1)S(1)}, u32[]{:S(2)}, u32[]{:S(2)}) collective-permute-start(bf16[8,16,128]{2,1,0:T(8,128)(2,1)S(1)} %get-tuple-element.54), channel_id=1, source_target_pairs={{0,128},{128,256},{256,384},{384,0},{1,129},{129,257},{257,385},{3... | collective-permute-start | bytes 98312 | tf_op jit(solution)/shard_map/ppermute | solution.py:579
  184.4 4.3 %collective-permute-start.12 = (bf16[8,16,128]{2,1,0:T(8,128)(2,1)S(1)}, bf16[8,16,128]{2,1,0:T(8,128)(2,1)S(1)}, u32[]{:S(2)}, u32[]{:S(2)}) collective-permute-start(bf16[8,16,128]{2,1,0:T(8,128)(2,1)S(1)} %get-tuple-element.53), channel_id=1, source_target_pairs={{0,256},{128,384},{256,0},{384,128},{1,257},{129,385},{257,1},{385... | collective-permute-start | bytes 98312 | tf_op jit(solution)/shard_map/ppermute | solution.py:579
  188.7 3.1 %collective-permute-start.13 = (bf16[8,16,128]{2,1,0:T(8,128)(2,1)S(1)}, bf16[8,16,128]{2,1,0:T(8,128)(2,1)S(1)}, u32[]{:S(2)}, u32[]{:S(2)}) collective-permute-start(bf16[8,16,128]{2,1,0:T(8,128)(2,1)S(1)} %get-tuple-element.52), channel_id=1, source_target_pairs={{0,384},{128,0},{256,128},{384,256},{1,385},{129,1},{257,129},{385... | collective-permute-start | bytes 98312 | tf_op jit(solution)/shard_map/ppermute | solution.py:579
  193.6 15.5 %all_to_all.26.pieces_ref = bf16[8,16,912]{2,1,0:T(8,128)(2,1)S(1)} all-to-all(bf16[8,16,912]{2,1,0:T(8,128)(2,1)S(1)} %merge.1), channel_id=1, replica_groups=mesh['x'=4,'z'=8,'core'=2,'tile'=8] {'z'}, dimensions={0} | all-to-all | bytes 466944 | tf_op jit(solution)/shard_map/all_to_all | solution.py:517
  (50 shorter events, 23.1 us)
Async XLA Ops:
  0.6 80.2 %copy-start = (bf16[1,512,1024]{2,1,0:T(8,128)(2,1)S(1)}, bf16[1,512,1024]{2,1,0:T(8,128)(2,1)}, u32[]{:S(2)}) copy-start(bf16[1,512,1024]{2,1,0:T(8,128)(2,1)} %param.13) | copy-start | bytes 3145732
  4.1 76.7 %all-to-all-start = ((bf16[64,16,912]{2,1,0:T(8,128)(2,1)}), bf16[64,16,912]{2,1,0:T(8,128)(2,1)}, u32[]{:S(2)}, u32[]{:S(2)}) async-start(bf16[64,16,912]{2,1,0:T(8,128)(2,1)} %copies.1), calls=%async_computation | async-start | bytes 4194304 | tf_op jit(solution)/shard_map/all_to_all | solution.py:517
  19.1 5.0 %copy-start.6 = (s32[1,4,512]{2,1,0:T(4,128)S(1)}, s32[1,4,512]{2,1,0:T(4,128)}, u32[]{:S(2)}) copy-start(s32[1,4,512]{2,1,0:T(4,128)} %param.7) | copy-start | bytes 24580
  19.1 5.0 %copy-start.8 = (s32[1,512]{1,0:T(1,128)S(1)}, s32[1,512]{1,0:T(1,128)}, u32[]{:S(2)}) copy-start(s32[1,512]{1,0:T(1,128)} %refs_2_.1) | copy-start | bytes 6148
  19.1 5.4 %copy-start.1 = (bf16[1,42,168,128]{3,2,1,0:T(8,128)(2,1)S(1)}, bf16[1,42,168,128]{3,2,1,0:T(8,128)(2,1)}, u32[]{:S(2)}) copy-start(bf16[1,42,168,128]{3,2,1,0:T(8,128)(2,1)} %param.9) | copy-start | bytes 5419012
  19.1 5.4 %copy-start.2 = (bf16[1,21,84,128]{3,2,1,0:T(8,128)(2,1)S(1)}, bf16[1,21,84,128]{3,2,1,0:T(8,128)(2,1)}, u32[]{:S(2)}) copy-start(bf16[1,21,84,128]{3,2,1,0:T(8,128)(2,1)} %param.10) | copy-start | bytes 1354756
  21.5 23.6 %collective-permute-start = (bf16[14,168,128]{2,1,0:T(8,128)(2,1)}, bf16[14,168,128]{2,1,0:T(8,128)(2,1)}, u32[]{:S(2)}, u32[]{:S(2)}) collective-permute-start(bf16[14,168,128]{2,1,0:T(8,128)(2,1)} %get-tuple-element.30), channel_id=1, source_target_pairs={{1,0},{2,1},{3,2},{4,3},{5,4},{6,5},{7,6},{9,8},{10,9},{11,10},{12... | collective-permute-start | bytes 1806344 | tf_op jit(solution)/shard_map/ppermute | solution.py:530
  22.8 22.3 %collective-permute-start.1 = (bf16[14,84,128]{2,1,0:T(8,128)(2,1)}, bf16[14,84,128]{2,1,0:T(8,128)(2,1)}, u32[]{:S(2)}, u32[]{:S(2)}) collective-permute-start(bf16[14,84,128]{2,1,0:T(8,128)(2,1)} %get-tuple-element.31), channel_id=1, source_target_pairs={{1,0},{2,1},{3,2},{4,3},{5,4},{6,5},{7,6},{9,8},{10,9},{11,10},{12... | collective-permute-start | bytes 903176 | tf_op jit(solution)/shard_map/ppermute | solution.py:531
  49.7 18.5 %collective-permute-start.2 = (bf16[784,128]{1,0:T(8,128)(2,1)S(1)}, bf16[784,128]{1,0:T(8,128)(2,1)S(1)}, u32[]{:S(2)}, u32[]{:S(2)}) collective-permute-start(bf16[784,128]{1,0:T(8,128)(2,1)S(1)} %get-tuple-element.33), channel_id=1, source_target_pairs={{0,4},{1,5},{2,6},{3,7},{4,0},{5,1},{6,2},{7,3},{8,12},{9,13},{10,... | collective-permute-start | bytes 602120 | tf_op jit(solution)/shard_map/ppermute | solution.py:551
  56.3 16.2 %collective-permute-start.3 = (bf16[784,128]{1,0:T(8,128)(2,1)S(1)}, bf16[784,128]{1,0:T(8,128)(2,1)S(1)}, u32[]{:S(2)}, u32[]{:S(2)}) collective-permute-start(bf16[784,128]{1,0:T(8,128)(2,1)S(1)} %get-tuple-element.34), channel_id=1, source_target_pairs={{0,7},{1,0},{2,1},{3,2},{4,3},{5,4},{6,5},{7,6},{8,15},{9,8},{10,9... | collective-permute-start | bytes 602120 | tf_op jit(solution)/shard_map/ppermute | solution.py:551
  60.1 15.3 %collective-permute-start.4 = (bf16[784,128]{1,0:T(8,128)(2,1)S(1)}, bf16[784,128]{1,0:T(8,128)(2,1)S(1)}, u32[]{:S(2)}, u32[]{:S(2)}) collective-permute-start(bf16[784,128]{1,0:T(8,128)(2,1)S(1)} %get-tuple-element.35), channel_id=1, source_target_pairs={{0,1},{1,2},{2,3},{3,4},{4,5},{5,6},{6,7},{7,0},{8,9},{9,10},{10,1... | collective-permute-start | bytes 602120 | tf_op jit(solution)/shard_map/ppermute | solution.py:551
  62.0 17.2 %collective-permute-start.5 = (bf16[784,128]{1,0:T(8,128)(2,1)S(1)}, bf16[784,128]{1,0:T(8,128)(2,1)S(1)}, u32[]{:S(2)}, u32[]{:S(2)}) collective-permute-start(bf16[784,128]{1,0:T(8,128)(2,1)S(1)} %get-tuple-element.36), channel_id=1, source_target_pairs={{0,6},{1,7},{2,0},{3,1},{4,2},{5,3},{6,4},{7,5},{8,14},{9,15},{10,... | collective-permute-start | bytes 602120 | tf_op jit(solution)/shard_map/ppermute | solution.py:551
  65.2 17.1 %collective-permute-start.6 = (bf16[784,128]{1,0:T(8,128)(2,1)}, bf16[784,128]{1,0:T(8,128)(2,1)S(1)}, u32[]{:S(2)}, u32[]{:S(2)}) collective-permute-start(bf16[784,128]{1,0:T(8,128)(2,1)} %get-tuple-element.40), channel_id=1, source_target_pairs={{0,2},{1,3},{2,4},{3,5},{4,6},{5,7},{6,0},{7,1},{8,10},{9,11},{10,... | collective-permute-start | bytes 602120 | tf_op jit(solution)/shard_map/ppermute | solution.py:551
  68.3 22.0 %collective-permute-start.7 = (bf16[784,128]{1,0:T(8,128)(2,1)}, bf16[784,128]{1,0:T(8,128)(2,1)S(1)}, u32[]{:S(2)}, u32[]{:S(2)}) collective-permute-start(bf16[784,128]{1,0:T(8,128)(2,1)} %get-tuple-element.41), channel_id=1, source_target_pairs={{0,5},{1,6},{2,7},{3,0},{4,1},{5,2},{6,3},{7,4},{8,13},{9,14},{10,... | collective-permute-start | bytes 602120 | tf_op jit(solution)/shard_map/ppermute | solution.py:551
  72.6 17.7 %collective-permute-start.8 = (bf16[784,128]{1,0:T(8,128)(2,1)S(1)}, bf16[784,128]{1,0:T(8,128)(2,1)S(1)}, u32[]{:S(2)}, u32[]{:S(2)}) collective-permute-start(bf16[784,128]{1,0:T(8,128)(2,1)S(1)} %get-tuple-element.42), channel_id=1, source_target_pairs={{0,3},{1,4},{2,5},{3,6},{4,7},{5,0},{6,1},{7,2},{8,11},{9,12},{10,... | collective-permute-start | bytes 602120 | tf_op jit(solution)/shard_map/ppermute | solution.py:551
  93.7 37.0 %copy-start.3 = (bf16[784,512]{1,0:T(8,128)(2,1)}, bf16[784,512]{1,0:T(8,128)(2,1)S(1)}, u32[]{:S(2)}) copy-start(bf16[784,512]{1,0:T(8,128)(2,1)S(1)} %get-tuple-element.46.feats_ref) | copy-start | bytes 2408452
  130.7 32.7 %all-to-all-start.2 = ((bf16[8,128,512]{2,1,0:T(8,128)(2,1)}), bf16[8,128,512]{2,1,0:T(8,128)(2,1)S(1)}, u32[]{:S(2)}, u32[]{:S(2)}) async-start(bf16[8,128,512]{2,1,0:T(8,128)(2,1)} %get-tuple-element.45), calls=%async_computation.2 | async-start | bytes 2097152 | tf_op jit(solution)/shard_map/all_to_all | solution.py:517
  163.4 1.1 copy-start.4
  167.4 4.7 %collective-permute-start.9 = (bf16[32,16,784]{2,1,0:T(8,128)(2,1)}, bf16[32,16,784]{2,1,0:T(8,128)(2,1)S(1)}, u32[]{:S(2)}, u32[]{:S(2)}) collective-permute-start(bf16[32,16,784]{2,1,0:T(8,128)(2,1)} %get-tuple-element.48), channel_id=1, source_target_pairs={{0,8},{8,0},{1,9},{9,1},{2,10},{10,2},{3,11},{11,3},{4,12},{12,4},... | collective-permute-start | bytes 2408456 | tf_op jit(solution)/shard_map/ppermute | solution.py:584
  173.2 20.2 %all-to-all-start.3 = ((bf16[4,8,16,784]{3,2,1,0:T(8,128)(2,1)}), bf16[4,8,16,784]{3,2,1,0:T(8,128)(2,1)S(1)}, u32[]{:S(2)}, u32[]{:S(2)}) async-start(bf16[4,8,16,784]{3,2,1,0:T(8,128)(2,1)} %bitcast.11), calls=%async_computation.3 | async-start | bytes 1835008 | tf_op jit(solution)/shard_map/all_to_all | solution.py:517
  177.1 3.5 %collective-permute-start.10 = (bf16[4,8,16,128]{3,2,1,0:T(8,128)(2,1)S(1)}, bf16[4,8,16,128]{3,2,1,0:T(8,128)(2,1)S(1)}, u32[]{:S(2)}, u32[]{:S(2)}) collective-permute-start(bf16[4,8,16,128]{3,2,1,0:T(8,128)(2,1)S(1)} %fusion.6), channel_id=1, source_target_pairs={{0,8},{8,0},{1,9},{9,1},{2,10},{10,2},{3,11},{11,3},{4,12},{12,4},... | collective-permute-start | bytes 393224 | tf_op jit(solution)/shard_map/ppermute | solution.py:572
  180.8 11.1 %collective-permute-start.11 = (bf16[8,16,128]{2,1,0:T(8,128)(2,1)S(1)}, bf16[8,16,128]{2,1,0:T(8,128)(2,1)S(1)}, u32[]{:S(2)}, u32[]{:S(2)}) collective-permute-start(bf16[8,16,128]{2,1,0:T(8,128)(2,1)S(1)} %get-tuple-element.54), channel_id=1, source_target_pairs={{0,128},{128,256},{256,384},{384,0},{1,129},{129,257},{257,385},{3... | collective-permute-start | bytes 98312 | tf_op jit(solution)/shard_map/ppermute | solution.py:579
  184.4 7.4 %collective-permute-start.12 = (bf16[8,16,128]{2,1,0:T(8,128)(2,1)S(1)}, bf16[8,16,128]{2,1,0:T(8,128)(2,1)S(1)}, u32[]{:S(2)}, u32[]{:S(2)}) collective-permute-start(bf16[8,16,128]{2,1,0:T(8,128)(2,1)S(1)} %get-tuple-element.53), channel_id=1, source_target_pairs={{0,256},{128,384},{256,0},{384,128},{1,257},{129,385},{257,1},{385... | collective-permute-start | bytes 98312 | tf_op jit(solution)/shard_map/ppermute | solution.py:579
  188.7 4.7 %collective-permute-start.13 = (bf16[8,16,128]{2,1,0:T(8,128)(2,1)S(1)}, bf16[8,16,128]{2,1,0:T(8,128)(2,1)S(1)}, u32[]{:S(2)}, u32[]{:S(2)}) collective-permute-start(bf16[8,16,128]{2,1,0:T(8,128)(2,1)S(1)} %get-tuple-element.52), channel_id=1, source_target_pairs={{0,384},{128,0},{256,128},{384,256},{1,385},{129,1},{257,129},{385... | collective-permute-start | bytes 98312 | tf_op jit(solution)/shard_map/ppermute | solution.py:579
  (2 other events, 1.5 us)

commit v5 on v3

--- a/solution.py
+++ b/solution.py
@@ -74,7 +74,7 @@
         out_shape=jax.ShapeDtypeStruct((count, first.shape[0], width), BF),
         in_specs=[vmem, vmem],
         out_specs=vmem,
-        compiler_params=pltpu.CompilerParams(vmem_limit_bytes=8 << 20),
+        compiler_params=pltpu.CompilerParams(vmem_limit_bytes=60 << 20),
         name="copies",
     )(first, second)
 
@@ -180,10 +180,12 @@
     )
     fine_copy.start()
     maps[0:base, fine_cols:pitch, :] = jnp.zeros((base, pitch - fine_cols, channels), BF)
-    maps[base:total, :, :] = jnp.zeros((total - base, pitch, channels), BF)
+    margin = coarse_cols // 16 * 16
+    maps[base:total, margin : margin + SPAN, :] = jnp.zeros((total - base, SPAN, channels), BF)
     maps[base : base + coarse_rows, 0:coarse_cols, :] = coarse_ref[...]
     if below is None:
         maps[fine_rows:base, 0:fine_cols, :] = jnp.zeros((REACH, fine_cols, channels), BF)
+        maps[base + coarse_rows : total, 0:margin, :] = jnp.zeros((REACH, margin, channels), BF)
     else:
         maps[fine_rows:base, 0:fine_cols, :] = below[0][...]
         maps[base + coarse_rows : total, 0:coarse_cols, :] = below[1][...]
@@ -241,10 +243,8 @@
 
 def edge_kernel(ints_ref, reals_ref, fine_ref, coarse_ref, fine_below_ref, coarse_below_ref,
                 inner_ref, band_ref, *rest):
-    *outs, maps, parts, bin_ref, cell_ref, arrived, crops, early, flipped = rest
+    *outs, maps, parts, bin_ref, cell_ref, arrived, crops, flipped = rest
     channels = fine_ref.shape[2]
-    early_copy = pltpu.make_async_copy(inner_ref, early, arrived.at[1])
-    early_copy.start()
     fill_cells(bin_ref, cell_ref)
     fill_maps(maps, fine_ref, coarse_ref, (fine_below_ref, coarse_below_ref), arrived)
     low = ints_ref[9, 0] // GROUP
@@ -255,11 +255,10 @@
         return carry
 
     lax.fori_loop(low, high, body, 0)
-    early_copy.wait()
     at = lax.broadcasted_iota(jnp.int32, (crops.shape[1], channels), 0)
     redone = (at >= low * GROUP) & (at < high * GROUP)
     for m in range(49):
-        block = jnp.where(redone, crops[m], early[m])
+        block = jnp.where(redone, crops[m], inner_ref[m])
         flipped[m * channels : (m + 1) * channels, :] = block.T.astype(BF)
     share = outs[0].shape[0]
     for k, out in enumerate(outs):
@@ -279,7 +278,7 @@
         pltpu.VMEM((GROUP, 56, channels), F32),
         pltpu.VMEM((8, 8 * SPAN), F32),
         pltpu.VMEM((8, 8 * SPAN), F32),
-        pltpu.SemaphoreType.DMA((2,)),
+        pltpu.SemaphoreType.DMA((1,)),
     ]
     every = jax.ShapeDtypeStruct((49, capacity, channels), F32)
     params = pltpu.CompilerParams(vmem_limit_bytes=24 << 20)
@@ -295,11 +294,10 @@
     edge = pl.pallas_call(
         edge_kernel,
         out_shape=[jax.ShapeDtypeStruct((49 * channels // tiles, capacity), BF)] * tiles,
-        in_specs=[smem, smem, away, vmem, vmem, vmem, away, smem],
+        in_specs=[smem, smem, away, vmem, vmem, vmem, vmem, smem],
         out_specs=[vmem] * tiles,
         scratch_shapes=common
         + [
-            pltpu.VMEM(every.shape, F32),
             pltpu.VMEM(every.shape, F32),
             pltpu.VMEM((49 * channels, capacity), BF),
         ],

time: 213 us -> 211 us (level)
  no operation moved by 1% of the time
where the time goes in v5:
time: 211 us; the launch traced here: 209 us
  starting transfers between devices  66.5 us (32%)
  waiting for transfers between devices  57.7 us (27%)
  blocking collectives  51.1 us (24%)
  Pallas kernels  27.9 us (13%)
    all_to_all x2, blocking collectives, swapped(): return lax.all_to_all(parts, axis, split_axis=0, concat_axis=0, tiled=True)  51.1 us
    all_to_all x3, waiting for transfers between devices, swapped(): return lax.all_to_all(parts, axis, split_axis=0, concat_axis=0, tiled=True)  29.1 us
    ppermute x7, starting transfers between devices, per_device(): recvs[k] = lax.ppermute(crops[k], 'tile', route)  25.5 us
    all_to_all x3, starting transfers between devices, swapped(): return lax.all_to_all(parts, axis, split_axis=0, concat_axis=0, tiled=True)  22.5 us
    ppermute x1, waiting for transfers between devices, per_device(): coarse_below = lax.ppermute(coarse_top, 'tile', up)  12.5 us
    ppermute x7, waiting for transfers between devices, per_device(): recvs[k] = lax.ppermute(crops[k], 'tile', route)  11.9 us
    ppermute x3, starting transfers between devices, per_device(): part = lax.ppermute(part, 'x', [(i, (i + k) % nx) for i in range(nx)])  11 us
    pallas_call x1, Pallas kernels, make_crops(): early = inner(ints, reals, fine, coarse)  7.99 us
  transfers between devices with their start and end apart: 17, of which 7 were waited for; matrix products, arithmetic and copies ran while one was open for 1% of the time, Pallas kernels for 8%

profile of v5, /device:TPU:1, one launch (start us, length us, event | category | flops | bytes accessed | tf_op | source)
XLA Modules:
  0.0 208.7 jit_solution(3075120958193462418)
XLA Ops:
  0.6 2.5 %copies.1 = bf16[64,16,912]{2,1,0:T(8,128)(2,1)} custom-call(bf16[16,784]{1,0:T(8,128)(2,1)} %bitcast.62, bf16[16,128]{1,0:T(8,128)(2,1)} %bitcast.63), custom_call_target="tpu_custom_call" | custom-call | tf_op jit(solution)/shard_map/copies/pallas_call | solution.py:72
  3.2 15.0 %all-to-all-start = ((bf16[64,16,912]{2,1,0:T(8,128)(2,1)}), bf16[64,16,912]{2,1,0:T(8,128)(2,1)}, u32[]{:S(2)}, u32[]{:S(2)}) async-start(bf16[64,16,912]{2,1,0:T(8,128)(2,1)} %copies.1), calls=%async_computation | async-start | bytes 4194304 | tf_op jit(solution)/shard_map/all_to_all | solution.py:513
  23.6 8.0 %inner.1.inner_ref = f32[49,128,128]{2,1,0:T(8,128)S(1)} custom-call(s32[16,128]{1,0:T(8,128)S(1)} %get-tuple-element.28.ints_ref, f32[24,128]{1,0:T(8,128)S(1)} %get-tuple-element.29.reals_ref, bf16[42,168,128]{2,1,0:T(8,128)(2,1)S(1)} %bitcast.52, bf16[21,84,128]{2,1,0:T(8,128)(2,1)S(1)} %bitcast.55), custom_call_target="tpu_custom_call" | custom-call | tf_op jit(solution)/shard_map/inner/pallas_call | solution.py:307
  31.6 12.5 %collective-permute-done.1.coarse_below_ref = bf16[14,84,128]{2,1,0:T(8,128)(2,1)} collective-permute-done((bf16[14,84,128]{2,1,0:T(8,128)(2,1)}, bf16[14,84,128]{2,1,0:T(8,128)(2,1)}, u32[]{:S(2)}, u32[]{:S(2)}) %collective-permute-start.1) | collective-permute-done | bytes 301088 | tf_op jit(solution)/shard_map/ppermute | solution.py:527
  44.1 4.6 %edge.1 = (bf16[784,128]{1,0:T(8,128)(2,1)S(1)}, bf16[784,128]{1,0:T(8,128)(2,1)S(1)}, bf16[784,128]{1,0:T(8,128)(2,1)}, bf16[784,128]{1,0:T(8,128)(2,1)S(1)}, b...) custom-call(s32[16,128]{1,0:T(8,128)S(1)} %get-tuple-element.28.ints, ...), custom_call_target="tpu_custom_call" | custom-call | tf_op jit(solution)/shard_map/edge/pallas_call | solution.py:308
  48.8 6.6 %collective-permute-start.2 = (bf16[784,128]{1,0:T(8,128)(2,1)S(1)}, bf16[784,128]{1,0:T(8,128)(2,1)S(1)}, u32[]{:S(2)}, u32[]{:S(2)}) collective-permute-start(bf16[784,128]{1,0:T(8,128)(2,1)S(1)} %get-tuple-element.33), channel_id=1, source_target_pairs={{0,4},{1,5},{2,6},{3,7},{4,0},{5,1},{6,2},{7,3},{8,12},{9,13},{10,... | collective-permute-start | bytes 602120 | tf_op jit(solution)/shard_map/ppermute | solution.py:547
  55.4 3.7 %collective-permute-start.3 = (bf16[784,128]{1,0:T(8,128)(2,1)S(1)}, bf16[784,128]{1,0:T(8,128)(2,1)S(1)}, u32[]{:S(2)}, u32[]{:S(2)}) collective-permute-start(bf16[784,128]{1,0:T(8,128)(2,1)S(1)} %get-tuple-element.34), channel_id=1, source_target_pairs={{0,7},{1,0},{2,1},{3,2},{4,3},{5,4},{6,5},{7,6},{8,15},{9,8},{10,9... | collective-permute-start | bytes 602120 | tf_op jit(solution)/shard_map/ppermute | solution.py:547
  61.0 3.1 %collective-permute-start.5 = (bf16[784,128]{1,0:T(8,128)(2,1)S(1)}, bf16[784,128]{1,0:T(8,128)(2,1)S(1)}, u32[]{:S(2)}, u32[]{:S(2)}) collective-permute-start(bf16[784,128]{1,0:T(8,128)(2,1)S(1)} %get-tuple-element.36), channel_id=1, source_target_pairs={{0,6},{1,7},{2,0},{3,1},{4,2},{5,3},{6,4},{7,5},{8,14},{9,15},{10,... | collective-permute-start | bytes 602120 | tf_op jit(solution)/shard_map/ppermute | solution.py:547
  64.2 3.1 %collective-permute-start.6 = (bf16[784,128]{1,0:T(8,128)(2,1)}, bf16[784,128]{1,0:T(8,128)(2,1)S(1)}, u32[]{:S(2)}, u32[]{:S(2)}) collective-permute-start(bf16[784,128]{1,0:T(8,128)(2,1)} %get-tuple-element.40), channel_id=1, source_target_pairs={{0,2},{1,3},{2,4},{3,5},{4,6},{5,7},{6,0},{7,1},{8,10},{9,11},{10,... | collective-permute-start | bytes 602120 | tf_op jit(solution)/shard_map/ppermute | solution.py:547
  67.3 4.3 %collective-permute-start.7 = (bf16[784,128]{1,0:T(8,128)(2,1)}, bf16[784,128]{1,0:T(8,128)(2,1)S(1)}, u32[]{:S(2)}, u32[]{:S(2)}) collective-permute-start(bf16[784,128]{1,0:T(8,128)(2,1)} %get-tuple-element.41), channel_id=1, source_target_pairs={{0,5},{1,6},{2,7},{3,0},{4,1},{5,2},{6,3},{7,4},{8,13},{9,14},{10,... | collective-permute-start | bytes 602120 | tf_op jit(solution)/shard_map/ppermute | solution.py:547
  71.6 2.8 %collective-permute-start.8 = (bf16[784,128]{1,0:T(8,128)(2,1)S(1)}, bf16[784,128]{1,0:T(8,128)(2,1)S(1)}, u32[]{:S(2)}, u32[]{:S(2)}) collective-permute-start(bf16[784,128]{1,0:T(8,128)(2,1)S(1)} %get-tuple-element.42), channel_id=1, source_target_pairs={{0,3},{1,4},{2,5},{3,6},{4,7},{5,0},{6,1},{7,2},{8,11},{9,12},{10,... | collective-permute-start | bytes 602120 | tf_op jit(solution)/shard_map/ppermute | solution.py:547
  74.4 3.8 %collective-permute-done.5.rest_4_ = bf16[784,128]{1,0:T(8,128)(2,1)S(1)} collective-permute-done((bf16[784,128]{1,0:T(8,128)(2,1)S(1)}, bf16[784,128]{1,0:T(8,128)(2,1)S(1)}, u32[]{:S(2)}, u32[]{:S(2)}) %collective-permute-start.5) | collective-permute-done | bytes 200736 | tf_op jit(solution)/shard_map/ppermute | solution.py:547
  81.3 8.0 %collective-permute-done.7.rest_1_ = bf16[784,128]{1,0:T(8,128)(2,1)S(1)} collective-permute-done((bf16[784,128]{1,0:T(8,128)(2,1)}, bf16[784,128]{1,0:T(8,128)(2,1)S(1)}, u32[]{:S(2)}, u32[]{:S(2)}) %collective-permute-start.7) | collective-permute-done | bytes 200736 | tf_op jit(solution)/shard_map/ppermute | solution.py:547
  89.4 3.4 %hidden.1 = (bf16[784,512]{1,0:T(8,128)(2,1)S(1)}, bf16[1024,512]{1,0:T(8,128)(2,1)S(1)}) custom-call(s32[2]{0:T(128)S(1)} %pad_add_fusion.band_ref, s32[1,512]{1,0:T(1,128)S(1)} %get-tuple-element.27.slot_ref, bf16[1024,912]{1,0:T(8,128)(2,1)} %bitcast.5.weight_ref, bf16[784,512]{1,0:T(8,128)(2,1)S(1)} %gather.1.begun_ref, ...), custom_call_target="tpu_custom_call" | custom-call | tf_op jit(solution)/shard_map/hidden/pallas_call | solution.py:375
  92.8 35.6 %all_to_all.25.pieces_ref = bf16[8,128,512]{2,1,0:T(8,128)(2,1)S(1)} all-to-all(bf16[8,128,512]{2,1,0:T(8,128)(2,1)S(1)} %bitcast.58), channel_id=1, replica_groups=mesh['x'=4,'z'=8,'core'=2,'tile'=8] {'tile'}, dimensions={0} | all-to-all | bytes 2097152 | tf_op jit(solution)/shard_map/all_to_all | solution.py:513
  129.8 3.6 %all-to-all-start.2 = ((bf16[8,128,512]{2,1,0:T(8,128)(2,1)}), bf16[8,128,512]{2,1,0:T(8,128)(2,1)S(1)}, u32[]{:S(2)}, u32[]{:S(2)}) async-start(bf16[8,128,512]{2,1,0:T(8,128)(2,1)} %get-tuple-element.45), calls=%async_computation.2 | async-start | bytes 2097152 | tf_op jit(solution)/shard_map/all_to_all | solution.py:513
  133.3 29.1 %all-to-all-done.2 = bf16[8,128,512]{2,1,0:T(8,128)(2,1)S(1)} async-done(((bf16[8,128,512]{2,1,0:T(8,128)(2,1)}), bf16[8,128,512]{2,1,0:T(8,128)(2,1)S(1)}, u32[]{:S(2)}, u32[]{:S(2)}) %all-to-all-start.2) | async-done | bytes 1048608 | tf_op jit(solution)/shard_map/all_to_all | solution.py:513
  163.6 2.8 %grads.1 = (bf16[32,16,784]{2,1,0:T(8,128)(2,1)S(1)}, bf16[32,16,784]{2,1,0:T(8,128)(2,1)}) custom-call(s32[1]{0:T(128)} %bitcast.core_ref, bf16[1024,512]{1,0:T(8,128)(2,1)S(1)} %bitcast.57, bf16[784,512]{1,0:T(8,128)(2,1)S(1)} %copy-done.4), custom_call_target="tpu_custom_call" | custom-call | tf_op jit(solution)/shard_map/grads/pallas_call | solution.py:443
  172.3 3.9 %all-to-all-start.3 = ((bf16[4,8,16,784]{3,2,1,0:T(8,128)(2,1)}), bf16[4,8,16,784]{3,2,1,0:T(8,128)(2,1)S(1)}, u32[]{:S(2)}, u32[]{:S(2)}) async-start(bf16[4,8,16,784]{3,2,1,0:T(8,128)(2,1)} %bitcast.11), calls=%async_computation.3 | async-start | bytes 1835008 | tf_op jit(solution)/shard_map/all_to_all | solution.py:513
  176.2 2.6 %collective-permute-start.10 = (bf16[4,8,16,128]{3,2,1,0:T(8,128)(2,1)S(1)}, bf16[4,8,16,128]{3,2,1,0:T(8,128)(2,1)S(1)}, u32[]{:S(2)}, u32[]{:S(2)}) collective-permute-start(bf16[4,8,16,128]{3,2,1,0:T(8,128)(2,1)S(1)} %fusion.6), channel_id=1, source_target_pairs={{0,8},{8,0},{1,9},{9,1},{2,10},{10,2},{3,11},{11,3},{4,12},{12,4},... | collective-permute-start | bytes 393224 | tf_op jit(solution)/shard_map/ppermute | solution.py:568
  179.8 3.7 %collective-permute-start.11 = (bf16[8,16,128]{2,1,0:T(8,128)(2,1)S(1)}, bf16[8,16,128]{2,1,0:T(8,128)(2,1)S(1)}, u32[]{:S(2)}, u32[]{:S(2)}) collective-permute-start(bf16[8,16,128]{2,1,0:T(8,128)(2,1)S(1)} %get-tuple-element.54), channel_id=1, source_target_pairs={{0,128},{128,256},{256,384},{384,0},{1,129},{129,257},{257,385},{3... | collective-permute-start | bytes 98312 | tf_op jit(solution)/shard_map/ppermute | solution.py:575
  183.5 4.3 %collective-permute-start.12 = (bf16[8,16,128]{2,1,0:T(8,128)(2,1)S(1)}, bf16[8,16,128]{2,1,0:T(8,128)(2,1)S(1)}, u32[]{:S(2)}, u32[]{:S(2)}) collective-permute-start(bf16[8,16,128]{2,1,0:T(8,128)(2,1)S(1)} %get-tuple-element.53), channel_id=1, source_target_pairs={{0,256},{128,384},{256,0},{384,128},{1,257},{129,385},{257,1},{385... | collective-permute-start | bytes 98312 | tf_op jit(solution)/shard_map/ppermute | solution.py:575
  187.8 3.1 %collective-permute-start.13 = (bf16[8,16,128]{2,1,0:T(8,128)(2,1)S(1)}, bf16[8,16,128]{2,1,0:T(8,128)(2,1)S(1)}, u32[]{:S(2)}, u32[]{:S(2)}) collective-permute-start(bf16[8,16,128]{2,1,0:T(8,128)(2,1)S(1)} %get-tuple-element.52), channel_id=1, source_target_pairs={{0,384},{128,0},{256,128},{384,256},{1,385},{129,1},{257,129},{385... | collective-permute-start | bytes 98312 | tf_op jit(solution)/shard_map/ppermute | solution.py:575
  192.6 15.5 %all_to_all.26.pieces_ref = bf16[8,16,912]{2,1,0:T(8,128)(2,1)S(1)} all-to-all(bf16[8,16,912]{2,1,0:T(8,128)(2,1)S(1)} %merge.1), channel_id=1, replica_groups=mesh['x'=4,'z'=8,'core'=2,'tile'=8] {'z'}, dimensions={0} | all-to-all | bytes 466944 | tf_op jit(solution)/shard_map/all_to_all | solution.py:513
  (46 shorter events, 22.0 us)
Async XLA Ops:
  0.6 79.2 %copy-start = (bf16[1,512,1024]{2,1,0:T(8,128)(2,1)S(1)}, bf16[1,512,1024]{2,1,0:T(8,128)(2,1)}, u32[]{:S(2)}) copy-start(bf16[1,512,1024]{2,1,0:T(8,128)(2,1)} %param.13) | copy-start | bytes 3145732
  3.2 76.7 %all-to-all-start = ((bf16[64,16,912]{2,1,0:T(8,128)(2,1)}), bf16[64,16,912]{2,1,0:T(8,128)(2,1)}, u32[]{:S(2)}, u32[]{:S(2)}) async-start(bf16[64,16,912]{2,1,0:T(8,128)(2,1)} %copies.1), calls=%async_computation | async-start | bytes 4194304 | tf_op jit(solution)/shard_map/all_to_all | solution.py:513
  18.2 4.9 %copy-start.5 = (s32[1,4,512]{2,1,0:T(4,128)S(1)}, s32[1,4,512]{2,1,0:T(4,128)}, u32[]{:S(2)}) copy-start(s32[1,4,512]{2,1,0:T(4,128)} %param.7) | copy-start | bytes 24580
  18.2 4.9 %copy-start.6 = (s32[1,512]{1,0:T(1,128)S(1)}, s32[1,512]{1,0:T(1,128)}, u32[]{:S(2)}) copy-start(s32[1,512]{1,0:T(1,128)} %refs_2_.1) | copy-start | bytes 6148
  18.2 5.4 %copy-start.1 = (bf16[1,42,168,128]{3,2,1,0:T(8,128)(2,1)S(1)}, bf16[1,42,168,128]{3,2,1,0:T(8,128)(2,1)}, u32[]{:S(2)}) copy-start(bf16[1,42,168,128]{3,2,1,0:T(8,128)(2,1)} %param.9) | copy-start | bytes 5419012
  18.2 5.4 %copy-start.2 = (bf16[1,21,84,128]{3,2,1,0:T(8,128)(2,1)S(1)}, bf16[1,21,84,128]{3,2,1,0:T(8,128)(2,1)}, u32[]{:S(2)}) copy-start(bf16[1,21,84,128]{3,2,1,0:T(8,128)(2,1)} %param.10) | copy-start | bytes 1354756
  20.5 23.6 %collective-permute-start = (bf16[14,168,128]{2,1,0:T(8,128)(2,1)}, bf16[14,168,128]{2,1,0:T(8,128)(2,1)}, u32[]{:S(2)}, u32[]{:S(2)}) collective-permute-start(bf16[14,168,128]{2,1,0:T(8,128)(2,1)} %get-tuple-element.30), channel_id=1, source_target_pairs={{1,0},{2,1},{3,2},{4,3},{5,4},{6,5},{7,6},{9,8},{10,9},{11,10},{12... | collective-permute-start | bytes 1806344 | tf_op jit(solution)/shard_map/ppermute | solution.py:526
  21.8 22.3 %collective-permute-start.1 = (bf16[14,84,128]{2,1,0:T(8,128)(2,1)}, bf16[14,84,128]{2,1,0:T(8,128)(2,1)}, u32[]{:S(2)}, u32[]{:S(2)}) collective-permute-start(bf16[14,84,128]{2,1,0:T(8,128)(2,1)} %get-tuple-element.31), channel_id=1, source_target_pairs={{1,0},{2,1},{3,2},{4,3},{5,4},{6,5},{7,6},{9,8},{10,9},{11,10},{12... | collective-permute-start | bytes 903176 | tf_op jit(solution)/shard_map/ppermute | solution.py:527
  48.8 18.5 %collective-permute-start.2 = (bf16[784,128]{1,0:T(8,128)(2,1)S(1)}, bf16[784,128]{1,0:T(8,128)(2,1)S(1)}, u32[]{:S(2)}, u32[]{:S(2)}) collective-permute-start(bf16[784,128]{1,0:T(8,128)(2,1)S(1)} %get-tuple-element.33), channel_id=1, source_target_pairs={{0,4},{1,5},{2,6},{3,7},{4,0},{5,1},{6,2},{7,3},{8,12},{9,13},{10,... | collective-permute-start | bytes 602120 | tf_op jit(solution)/shard_map/ppermute | solution.py:547
  55.4 16.2 %collective-permute-start.3 = (bf16[784,128]{1,0:T(8,128)(2,1)S(1)}, bf16[784,128]{1,0:T(8,128)(2,1)S(1)}, u32[]{:S(2)}, u32[]{:S(2)}) collective-permute-start(bf16[784,128]{1,0:T(8,128)(2,1)S(1)} %get-tuple-element.34), channel_id=1, source_target_pairs={{0,7},{1,0},{2,1},{3,2},{4,3},{5,4},{6,5},{7,6},{8,15},{9,8},{10,9... | collective-permute-start | bytes 602120 | tf_op jit(solution)/shard_map/ppermute | solution.py:547
  59.1 15.3 %collective-permute-start.4 = (bf16[784,128]{1,0:T(8,128)(2,1)S(1)}, bf16[784,128]{1,0:T(8,128)(2,1)S(1)}, u32[]{:S(2)}, u32[]{:S(2)}) collective-permute-start(bf16[784,128]{1,0:T(8,128)(2,1)S(1)} %get-tuple-element.35), channel_id=1, source_target_pairs={{0,1},{1,2},{2,3},{3,4},{4,5},{5,6},{6,7},{7,0},{8,9},{9,10},{10,1... | collective-permute-start | bytes 602120 | tf_op jit(solution)/shard_map/ppermute | solution.py:547
  61.0 17.2 %collective-permute-start.5 = (bf16[784,128]{1,0:T(8,128)(2,1)S(1)}, bf16[784,128]{1,0:T(8,128)(2,1)S(1)}, u32[]{:S(2)}, u32[]{:S(2)}) collective-permute-start(bf16[784,128]{1,0:T(8,128)(2,1)S(1)} %get-tuple-element.36), channel_id=1, source_target_pairs={{0,6},{1,7},{2,0},{3,1},{4,2},{5,3},{6,4},{7,5},{8,14},{9,15},{10,... | collective-permute-start | bytes 602120 | tf_op jit(solution)/shard_map/ppermute | solution.py:547
  64.2 17.1 %collective-permute-start.6 = (bf16[784,128]{1,0:T(8,128)(2,1)}, bf16[784,128]{1,0:T(8,128)(2,1)S(1)}, u32[]{:S(2)}, u32[]{:S(2)}) collective-permute-start(bf16[784,128]{1,0:T(8,128)(2,1)} %get-tuple-element.40), channel_id=1, source_target_pairs={{0,2},{1,3},{2,4},{3,5},{4,6},{5,7},{6,0},{7,1},{8,10},{9,11},{10,... | collective-permute-start | bytes 602120 | tf_op jit(solution)/shard_map/ppermute | solution.py:547
  67.3 22.0 %collective-permute-start.7 = (bf16[784,128]{1,0:T(8,128)(2,1)}, bf16[784,128]{1,0:T(8,128)(2,1)S(1)}, u32[]{:S(2)}, u32[]{:S(2)}) collective-permute-start(bf16[784,128]{1,0:T(8,128)(2,1)} %get-tuple-element.41), channel_id=1, source_target_pairs={{0,5},{1,6},{2,7},{3,0},{4,1},{5,2},{6,3},{7,4},{8,13},{9,14},{10,... | collective-permute-start | bytes 602120 | tf_op jit(solution)/shard_map/ppermute | solution.py:547
  71.6 17.7 %collective-permute-start.8 = (bf16[784,128]{1,0:T(8,128)(2,1)S(1)}, bf16[784,128]{1,0:T(8,128)(2,1)S(1)}, u32[]{:S(2)}, u32[]{:S(2)}) collective-permute-start(bf16[784,128]{1,0:T(8,128)(2,1)S(1)} %get-tuple-element.42), channel_id=1, source_target_pairs={{0,3},{1,4},{2,5},{3,6},{4,7},{5,0},{6,1},{7,2},{8,11},{9,12},{10,... | collective-permute-start | bytes 602120 | tf_op jit(solution)/shard_map/ppermute | solution.py:547
  92.8 37.0 %copy-start.3 = (bf16[784,512]{1,0:T(8,128)(2,1)}, bf16[784,512]{1,0:T(8,128)(2,1)S(1)}, u32[]{:S(2)}) copy-start(bf16[784,512]{1,0:T(8,128)(2,1)S(1)} %get-tuple-element.46.feats_ref) | copy-start | bytes 2408452
  129.8 32.7 %all-to-all-start.2 = ((bf16[8,128,512]{2,1,0:T(8,128)(2,1)}), bf16[8,128,512]{2,1,0:T(8,128)(2,1)S(1)}, u32[]{:S(2)}, u32[]{:S(2)}) async-start(bf16[8,128,512]{2,1,0:T(8,128)(2,1)} %get-tuple-element.45), calls=%async_computation.2 | async-start | bytes 2097152 | tf_op jit(solution)/shard_map/all_to_all | solution.py:513
  162.4 1.1 copy-start.4
  166.4 4.7 %collective-permute-start.9 = (bf16[32,16,784]{2,1,0:T(8,128)(2,1)}, bf16[32,16,784]{2,1,0:T(8,128)(2,1)S(1)}, u32[]{:S(2)}, u32[]{:S(2)}) collective-permute-start(bf16[32,16,784]{2,1,0:T(8,128)(2,1)} %get-tuple-element.48), channel_id=1, source_target_pairs={{0,8},{8,0},{1,9},{9,1},{2,10},{10,2},{3,11},{11,3},{4,12},{12,4},... | collective-permute-start | bytes 2408456 | tf_op jit(solution)/shard_map/ppermute | solution.py:580
  172.3 20.2 %all-to-all-start.3 = ((bf16[4,8,16,784]{3,2,1,0:T(8,128)(2,1)}), bf16[4,8,16,784]{3,2,1,0:T(8,128)(2,1)S(1)}, u32[]{:S(2)}, u32[]{:S(2)}) async-start(bf16[4,8,16,784]{3,2,1,0:T(8,128)(2,1)} %bitcast.11), calls=%async_computation.3 | async-start | bytes 1835008 | tf_op jit(solution)/shard_map/all_to_all | solution.py:513
  176.2 3.5 %collective-permute-start.10 = (bf16[4,8,16,128]{3,2,1,0:T(8,128)(2,1)S(1)}, bf16[4,8,16,128]{3,2,1,0:T(8,128)(2,1)S(1)}, u32[]{:S(2)}, u32[]{:S(2)}) collective-permute-start(bf16[4,8,16,128]{3,2,1,0:T(8,128)(2,1)S(1)} %fusion.6), channel_id=1, source_target_pairs={{0,8},{8,0},{1,9},{9,1},{2,10},{10,2},{3,11},{11,3},{4,12},{12,4},... | collective-permute-start | bytes 393224 | tf_op jit(solution)/shard_map/ppermute | solution.py:568
  179.8 11.1 %collective-permute-start.11 = (bf16[8,16,128]{2,1,0:T(8,128)(2,1)S(1)}, bf16[8,16,128]{2,1,0:T(8,128)(2,1)S(1)}, u32[]{:S(2)}, u32[]{:S(2)}) collective-permute-start(bf16[8,16,128]{2,1,0:T(8,128)(2,1)S(1)} %get-tuple-element.54), channel_id=1, source_target_pairs={{0,128},{128,256},{256,384},{384,0},{1,129},{129,257},{257,385},{3... | collective-permute-start | bytes 98312 | tf_op jit(solution)/shard_map/ppermute | solution.py:575
  183.5 7.4 %collective-permute-start.12 = (bf16[8,16,128]{2,1,0:T(8,128)(2,1)S(1)}, bf16[8,16,128]{2,1,0:T(8,128)(2,1)S(1)}, u32[]{:S(2)}, u32[]{:S(2)}) collective-permute-start(bf16[8,16,128]{2,1,0:T(8,128)(2,1)S(1)} %get-tuple-element.53), channel_id=1, source_target_pairs={{0,256},{128,384},{256,0},{384,128},{1,257},{129,385},{257,1},{385... | collective-permute-start | bytes 98312 | tf_op jit(solution)/shard_map/ppermute | solution.py:575
  187.8 4.7 %collective-permute-start.13 = (bf16[8,16,128]{2,1,0:T(8,128)(2,1)S(1)}, bf16[8,16,128]{2,1,0:T(8,128)(2,1)S(1)}, u32[]{:S(2)}, u32[]{:S(2)}) collective-permute-start(bf16[8,16,128]{2,1,0:T(8,128)(2,1)S(1)} %get-tuple-element.52), channel_id=1, source_target_pairs={{0,384},{128,0},{256,128},{384,256},{1,385},{129,1},{257,129},{385... | collective-permute-start | bytes 98312 | tf_op jit(solution)/shard_map/ppermute | solution.py:575
